TPU v7x, 32 devices: a 4x4x1 block of a 4x4x8 slice. The times are simulated.
32 devices in a mesh: dp: 1 (over z), tp: 4 (over y), sp: 8 (over x, core).
Axes of the slice: x: 4, y: 4, z: 1, core: 2. Of those that a mesh axis runs over, the one named last changes fastest.
The devices are a block of a 4x4x8 slice.
Arguments:
- hidden: bfloat16 [128, 5120], P('dp')
- seq_lens: int32 [128], P('dp')
- rope_cos: float32 [128, 64], P('dp')
- rope_sin: float32 [128, 64], P('dp')
- k_cache: bfloat16 [128, 512, 8, 128], P('dp', 'sp', 'tp')
- v_cache: bfloat16 [128, 512, 8, 128], P('dp', 'sp', 'tp')
- norm_gain: bfloat16 [5120], replicated
- w_qkv: bfloat16 [5120, 8, 1280], P(None, 'tp')
- b_qkv: bfloat16 [8, 1280], P('tp')
- sink_logits: float32 [64], P('tp')
- w_o: bfloat16 [8192, 5120], P('tp')
- b_o: bfloat16 [5120], replicated
Outputs:
- output 1: bfloat16 [128, 5120], P('dp')
- output 2: bfloat16 [128, 512, 8, 128], P('dp', 'sp', 'tp')
- output 3: bfloat16 [128, 512, 8, 128], P('dp', 'sp', 'tp')
All inputs are finite; a program needn't handle non-finite values.
Results may differ from a plain program's by a relative error of at most 0.00575541.
Values sent between devices are 32-bit elements.
A program may use at most 768 MiB of HBM per device.

v0:
```python
import jax
import jax.numpy as jnp
from jax import lax
from jax.sharding import PartitionSpec as P

NORM_EPS = 1e-5


def rotate_half(heads_in, cos_part, sin_part):
    half_dim = heads_in.shape[-1] // 2
    first_half = heads_in[..., :half_dim]
    second_half = heads_in[..., half_dim:]
    return jnp.concatenate([first_half * cos_part - second_half * sin_part, second_half * cos_part + first_half * sin_part], axis=-1)


def local_partials(hidden, seq_lens, rope_cos, rope_sin, k_cache, v_cache, norm_gain, w_qkv, b_qkv, sink_logits):
    num_seqs, ctx_local, kv_local, head_dim = k_cache.shape
    group_size = w_qkv.shape[2] // head_dim - 2
    x_wide = hidden.astype(jnp.float32)
    inv_rms = lax.rsqrt(jnp.mean(x_wide * x_wide, axis=-1, keepdims=True) + NORM_EPS)
    normed = (x_wide * inv_rms * norm_gain.astype(jnp.float32)).astype(jnp.bfloat16)
    qkv_all = jnp.einsum("bd,dkc->bkc", normed, w_qkv, preferred_element_type=jnp.float32) + b_qkv.astype(jnp.float32)
    qkv_all = qkv_all.reshape(num_seqs, kv_local, group_size + 2, head_dim)
    q_rot = rotate_half(qkv_all[:, :, :group_size], rope_cos[:, None, None, :], rope_sin[:, None, None, :]).astype(jnp.bfloat16)
    k_new = rotate_half(qkv_all[:, :, group_size], rope_cos[:, None, :], rope_sin[:, None, :]).astype(jnp.bfloat16)
    v_new = qkv_all[:, :, group_size + 1].astype(jnp.bfloat16)
    positions = lax.axis_index("sp") * ctx_local + jnp.arange(ctx_local)
    is_new = (positions[None, :] == seq_lens[:, None])[:, :, None, None]
    k_out = jnp.where(is_new, k_new[:, None], k_cache)
    v_out = jnp.where(is_new, v_new[:, None], v_cache)
    logits = jnp.einsum("bkgd,blkd->bkgl", q_rot, k_out, preferred_element_type=jnp.float32) * head_dim ** -0.5
    logits = jnp.where((positions[None, :] <= seq_lens[:, None])[:, None, None, :], logits, -jnp.inf)
    row_max = jnp.maximum(jnp.max(logits, axis=-1), sink_logits.reshape(kv_local, group_size))
    weights = jnp.exp(logits - row_max[..., None])
    row_sum = jnp.sum(weights, axis=-1)
    weighted = jnp.einsum("bkgl,blkd->bkgd", weights.astype(jnp.bfloat16), v_out, preferred_element_type=jnp.float32)
    packed = jnp.concatenate([row_max[..., None], row_sum[..., None], weighted], axis=-1)
    return packed.reshape(num_seqs, kv_local * group_size, head_dim + 2), k_out, v_out


def combine_shards(parts_in, sinks_here):
    shard_max = parts_in[..., 0]
    shard_sum = parts_in[..., 1]
    top_max = jnp.max(shard_max, axis=1)
    rescale = jnp.exp(shard_max - top_max[:, None])
    denominator = jnp.sum(shard_sum * rescale, axis=1) + jnp.exp(sinks_here[None, :] - top_max)
    combined = jnp.sum(parts_in[..., 2:] * rescale[..., None], axis=1)
    return combined / denominator[..., None]


def solution(mesh):
    sp_size = mesh.shape["sp"]
    cache_spec = P("dp", "sp", "tp", None)

    def block_step(hidden, seq_lens, rope_cos, rope_sin, k_cache, v_cache, norm_gain, w_qkv, b_qkv, sink_logits, w_o, b_o):
        packed, k_out, v_out = local_partials(hidden, seq_lens, rope_cos, rope_sin, k_cache, v_cache, norm_gain, w_qkv, b_qkv, sink_logits)
        num_seqs, local_heads, width = packed.shape
        head_dim = width - 2
        head_share = local_heads // sp_size
        received = lax.all_to_all(packed.reshape(num_seqs, sp_size, head_share, width), "sp", 1, 1, tiled=True)
        sp_index = lax.axis_index("sp")
        sinks_here = sink_logits.reshape(sp_size, head_share)[sp_index]
        combined = combine_shards(received, sinks_here)
        w_rows = w_o.reshape(sp_size, head_share * head_dim, w_o.shape[1])[sp_index]
        partial_out = jnp.dot(combined.astype(jnp.bfloat16).reshape(num_seqs, head_share * head_dim), w_rows, preferred_element_type=jnp.float32)
        summed = lax.psum(partial_out, ("tp", "sp"))
        out_hidden = (hidden.astype(jnp.float32) + summed + b_o.astype(jnp.float32)).astype(jnp.bfloat16)
        return out_hidden, k_out, v_out

    return jax.shard_map(block_step, mesh=mesh, in_specs=(P("dp", None), P("dp"), P("dp", None), P("dp", None), cache_spec, cache_spec, P(None), P(None, "tp", None), P("tp", None), P("tp"), P("tp", None), P(None)), out_specs=(P("dp", None), cache_spec, cache_spec), check_vma=False)
```

profile of v0, /device:TPU:97, one launch (start us, length us, event | category | flops | bytes accessed | tf_op | source)
XLA Modules:
  0.0 189.9 jit_solution(18041043566286641919)
XLA Ops:
  7.2 0.7 convert_element_type.50
  7.9 0.7 convert_element_type.52
  8.6 1.6 fusion.9
  10.2 16.9 %fusion.6 = f32[128,2,1280]{2,0,1:T(8,128)S(1)} fusion(bf16[5120,2,1280]{2,1,0:T(2,128)(2,1)} %param.19, bf16[128,5120]{1,0:T(8,128)(2,1)} %param.12, f32[5120]{0:T(1024)S(1)} %convert_element_type.50, f32[128]{0:T(128)S(1)} %add_rsqrt_fusion, f32[2,1280]{1,0:T(2,128)S(1)} %convert_element_type.52), kind=kOutput, calls=%fused_computation.11 | convolution fusion | flops 3358392320 | bytes 28867072 | tf_op jit(solution)/shard_map/bd,dkc->bkc/dot_general | solution.py:22
  27.1 0.0 copy-start.6
  27.1 0.0 copy-start.3
  27.1 0.0 copy-start.2
  27.2 0.4 copy.86
  27.6 0.0 copy-start.5
  27.6 0.1 fusion.41
  27.7 0.1 copy-done.6
  27.8 0.1 max.30
  27.9 0.1 max.27
  27.9 0.0 copy-done.3
  27.9 0.1 copy.88
  28.0 0.0 copy-done.2
  28.1 0.1 copy.90
  28.2 0.1 copy.91
  28.3 0.1 copy.96
  28.5 0.5 copy.110
  29.0 0.5 copy.111
  29.5 0.0 copy-done.5
  29.5 0.1 broadcast_compare_fusion.1
  29.6 0.3 subtract_convert_fusion
  29.9 14.1 %broadcast_select_fusion.1 = (bf16[128,64,2,128]{3,2,1,0:T(2,128)(2,1)S(1)}, bf16[128,64,2,128]{3,2,1,0:T(2,128)(2,1)}) fusion(bf16[128,64,2,128]{3,2,1,0:T(2,128)(2,1)} %param.16, pred[128,64]{1,0:T(8,128)(4,1)S(1)} %get-tuple-element.15, bf16[128,2,128]{2,1,0:T(2,128)(2,1)S(1)} %copy.91, bf16[128,64,2,128]{3,2,1,0:T(2,128)(2,1)} %param.17, ...), kind=kLoop, calls=%fused_computation.3 | loop fusion | flops 4194304 | bytes 16916480 | tf_op jit(solution)/shard_map/jit(_where)/select_n | solution.py:29
  44.0 0.0 copy-start
  44.0 2.6 %fusion.43 = (f32[128,2,8]{2,1,0:T(2,128)S(1)}, f32[128,2,8,64]{3,2,1,0:T(8,128)S(1)}) fusion(bf16[128,64,2,128]{3,2,1,0:T(2,128)(2,1)S(1)} %get-tuple-element.12, bf16[128,2,8,64]{3,2,1,0:T(8,128)(2,1)S(1)} %get-tuple-element.4, bf16[128,2,8,64]{3,2,1,0:T(8,128)(2,1)S(1)} %get-tuple-element.3, pred[128,64]{1,0:T(8,128)(4,1)S(1)} %get-tuple-element.14), kind=kOutput, calls=%fused_computation.63 | convolution fusion | flops 34994176 | bytes 5259264 | tf_op jit(solution)/shard_map/bkgd,blkd->bkgl/dot_general | solution.py:31
  46.6 0.0 copy-done
  46.6 0.1 copy.93
  46.7 0.8 fusion.29
  47.4 3.4 %fusion.2 = f32[128,2,8,128]{3,2,1,0:T(8,128)S(1)} fusion(bf16[128,64,2,128]{3,2,1,0:T(2,128)(2,1)} %get-tuple-element.13, f32[128,2,8,64]{3,2,1,0:T(8,128)S(1)} %get-tuple-element.17, f32[128,2,8]{2,1,0:T(2,128)S(1)} %bitcast.46), kind=kOutput, calls=%fused_computation.4 | convolution fusion | flops 33816576 | bytes 5775360 | tf_op jit(solution)/shard_map/bkgl,blkd->bkgd/dot_general | solution.py:36
  50.9 1.6 copy.100
  52.5 0.1 copy.94
  52.6 0.1 maximum_bitcast_fusion
  52.6 1.5 pad_maximum_fusion
  54.2 6.0 %all-to-all-start = ((f32[128,8,2,130]{0,2,3,1:T(2,128)}), f32[128,8,2,130]{0,2,3,1:T(2,128)S(1)}, u32[]{:S(2)}, u32[]{:S(2)}) async-start(f32[128,8,2,130]{0,2,3,1:T(2,128)} %pad_maximum_fusion), calls=%async_computation | async-start | bytes 2129920 | tf_op jit(solution)/shard_map/all_to_all | solution.py:60
  60.2 0.0 all-reduce.2.cloned.1.call-start
  60.2 14.9 %all-to-all-done = f32[128,8,2,130]{0,2,3,1:T(2,128)S(1)} async-done(((f32[128,8,2,130]{0,2,3,1:T(2,128)}), f32[128,8,2,130]{0,2,3,1:T(2,128)S(1)}, u32[]{:S(2)}, u32[]{:S(2)}) %all-to-all-start) | async-done | bytes 1064992 | tf_op jit(solution)/shard_map/all_to_all | solution.py:60
  75.2 0.5 fusion.27
  75.7 0.1 copy.105
  75.8 0.1 exponential_add_fusion
  75.9 0.1 divide_convert_fusion
  76.0 0.1 copy.106
  76.1 3.8 %fusion.14 = f32[128,5120]{1,0:T(8,128)} fusion(bf16[128,256]{0,1:T(8,128)(2,1)S(1)} %bitcast.48, bf16[8,256,5120]{2,1,0:T(8,128)(2,1)} %bitcast.47, s32[]{:T(128)S(6)} %select_n.18), kind=kOutput, calls=%fused_computation.17 | convolution fusion | flops 335544320 | bytes 5308420 | tf_op jit(solution)/shard_map/dot_general | solution.py:65
  79.9 0.0 copy-start.4
  79.9 0.0 copy-start.1
  79.9 0.1 all-reduce.2.cloned.1.call-update
  80.0 0.6 copy-done.4
  80.6 99.3 %all-reduce.2.cloned.1.call-done = f32[128,5120]{1,0:T(8,128)} async-done(((f32[128,5120]{1,0:T(8,128)}), f32[128,5120]{1,0:T(8,128)}) %all-reduce.2.cloned.1.call-update) | async-done | bytes 2621456 | tf_op jit(solution)/shard_map/psum | solution.py:66
  179.9 0.0 copy-done.1
  179.9 3.1 %fusion.13 = bf16[128,5120]{1,0:T(8,128)(2,1)} fusion(f32[128,5120]{1,0:T(8,128)} %all-reduce.2.cloned.1.call-done, bf16[128,5120]{1,0:T(8,128)(2,1)S(1)} %copy-done.1, f32[5120]{0:T(1024)S(1)} %convert_element_type.57), kind=kLoop, calls=%fused_computation.16 | loop fusion | flops 2621440 | bytes 5263360 | tf_op jit(solution)/shard_map/convert_element_type | solution.py:67
  (14 shorter events, 0.2 us)
Async XLA Ops:
  27.1 0.7 copy-start.6
  27.1 0.8 copy-start.3
  27.1 0.9 copy-start.2
  27.6 1.9 copy-start.5
  44.0 2.6 %copy-start = (bf16[128,64,2,128]{3,2,1,0:T(2,128)(2,1)}, bf16[128,64,2,128]{3,2,1,0:T(2,128)(2,1)S(1)}, u32[]{:S(2)}) copy-start(bf16[128,64,2,128]{3,2,1,0:T(2,128)(2,1)S(1)} %get-tuple-element.12) | copy-start | bytes 12582916
  54.2 20.9 %all-to-all-start = ((f32[128,8,2,130]{0,2,3,1:T(2,128)}), f32[128,8,2,130]{0,2,3,1:T(2,128)S(1)}, u32[]{:S(2)}, u32[]{:S(2)}) async-start(f32[128,8,2,130]{0,2,3,1:T(2,128)} %pad_maximum_fusion), calls=%async_computation | async-start | bytes 2129920 | tf_op jit(solution)/shard_map/all_to_all | solution.py:60
  60.2 119.7 %all-reduce.2.cloned.1.call-start = ((), (), s32[]{:S(2)}) async-start(), calls=%async_computation.1 | async-start | bytes 5242880 | tf_op jit(solution)/shard_map/psum | solution.py:66
  79.9 0.7 copy-start.4
  79.9 100.0 %copy-start.1 = (bf16[128,5120]{1,0:T(8,128)(2,1)S(1)}, bf16[128,5120]{1,0:T(8,128)(2,1)}, u32[]{:S(2)}) copy-start(bf16[128,5120]{1,0:T(8,128)(2,1)} %param.12) | copy-start | bytes 3932164
Sparse Core Ops, SparseCore 0:
  80.1 99.7 all-reduce.1
where the time goes:
time: 190 us
  waiting for transfers between devices  114 us (60%)
  matrix products  26.7 us (14%)
  other arithmetic  23.8 us (13%)
  between operations  14.3 us (8%)
  starting transfers between devices  6.01 us (3%)
  local copies, waits for them, and re-layouts  4.79 us (3%)
    psum x1, waiting for transfers between devices, block_step(): summed = lax.psum(partial_out, ('tp', 'sp'))  99.3 us
    dot_general x1, matrix products, local_partials(): jnp.einsum('bd,dkc->bkc', normed, w_qkv, preferred_element_type=jnp.float32)  16.9 us
    all_to_all x1, waiting for transfers between devices, block_step(): lax.all_to_all(packed.reshape(num_seqs, sp_size, head_share, width), 'sp'...  14.9 us
    select_n x1, other arithmetic, local_partials(): k_out = jnp.where(is_new, k_new[:, None], k_cache)  14.1 us
    all_to_all x1, starting transfers between devices, block_step(): lax.all_to_all(packed.reshape(num_seqs, sp_size, head_share, width), 'sp'...  6.01 us
    dot_general x1, matrix products, block_step(): jnp.dot(combined.astype(jnp.bfloat16).reshape(num_seqs, head_share * head...  3.82 us
  transfers between devices with their start and end apart: 2, of which 2 were waited for; matrix products, arithmetic and copies ran while one was open for 0% of the time, Pallas kernels for 0%

commit v1 on v0

v1 whole, which is shorter than its diff:
```python
import functools

import jax
import jax.numpy as jnp
from jax import lax
from jax.experimental import pallas as pl
from jax.experimental.pallas import tpu as pltpu
from jax.sharding import PartitionSpec as P

NORM_EPS = 1e-5
MESH = pl.DeviceIdType.MESH
LANES = 128
HALF = LANES // 2
SUBS = 2
CORES = 2
RING = 4


def lane_column(tile, index):
    return tile[:, index : index + 1]


def merge_parts(parts, seqs):
    stats = [part[seqs] for part in parts]
    top = functools.reduce(jnp.maximum, stats)
    scales = [jnp.exp(stat - top) for stat in stats]
    total = sum(pltpu.roll(scale, HALF, 1) * stat for scale, stat in zip(scales, stats))
    return top, total, scales


def merge_into(dst, parts, seqs):
    top, total, scales = merge_parts(parts, seqs)
    for i in range(seqs):
        dst[i] = sum(lane_column(scale, i) * part[i] for scale, part in zip(scales, parts))
    lane = lax.broadcasted_iota(jnp.int32, top.shape, 1)
    dst[seqs] = jnp.where(lane < HALF, top, total)


def combine_kernel(
    seqs, p_ref, sink_ref, x_hbm, bo_ref, wo_hbm, out_ref,
    ra, cb, rl, rm, rd, own_o, other_o, wbuf, xbuf, z, yrl, ym, yrm, yrd, g, gp,
    w_sem, x_sem, a_send, a_recv, b_send, rl_recv, rm_recv, rd_recv, o_send, o_recv,
    d_send, yrl_recv, yrm_recv, yrd_recv, g_send, g_recv, gp_send, gp_recv,
):
    y = lax.axis_index("tp")
    sp = lax.axis_index("sp")
    x = sp // CORES
    c = sp % CORES
    step = 1 - 2 * c
    xn, xp, xo = (x + step + RING) % RING, (x - step + RING) % RING, (x + 2) % RING
    yn, yp, yo = (y + step + RING) % RING, (y - step + RING) % RING, (y + 2) % RING
    partner = {"sp": x * CORES + 1 - c}
    to_xn, to_xp = {"sp": xn * CORES + c}, {"sp": xp * CORES + c}
    to_yn, to_yp = {"tp": yn}, {"tp": yp}

    rows_half = wo_hbm.shape[0] // 2
    cols_core = wo_hbm.shape[1] // CORES
    cols_sub = cols_core // SUBS
    heads = p_ref.shape[4]
    block_rows = z.shape[2]

    w_copies = []
    for k in range(2):
        rows = (c if k == 0 else 1 - c) * rows_half
        copy = pltpu.make_async_copy(
            wo_hbm.at[pl.ds(pl.multiple_of(rows, LANES), rows_half), pl.ds(pl.multiple_of(c * cols_core, LANES), cols_core)],
            wbuf.at[k], w_sem.at[k])
        copy.start()
        w_copies.append(copy)
    row0 = pl.multiple_of((x * RING + y) * block_rows, block_rows)
    x_copy = pltpu.make_async_copy(
        x_hbm.at[pl.ds(row0, block_rows), pl.ds(pl.multiple_of(c * cols_core, LANES), cols_core)], xbuf, x_sem.at[0])
    x_copy.start()

    barrier = pltpu.get_barrier_semaphore()
    for where in (partner, to_xn, to_xp, to_yn, to_yp):
        pl.semaphore_signal(barrier, inc=1, device_id=where, device_id_type=MESH)
    pl.semaphore_wait(barrier, 5)

    sends = []

    def send(src, dst, send_sem, recv_sem, where):
        copy = pltpu.make_async_remote_copy(
            src_ref=src, dst_ref=dst, send_sem=send_sem, recv_sem=recv_sem, device_id=where, device_id_type=MESH)
        copy.start()
        sends.append(copy)

    def arrived(dst, recv_sem):
        pltpu.make_async_remote_copy(
            src_ref=dst, dst_ref=dst, send_sem=recv_sem, recv_sem=recv_sem, device_id=partner, device_id_type=MESH).wait_recv()

    for k, b in enumerate((xo, xp, xn, x)):
        for s in range(SUBS):
            send(p_ref.at[b, s, 1 - c], ra.at[b, s], a_send.at[k, s], a_recv.at[b, s], partner)

    for s in range(SUBS):
        arrived(ra.at[xo, s], a_recv.at[xo, s])
        merge_into(cb.at[0, s], (p_ref.at[xo, s, c], ra.at[xo, s]), seqs)
        send(cb.at[0, s], rl.at[s], b_send.at[0, s], rl_recv.at[s], to_xn)
    for s in range(SUBS):
        arrived(ra.at[xp, s], a_recv.at[xp, s])
        merge_into(cb.at[1, s], (p_ref.at[xp, s, c], ra.at[xp, s]), seqs)
        send(cb.at[1, s], rd.at[s], b_send.at[1, s], rd_recv.at[s], to_xp)
    for s in range(SUBS):
        arrived(ra.at[xn, s], a_recv.at[xn, s])
        arrived(rl.at[s], rl_recv.at[s])
        merge_into(cb.at[2, s], (p_ref.at[xn, s, c], ra.at[xn, s], rl.at[s]), seqs)
        send(cb.at[2, s], rm.at[s], b_send.at[2, s], rm_recv.at[s], to_xn)
    for s in range(SUBS):
        arrived(ra.at[x, s], a_recv.at[x, s])
        merge_into(cb.at[3, s], (p_ref.at[x, s, c], ra.at[x, s]), seqs)
    sink = sink_ref[pl.ds(pl.multiple_of(c * heads, heads), heads), :]
    for s in range(SUBS):
        arrived(rd.at[s], rd_recv.at[s])
        arrived(rm.at[s], rm_recv.at[s])
        parts = (cb.at[3, s], rd.at[s], rm.at[s])
        top, total, scales = merge_parts(parts, seqs)
        inverse = 1.0 / (pltpu.roll(total, HALF, 1) + jnp.exp(sink - top))
        for i in range(seqs):
            summed = sum(lane_column(scale, i) * part[i] for scale, part in zip(scales, parts))
            head_out = summed * lane_column(inverse, i)
            own_o[s, pl.ds(i * heads, heads), :] = head_out.astype(jnp.bfloat16).astype(jnp.float32)
        send(own_o.at[s], other_o.at[s], o_send.at[s], o_recv.at[s], partner)

    def head_rows(ref):
        columns = []
        for h in range(heads):
            columns.append(jnp.concatenate(
                [ref[s, pl.ds(h, seqs, stride=heads), :] for s in range(SUBS)], axis=0).astype(jnp.bfloat16))
        return jnp.concatenate(columns, axis=1)

    own_rows = head_rows(own_o)
    w_copies[0].wait()
    for q in range(SUBS):
        part = jnp.dot(own_rows, wbuf[0, :, pl.ds(q * cols_sub, cols_sub)], preferred_element_type=jnp.float32)
        for r in range(RING):
            z[q, r] = part[r * block_rows : (r + 1) * block_rows]
    for s in range(SUBS):
        arrived(other_o.at[s], o_recv.at[s])
    other_rows = head_rows(other_o)
    w_copies[1].wait()
    for q in range(SUBS):
        part = jnp.dot(other_rows, wbuf[1, :, pl.ds(q * cols_sub, cols_sub)], preferred_element_type=jnp.float32)
        for r in range(RING):
            z[q, r] += part[r * block_rows : (r + 1) * block_rows]
        send(z.at[q, yo], yrl.at[q], d_send.at[0, q], yrl_recv.at[q], to_yn)
        send(z.at[q, yp], yrd.at[q], d_send.at[1, q], yrd_recv.at[q], to_yp)
    for q in range(SUBS):
        arrived(yrl.at[q], yrl_recv.at[q])
        ym[q] = z[q, yn] + yrl[q]
        send(ym.at[q], yrm.at[q], d_send.at[2, q], yrm_recv.at[q], to_yn)
    x_copy.wait()

    def store(q, xx, yy, core, value):
        rows = pl.ds(pl.multiple_of((xx * RING + yy) * block_rows, block_rows), block_rows)
        cols = pl.ds(pl.multiple_of(core * cols_core + q * cols_sub, LANES), cols_sub)
        out_ref[rows, cols] = value.astype(jnp.bfloat16)

    def slot(q, first, second):
        return (first, second) if q == 0 else (second, first)

    ahead = ((to_xn, to_xp), (to_yn, to_yp))
    first_now, first_n, first_p, first_o = (x, y), (xn, yn), (xp, yp), (xo, yo)

    def push(q, first, second, kind, where):
        xx, yy = slot(q, first, second)
        send(g.at[q, xx, yy], g.at[q, xx, yy], g_send.at[q, xx, yy, kind], g_recv.at[q, xx, yy], where)

    def share(q, first, second):
        xx, yy = slot(q, first, second)
        send(g.at[q, xx, yy], gp.at[q, xx, yy], gp_send.at[q, xx, yy], gp_recv.at[q, xx, yy], partner)

    def receive(q, first, second):
        xx, yy = slot(q, first, second)
        arrived(g.at[q, xx, yy], g_recv.at[q, xx, yy])

    def keep(q, first, second):
        xx, yy = slot(q, first, second)
        store(q, xx, yy, c, g[q, xx, yy])

    for q in range(SUBS):
        arrived(yrd.at[q], yrd_recv.at[q])
        arrived(yrm.at[q], yrm_recv.at[q])
        cols = pl.ds(q * cols_sub, cols_sub)
        bias = bo_ref[:, pl.ds(pl.multiple_of(c * cols_core + q * cols_sub, LANES), cols_sub)]
        summed = z[q, y] + yrd[q] + yrm[q]
        final = xbuf[:, cols].astype(jnp.float32) + summed + bias.astype(jnp.float32)
        g[q, x, y] = final.astype(jnp.bfloat16).astype(jnp.float32)
        for axis in (q, 1 - q):
            for kind in range(2):
                push(q, first_now[q], first_now[1 - q], 2 * (axis != q) + kind, ahead[axis][kind])
        share(q, first_now[q], first_now[1 - q])

    def spread(q, first, forward):
        other = 1 - q
        receive(q, first, first_now[other])
        if forward:
            push(q, first, first_now[other], 0, ahead[q][0])
        for kind in range(2):
            push(q, first, first_now[other], 2 + kind, ahead[other][kind])
        share(q, first, first_now[other])
        keep(q, first, first_now[other])

    def settle(q, first, second, forward):
        receive(q, first, second)
        if forward:
            push(q, first, second, 2, ahead[1 - q][0])
        share(q, first, second)
        keep(q, first, second)

    both = range(SUBS)
    for q in both:
        spread(q, first_p[q], True)
    for q in both:
        spread(q, first_n[q], False)
    for q in both:
        keep(q, first_now[q], first_now[1 - q])
    for q in both:
        settle(q, first_now[q], first_p[1 - q], True)
    for q in both:
        settle(q, first_now[q], first_n[1 - q], False)
    for q in both:
        spread(q, first_o[q], False)
    for first in (first_p, first_n):
        for q in both:
            settle(q, first[q], first_p[1 - q], True)
        for q in both:
            settle(q, first[q], first_n[1 - q], False)
    for q in both:
        settle(q, first_now[q], first_o[1 - q], False)
    for q in both:
        settle(q, first_o[q], first_p[1 - q], True)
    for q in both:
        settle(q, first_o[q], first_n[1 - q], False)
    for first in (first_p, first_n, first_o):
        for q in both:
            settle(q, first[q], first_o[1 - q], False)
    orders = [first_now, first_p, first_n, first_o]
    for xi in range(RING):
        for yi in range(RING):
            for q in both:
                xx, yy = slot(q, orders[xi][q], orders[yi][1 - q])
                arrived(gp.at[q, xx, yy], gp_recv.at[q, xx, yy])
                store(q, xx, yy, 1 - c, gp[q, xx, yy])
    for copy in sends:
        copy.wait_send()


def combine(p, sinks, hidden, b_o, w_o):
    seqs = p.shape[3] - 1
    heads = p.shape[4]
    num_seqs, d_model = hidden.shape
    cols_core = d_model // CORES
    cols_sub = cols_core // SUBS
    block_rows = num_seqs // (RING * RING)
    part = (seqs + 1, heads, LANES)
    f32, bf16 = jnp.float32, jnp.bfloat16
    dma = pltpu.SemaphoreType.DMA
    vmem = pl.BlockSpec(memory_space=pltpu.VMEM)
    hbm = pl.BlockSpec(memory_space=pl.ANY)
    chunk = (block_rows, cols_sub)
    return pl.pallas_call(
        functools.partial(combine_kernel, seqs),
        out_shape=jax.ShapeDtypeStruct((num_seqs, d_model), bf16),
        in_specs=[vmem, vmem, hbm, vmem, hbm],
        out_specs=vmem,
        scratch_shapes=[
            pltpu.VMEM((RING, SUBS) + part, f32),
            pltpu.VMEM((RING, SUBS) + part, f32),
            pltpu.VMEM((SUBS,) + part, f32),
            pltpu.VMEM((SUBS,) + part, f32),
            pltpu.VMEM((SUBS,) + part, f32),
            pltpu.VMEM((SUBS, seqs * heads, LANES), f32),
            pltpu.VMEM((SUBS, seqs * heads, LANES), f32),
            pltpu.VMEM((2, w_o.shape[0] // 2, cols_core), bf16),
            pltpu.VMEM((block_rows, cols_core), bf16),
            pltpu.VMEM((SUBS, RING) + chunk, f32),
            pltpu.VMEM((SUBS,) + chunk, f32),
            pltpu.VMEM((SUBS,) + chunk, f32),
            pltpu.VMEM((SUBS,) + chunk, f32),
            pltpu.VMEM((SUBS,) + chunk, f32),
            pltpu.VMEM((SUBS, RING, RING) + chunk, f32),
            pltpu.VMEM((SUBS, RING, RING) + chunk, f32),
            dma((2,)), dma((1,)), dma((RING, SUBS)), dma((RING, SUBS)), dma((3, SUBS)),
            dma((SUBS,)), dma((SUBS,)), dma((SUBS,)), dma((SUBS,)), dma((SUBS,)),
            dma((3, SUBS)), dma((SUBS,)), dma((SUBS,)), dma((SUBS,)),
            dma((SUBS, RING, RING, 4)), dma((SUBS, RING, RING)), dma((SUBS, RING, RING)), dma((SUBS, RING, RING)),
        ],
        compiler_params=pltpu.CompilerParams(collective_id=0, has_side_effects=True, vmem_limit_bytes=48 * 2**20),
        cost_estimate=pl.CostEstimate(flops=2 * num_seqs // RING * w_o.shape[0] * cols_core, bytes_accessed=30 * 2**20, transcendentals=0),
        name="combine",
    )(p, sinks, hidden, b_o, w_o)


def rotate_half(heads_in, cos_part, sin_part):
    half_dim = heads_in.shape[-1] // 2
    first_half = heads_in[..., :half_dim]
    second_half = heads_in[..., half_dim:]
    return jnp.concatenate([first_half * cos_part - second_half * sin_part, second_half * cos_part + first_half * sin_part], axis=-1)


def local_partials(hidden, seq_lens, rope_cos, rope_sin, k_cache, v_cache, norm_gain, w_qkv, b_qkv, sink_logits):
    num_seqs, ctx_local, kv_local, head_dim = k_cache.shape
    group_size = w_qkv.shape[2] // head_dim - 2
    x_wide = hidden.astype(jnp.float32)
    inv_rms = lax.rsqrt(jnp.mean(x_wide * x_wide, axis=-1, keepdims=True) + NORM_EPS)
    normed = (x_wide * inv_rms * norm_gain.astype(jnp.float32)).astype(jnp.bfloat16)
    qkv_all = jnp.einsum("bd,dkc->bkc", normed, w_qkv, preferred_element_type=jnp.float32) + b_qkv.astype(jnp.float32)
    qkv_all = qkv_all.reshape(num_seqs, kv_local, group_size + 2, head_dim)
    q_rot = rotate_half(qkv_all[:, :, :group_size], rope_cos[:, None, None, :], rope_sin[:, None, None, :]).astype(jnp.bfloat16)
    k_new = rotate_half(qkv_all[:, :, group_size], rope_cos[:, None, :], rope_sin[:, None, :]).astype(jnp.bfloat16)
    v_new = qkv_all[:, :, group_size + 1].astype(jnp.bfloat16)
    positions = lax.axis_index("sp") * ctx_local + jnp.arange(ctx_local)
    is_new = (positions[None, :] == seq_lens[:, None])[:, :, None, None]
    k_out = jnp.where(is_new, k_new[:, None], k_cache)
    v_out = jnp.where(is_new, v_new[:, None], v_cache)
    logits = jnp.einsum("bkgd,blkd->bkgl", q_rot, k_out, preferred_element_type=jnp.float32) * head_dim ** -0.5
    logits = jnp.where((positions[None, :] <= seq_lens[:, None])[:, None, None, :], logits, -jnp.inf)
    row_max = jnp.maximum(jnp.max(logits, axis=-1), sink_logits.reshape(kv_local, group_size))
    weights = jnp.exp(logits - row_max[..., None])
    row_sum = jnp.sum(weights, axis=-1)
    weighted = jnp.einsum("bkgl,blkd->bkgd", weights.astype(jnp.bfloat16), v_out, preferred_element_type=jnp.float32)
    seqs = num_seqs // (RING * SUBS)
    numer = weighted.reshape(RING, SUBS, seqs, kv_local, group_size, head_dim).transpose(0, 1, 3, 2, 4, 5)
    stat = lambda a: a.reshape(RING, SUBS, seqs, kv_local, group_size).transpose(0, 1, 3, 4, 2)
    pad = jnp.zeros((RING, SUBS, kv_local, group_size, HALF - seqs), jnp.float32)
    stats = jnp.concatenate([stat(row_max), pad, stat(row_sum), pad], axis=-1)
    return jnp.concatenate([numer, stats[:, :, :, None]], axis=3), k_out, v_out


def solution(mesh):
    cache_spec = P("dp", "sp", "tp", None)

    def block_step(hidden, seq_lens, rope_cos, rope_sin, k_cache, v_cache, norm_gain, w_qkv, b_qkv, sink_logits, w_o, b_o):
        packed, k_out, v_out = local_partials(hidden, seq_lens, rope_cos, rope_sin, k_cache, v_cache, norm_gain, w_qkv, b_qkv, sink_logits)
        sinks = jnp.broadcast_to(sink_logits[:, None], (sink_logits.shape[0], LANES))
        out_hidden = combine(packed, sinks, hidden, b_o[None, :], w_o)
        return out_hidden, k_out, v_out

    return jax.shard_map(block_step, mesh=mesh, in_specs=(P("dp", None), P("dp"), P("dp", None), P("dp", None), cache_spec, cache_spec, P(None), P(None, "tp", None), P("tp", None), P("tp"), P("tp", None), P(None)), out_specs=(P("dp", None), cache_spec, cache_spec), check_vma=False)
```

time: 190 us -> 93 us (0.49)
  waiting for transfers between devices: 114 us -> 0 us
  Pallas kernels: 0 us -> 41.3 us
  between operations: 14.3 us -> 0.84 us
  starting transfers between devices: 6.01 us -> 0 us
  other arithmetic: 23.8 us -> 19.3 us
  matrix products: 26.7 us -> 23 us
  local copies, waits for them, and re-layouts: 4.79 us -> 7.98 us
    psum x1 -> x0, waiting for transfers between devices: 99.3 us -> none  [block_step(): summed = lax.psum(partial_out, ('tp', 'sp'))]
    pallas_call x0 -> x1, Pallas kernels: none -> 41.3 us  [combine(): pl.pallas_call(functools.partial(combine_kernel, seqs), out_shape=jax.Sha...]
    all_to_all x1 -> x0, waiting for transfers between devices: 14.9 us -> none  [block_step(): lax.all_to_all(packed.reshape(num_seqs, sp_size, head_share, width), 'sp'...]
    all_to_all x1 -> x0, starting transfers between devices: 6.01 us -> none  [block_step(): lax.all_to_all(packed.reshape(num_seqs, sp_size, head_share, width), 'sp'...]
    dot_general x1 -> x0, matrix products: 3.82 us -> none  [block_step(): jnp.dot(combined.astype(jnp.bfloat16).reshape(num_seqs, head_share * head...]
    convert_element_type x3 -> x0, other arithmetic: 3.25 us -> none  [the longest x1 3.13 us: block_step(): (hidden.astype(jnp.float32) + summed + b_o.astype(jnp.float32)).astype(jn...]
    unnamed x19 -> x14, local copies, waits for them, and re-layouts: 1.91 us -> 4.72 us
  transfers between devices with their start and end apart: 2 -> 0, of which waited for: 2 -> 0; matrix products, arithmetic and copies ran while one was open for 0% -> 0% of each run, Pallas kernels for 0% -> 0%
where the time goes in v1:
time: 93 us; the launch traced here: 92.4 us
  Pallas kernels  41.3 us (44%)
  matrix products  23 us (25%)
  other arithmetic  19.3 us (21%)
  local copies, waits for them, and re-layouts  7.98 us (9%)
    pallas_call x1, Pallas kernels, combine(): pl.pallas_call(functools.partial(combine_kernel, seqs), out_shape=jax.Sha...  41.3 us
    dot_general x1, matrix products, local_partials(): jnp.einsum('bd,dkc->bkc', normed, w_qkv, preferred_element_type=jnp.float32)  16.9 us
    select_n x1, other arithmetic, local_partials(): v_out = jnp.where(is_new, v_new[:, None], v_cache)  14.1 us
    unnamed x14, local copies, waits for them, and re-layouts  4.72 us
    dot_general x1, matrix products, local_partials(): jnp.einsum('bkgl,blkd->bkgd', weights.astype(jnp.bfloat16), v_out, prefer...  3.47 us
    dot_general x1, matrix products, local_partials(): jnp.einsum('bkgd,blkd->bkgl', q_rot, k_out, preferred_element_type=jnp.fl...  2.59 us

profile of v1, /device:TPU:97, one launch (start us, length us, event | category | flops | bytes accessed | tf_op | source)
XLA Modules:
  0.0 92.4 jit_solution(8003179163404209629)
XLA Ops:
  0.6 1.7 %fusion.9 = f32[128]{0:T(128)S(1)} fusion(bf16[128,5120]{1,0:T(8,128)(2,1)} %x_hbm.1), kind=kLoop, calls=%fused_computation.11 | loop fusion | flops 1965952 | bytes 1311232 | tf_op jit(solution)/shard_map/reduce_sum | solution.py:306
  2.3 0.7 max.19
  3.1 0.7 broadcast_in_dim.74.sink_ref
  3.8 0.7 convert_element_type.32
  4.5 0.7 convert_element_type.30
  5.2 0.7 broadcast_in_dim.75.bo_ref
  5.9 0.7 broadcast_compare_fusion.1
  6.7 0.8 copy.44
  7.5 0.9 copy.46
  8.4 16.9 %fusion.6 = f32[128,2,1280]{2,0,1:T(8,128)S(1)} fusion(bf16[5120,2,1280]{2,1,0:T(2,128)(2,1)} %param.19, bf16[128,5120]{1,0:T(8,128)(2,1)} %x_hbm.1, f32[5120]{0:T(1024)S(1)} %convert_element_type.30, f32[128]{0:T(128)S(1)} %add_rsqrt_fusion, f32[2,1280]{1,0:T(2,128)S(1)} %convert_element_type.32), kind=kOutput, calls=%fused_computation.10 | convolution fusion | flops 3358392320 | bytes 28867072 | tf_op jit(solution)/shard_map/bd,dkc->bkc/dot_general | solution.py:308
  25.3 0.0 copy-start.2
  25.3 0.0 copy-start.3
  25.3 0.4 copy.42
  25.7 0.1 copy.50
  25.9 0.1 fusion.31
  26.0 0.1 copy-done.2
  26.0 0.0 copy-done.3
  26.1 0.1 copy.47
  26.2 0.5 copy.64
  26.7 0.5 copy.63
  27.2 0.3 subtract_convert_fusion
  27.5 14.1 %broadcast_select_fusion = (bf16[128,64,2,128]{3,2,1,0:T(2,128)(2,1)}, bf16[128,64,2,128]{3,2,1,0:T(2,128)(2,1)S(1)}) fusion(bf16[128,64,2,128]{3,2,1,0:T(2,128)(2,1)} %param.17, pred[128,64]{1,0:T(8,128)(4,1)S(1)} %get-tuple-element.12, bf16[128,2,128]{2,1,0:T(2,128)(2,1)S(1)} %copy.50, bf16[128,64,2,128]{3,2,1,0:T(2,128)(2,1)} %param.16, ...), kind=kLoop, calls=%fused_computation.2 | loop fusion | flops 4194304 | bytes 16916480 | tf_op jit(solution)/shard_map/jit(_where)/select_n | solution.py:316
  41.6 0.0 copy-start.1
  41.7 2.6 %fusion.32 = (f32[128,2,8]{2,1,0:T(2,128)S(1)}, f32[128,2,8,64]{3,2,1,0:T(8,128)S(1)}) fusion(bf16[128,64,2,128]{3,2,1,0:T(2,128)(2,1)S(1)} %get-tuple-element.19, bf16[128,2,8,64]{3,2,1,0:T(8,128)(2,1)S(1)} %get-tuple-element.4, bf16[128,2,8,64]{3,2,1,0:T(8,128)(2,1)S(1)} %get-tuple-element.3, pred[128,64]{1,0:T(8,128)(4,1)S(1)} %get-tuple-element.11), kind=kOutput, calls=%fused_computation.45 | convolution fusion | flops 34994176 | bytes 5259264 | tf_op jit(solution)/shard_map/bkgd,blkd->bkgl/dot_general | solution.py:317
  44.3 0.0 copy-done.1
  44.3 0.1 copy.54
  44.4 0.1 maximum_bitcast_fusion.1
  44.5 0.8 fusion.22
  45.2 3.5 %fusion.2 = f32[128,2,8,128]{3,2,1,0:T(8,128)S(1)} fusion(bf16[128,64,2,128]{3,2,1,0:T(2,128)(2,1)} %get-tuple-element.20, f32[128,2,8,64]{3,2,1,0:T(8,128)S(1)} %get-tuple-element.14, f32[128,2,8]{2,1,0:T(2,128)S(1)} %bitcast.31), kind=kOutput, calls=%fused_computation.4 | convolution fusion | flops 33816576 | bytes 5775360 | tf_op jit(solution)/shard_map/bkgl,blkd->bkgd/dot_general | solution.py:322
  48.7 0.0 copy-start
  48.7 0.1 copy.80
  48.8 0.1 copy.56
  49.0 0.1 maximum_bitcast_fusion
  49.1 0.1 pad_maximum_fusion.p_ref
  49.2 0.9 copy-done
  50.0 41.3 %combine.1 = bf16[128,5120]{1,0:T(8,128)(2,1)S(1)} custom-call(f32[4,2,2,17,8,128]{5,4,3,2,1,0:T(8,128)S(1)} %pad_maximum_fusion.p_ref, f32[16,128]{1,0:T(8,128)S(1)} %broadcast_in_dim.74.sink_ref, bf16[128,5120]{1,0:T(8,128)(2,1)S(1)} %copy-done, bf16[1,5120]{1,0:T(2,128)(2,1)S(1)} %broadcast_in_dim.75.bo_ref, bf16[2048,5120]{1,0:T(8,128)(2,1)} %wo_hbm.1), custom_call_target="tpu_custom_call" | custom-call | flops 335544320 | bytes 31457280 | tf_op jit(solution)/shard_map/combine/pallas_call | solution.py:262
  91.4 1.1 %copy.82 = bf16[128,5120]{1,0:T(8,128)(2,1)} copy(bf16[128,5120]{1,0:T(8,128)(2,1)S(1)} %combine.1) | data formatting | bytes 2621440
  (9 shorter events, 0.1 us)
Async XLA Ops:
  25.3 0.8 copy-start.2
  25.3 0.8 copy-start.3
  41.6 2.6 %copy-start.1 = (bf16[128,64,2,128]{3,2,1,0:T(2,128)(2,1)}, bf16[128,64,2,128]{3,2,1,0:T(2,128)(2,1)S(1)}, u32[]{:S(2)}) copy-start(bf16[128,64,2,128]{3,2,1,0:T(2,128)(2,1)S(1)} %get-tuple-element.19) | copy-start | bytes 12582916
  48.7 1.3 %copy-start = (bf16[128,5120]{1,0:T(8,128)(2,1)S(1)}, bf16[128,5120]{1,0:T(8,128)(2,1)}, u32[]{:S(2)}) copy-start(bf16[128,5120]{1,0:T(8,128)(2,1)} %x_hbm.1) | copy-start | bytes 3932164

commit v2 on v1

--- a/solution.py
+++ b/solution.py
@@ -292,49 +292,221 @@
     )(p, sinks, hidden, b_o, w_o)
 
 
-def rotate_half(heads_in, cos_part, sin_part):
-    half_dim = heads_in.shape[-1] // 2
-    first_half = heads_in[..., :half_dim]
-    second_half = heads_in[..., half_dim:]
-    return jnp.concatenate([first_half * cos_part - second_half * sin_part, second_half * cos_part + first_half * sin_part], axis=-1)
-
-
-def local_partials(hidden, seq_lens, rope_cos, rope_sin, k_cache, v_cache, norm_gain, w_qkv, b_qkv, sink_logits):
-    num_seqs, ctx_local, kv_local, head_dim = k_cache.shape
-    group_size = w_qkv.shape[2] // head_dim - 2
-    x_wide = hidden.astype(jnp.float32)
-    inv_rms = lax.rsqrt(jnp.mean(x_wide * x_wide, axis=-1, keepdims=True) + NORM_EPS)
-    normed = (x_wide * inv_rms * norm_gain.astype(jnp.float32)).astype(jnp.bfloat16)
-    qkv_all = jnp.einsum("bd,dkc->bkc", normed, w_qkv, preferred_element_type=jnp.float32) + b_qkv.astype(jnp.float32)
-    qkv_all = qkv_all.reshape(num_seqs, kv_local, group_size + 2, head_dim)
-    q_rot = rotate_half(qkv_all[:, :, :group_size], rope_cos[:, None, None, :], rope_sin[:, None, None, :]).astype(jnp.bfloat16)
-    k_new = rotate_half(qkv_all[:, :, group_size], rope_cos[:, None, :], rope_sin[:, None, :]).astype(jnp.bfloat16)
-    v_new = qkv_all[:, :, group_size + 1].astype(jnp.bfloat16)
-    positions = lax.axis_index("sp") * ctx_local + jnp.arange(ctx_local)
-    is_new = (positions[None, :] == seq_lens[:, None])[:, :, None, None]
-    k_out = jnp.where(is_new, k_new[:, None], k_cache)
-    v_out = jnp.where(is_new, v_new[:, None], v_cache)
-    logits = jnp.einsum("bkgd,blkd->bkgl", q_rot, k_out, preferred_element_type=jnp.float32) * head_dim ** -0.5
-    logits = jnp.where((positions[None, :] <= seq_lens[:, None])[:, None, None, :], logits, -jnp.inf)
-    row_max = jnp.maximum(jnp.max(logits, axis=-1), sink_logits.reshape(kv_local, group_size))
-    weights = jnp.exp(logits - row_max[..., None])
-    row_sum = jnp.sum(weights, axis=-1)
-    weighted = jnp.einsum("bkgl,blkd->bkgd", weights.astype(jnp.bfloat16), v_out, preferred_element_type=jnp.float32)
+def front_kernel(
+    logit_scale, x_hbm, len_hbm, cos_hbm, sin_hbm, k_hbm, v_hbm, gain_hbm, w_hbm, bias_hbm, sink_hbm,
+    p_ref, k_out, v_out,
+    xbuf, lens, cos, sin, gain, bias, sinks, hexp, wbuf, acc, qs, kn, vn, kbuf, vbuf,
+    in_sem, w_sem, k_sem, v_sem, ko_sem, vo_sem,
+):
+    num_seqs, d_model = x_hbm.shape
+    kv = w_hbm.shape[1]
+    qkv = w_hbm.shape[2]
+    tiles = qkv // LANES
+    heads = tiles - 2
+    slots, _, depth2, _ = wbuf.shape
+    chunks = d_model * kv // depth2
+    blocks, _, seqs1 = p_ref.shape[0], p_ref.shape[1], p_ref.shape[2]
+    seqs = seqs1 - 1
+    ctx2 = k_hbm.shape[1]
+    w_rows = w_hbm.reshape(d_model * kv, qkv)
+
+    def w_copy(chunk, slot, t):
+        return pltpu.make_async_copy(
+            w_rows.at[pl.ds(pl.multiple_of(chunk * depth2, depth2), depth2), pl.ds(t * LANES, LANES)],
+            wbuf.at[slot, t], w_sem.at[slot])
+
+    def w_start(chunk, slot):
+        for t in range(tiles):
+            w_copy(chunk, slot, t).start()
+
+    small = [
+        pltpu.make_async_copy(src, dst, in_sem.at[i])
+        for i, (src, dst) in enumerate((
+            (x_hbm, xbuf), (gain_hbm, gain), (len_hbm, lens), (cos_hbm, cos), (sin_hbm, sin), (bias_hbm, bias), (sink_hbm, sinks)))
+    ]
+    for copy in small:
+        copy.start()
+    for slot in range(slots - 1):
+        w_start(slot, slot)
+
+    def cache_copy(hbm, buf, sem, block, out):
+        rows = pl.ds(block * seqs, seqs)
+        src, dst = hbm.at[rows], buf.at[rows]
+        return pltpu.make_async_copy(dst, src, sem.at[block]) if out else pltpu.make_async_copy(src, dst, sem.at[block])
+
+    small[0].wait()
+    small[1].wait()
+    row = lax.broadcasted_iota(jnp.int32, (LANES, kv * LANES), 0)
+    col = lax.broadcasted_iota(jnp.int32, (LANES, kv * LANES), 1)
+    picks = [(col == row * kv + k).astype(jnp.bfloat16) for k in range(kv)]
+    square = jnp.zeros((num_seqs, LANES), jnp.float32)
+    for t in range(d_model // LANES):
+        xt = xbuf[:, t * LANES : (t + 1) * LANES].astype(jnp.float32)
+        square += xt * xt
+    inv_rms = lax.rsqrt(jnp.sum(square, axis=-1, keepdims=True) / d_model + NORM_EPS)
+    per_chunk = depth2 // (kv * LANES)
+    for t in range(d_model // LANES):
+        xt = xbuf[:, t * LANES : (t + 1) * LANES].astype(jnp.float32)
+        ht = (xt * inv_rms * gain[:, t * LANES : (t + 1) * LANES].astype(jnp.float32)).astype(jnp.bfloat16)
+        for k in range(kv):
+            spread = jnp.dot(ht, picks[k], preferred_element_type=jnp.float32).astype(jnp.bfloat16)
+            place = t % per_chunk * kv * LANES
+            hexp[t // per_chunk, k * num_seqs : (k + 1) * num_seqs, place : place + kv * LANES] = spread
+    acc[...] = jnp.zeros_like(acc)
+
+    @pl.loop(0, chunks)
+    def _(chunk):
+        slot = lax.rem(chunk, slots)
+
+        @pl.when(chunk + slots - 1 < chunks)
+        def _():
+            w_start(chunk + slots - 1, lax.rem(chunk + slots - 1, slots))
+
+        @pl.when(chunk == chunks - slots)
+        def _():
+            for block in range(blocks):
+                cache_copy(k_hbm, kbuf, k_sem, block, False).start()
+                cache_copy(v_hbm, vbuf, v_sem, block, False).start()
+
+        for t in range(tiles):
+            w_copy(chunk, slot, t).wait()
+        lhs = hexp.at[chunk]
+        for t in range(0, tiles, 2):
+            rhs = jnp.concatenate([wbuf[slot, t], wbuf[slot, t + 1]], axis=1)
+            cols = slice(t * LANES, (t + 2) * LANES)
+            acc[:, cols] += jnp.dot(lhs[...], rhs, preferred_element_type=jnp.float32)
+
+    for copy in small[2:]:
+        copy.wait()
+    cos_t = jnp.transpose(jnp.concatenate([cos[...], cos[...]], axis=0))
+    sin_t = jnp.transpose(jnp.concatenate([-sin[...], sin[...]], axis=0))
+
+    def rotate(t):
+        return t * cos_t + pltpu.roll(t, HALF, 1) * sin_t
+
+    def rounded(t):
+        return t.astype(jnp.bfloat16).astype(jnp.float32)
+
+    for k in range(kv):
+        for t in range(tiles):
+            cols = slice(t * LANES, (t + 1) * LANES)
+            value = acc[k * num_seqs : (k + 1) * num_seqs, cols] + bias[k : k + 1, cols].astype(jnp.float32)
+            if t < heads:
+                qs[pl.ds(k * heads + t, num_seqs, stride=kv * heads), :] = rotate(value)
+            elif t == heads:
+                kn[pl.ds(k, num_seqs, stride=kv), :] = rotate(value)
+            else:
+                vn[pl.ds(k, num_seqs, stride=kv), :] = value
+
+    q_rows = kv * heads
+    base = lax.axis_index("sp") * (ctx2 // kv)
+    row = lax.broadcasted_iota(jnp.int32, (q_rows, LANES), 0)
+    lane = lax.broadcasted_iota(jnp.int32, (q_rows, LANES), 1)
+    assert ctx2 == LANES
+    position = jnp.where(lane % kv == row // heads, lane // kv + base, jnp.iinfo(jnp.int32).max)
+    sink = jnp.zeros((q_rows, LANES), jnp.float32)
+    for i in range(q_rows):
+        sink = jnp.where(row == i, sinks[i], sink)
+    sink_col = jnp.max(sink, axis=-1, keepdims=True)
+    group = 16
+    group_row = lax.broadcasted_iota(jnp.int32, (group, LANES), 0)
+
+    @pl.loop(0, blocks)
+    def _(block):
+        cache_copy(k_hbm, kbuf, k_sem, block, False).wait()
+        cache_copy(v_hbm, vbuf, v_sem, block, False).wait()
+        stats = jnp.zeros((q_rows, LANES), jnp.float32)
+        for i in range(seqs):
+            b = block * seqs + i
+            n = lens[b]
+            local = n - base
+            here = jnp.logical_and(local >= 0, local < ctx2 // kv)
+            place = jnp.where(here, local * kv, 0)
+            start = pl.multiple_of(place // group * group, group)
+            target = jnp.where(here, place - start, group)
+            for buf, new in ((kbuf, kn), (vbuf, vn)):
+                fresh = new[pl.ds(b * kv, kv), :]
+                value = buf[b, pl.ds(start, group), :].astype(jnp.float32)
+                for k in range(kv):
+                    value = jnp.where(group_row == target + k, fresh[k : k + 1], value)
+                buf[b, pl.ds(start, group), :] = value.astype(jnp.bfloat16)
+        for i in range(seqs):
+            b = block * seqs + i
+            q = qs[pl.ds(pl.multiple_of(b * q_rows, q_rows), q_rows), :].astype(jnp.bfloat16)
+            logits = lax.dot_general(q, kbuf[b], (((1,), (1,)), ((), ())), preferred_element_type=jnp.float32) * logit_scale
+            logits = jnp.where(position <= lens[b], logits, -jnp.inf)
+            top = jnp.maximum(jnp.max(logits, axis=-1, keepdims=True), sink_col)
+            weights = jnp.exp(logits - top)
+            total = jnp.sum(weights, axis=-1, keepdims=True)
+            numer = jnp.dot(weights.astype(jnp.bfloat16), vbuf[b], preferred_element_type=jnp.float32)
+            for k in range(kv):
+                p_ref[block, k, i] = numer[k * heads : (k + 1) * heads]
+            stats = jnp.where(lane == i, top, jnp.where(lane == HALF + i, total, stats))
+        for k in range(kv):
+            p_ref[block, k, seqs] = stats[k * heads : (k + 1) * heads]
+        cache_copy(k_out, kbuf, ko_sem, block, True).start()
+        cache_copy(v_out, vbuf, vo_sem, block, True).start()
+
+    for block in range(blocks):
+        cache_copy(k_out, kbuf, ko_sem, block, True).wait()
+        cache_copy(v_out, vbuf, vo_sem, block, True).wait()
+
+
+def front(hidden, seq_lens, cos_t, sin_t, k_cache, v_cache, gain, w_qkv, b_qkv, sinks):
+    num_seqs, d_model = hidden.shape
+    kv, qkv = w_qkv.shape[1:]
+    tiles = qkv // LANES
+    heads = tiles - 2
     seqs = num_seqs // (RING * SUBS)
-    numer = weighted.reshape(RING, SUBS, seqs, kv_local, group_size, head_dim).transpose(0, 1, 3, 2, 4, 5)
-    stat = lambda a: a.reshape(RING, SUBS, seqs, kv_local, group_size).transpose(0, 1, 3, 4, 2)
-    pad = jnp.zeros((RING, SUBS, kv_local, group_size, HALF - seqs), jnp.float32)
-    stats = jnp.concatenate([stat(row_max), pad, stat(row_sum), pad], axis=-1)
-    return jnp.concatenate([numer, stats[:, :, :, None]], axis=3), k_out, v_out
+    ctx2 = k_cache.shape[1]
+    depth2 = 1024
+    chunks = d_model * kv // depth2
+    slots = 4
+    f32, bf16 = jnp.float32, jnp.bfloat16
+    dma = pltpu.SemaphoreType.DMA
+    hbm = pl.BlockSpec(memory_space=pl.ANY)
+    cache = jax.ShapeDtypeStruct(k_cache.shape, bf16)
+    return pl.pallas_call(
+        functools.partial(front_kernel, LANES ** -0.5),
+        out_shape=(jax.ShapeDtypeStruct((RING * SUBS, kv, seqs + 1, heads, LANES), f32), cache, cache),
+        in_specs=[hbm] * 10,
+        out_specs=(pl.BlockSpec(memory_space=pltpu.VMEM), hbm, hbm),
+        scratch_shapes=[
+            pltpu.VMEM(hidden.shape, bf16),
+            pltpu.SMEM(seq_lens.shape, jnp.int32),
+            pltpu.VMEM(cos_t.shape, f32),
+            pltpu.VMEM(sin_t.shape, f32),
+            pltpu.VMEM(gain.shape, bf16),
+            pltpu.VMEM(b_qkv.shape, bf16),
+            pltpu.SMEM(sinks.shape, f32),
+            pltpu.VMEM((chunks, kv * num_seqs, depth2), bf16),
+            pltpu.VMEM((slots, tiles, depth2, LANES), bf16),
+            pltpu.VMEM((kv * num_seqs, qkv), f32),
+            pltpu.VMEM((num_seqs * kv * heads, LANES), f32),
+            pltpu.VMEM((num_seqs * kv, LANES), f32),
+            pltpu.VMEM((num_seqs * kv, LANES), f32),
+            pltpu.VMEM(k_cache.shape, bf16),
+            pltpu.VMEM(v_cache.shape, bf16),
+            dma((7,)), dma((slots,)), dma((RING * SUBS,)), dma((RING * SUBS,)), dma((RING * SUBS,)), dma((RING * SUBS,)),
+        ],
+        compiler_params=pltpu.CompilerParams(vmem_limit_bytes=44 * 2**20),
+        cost_estimate=pl.CostEstimate(flops=4 * num_seqs * d_model * kv * qkv, bytes_accessed=50 * 2**20, transcendentals=0),
+        name="front",
+    )(hidden, seq_lens, cos_t, sin_t, k_cache, v_cache, gain, w_qkv, b_qkv, sinks)
 
 
 def solution(mesh):
     cache_spec = P("dp", "sp", "tp", None)
 
     def block_step(hidden, seq_lens, rope_cos, rope_sin, k_cache, v_cache, norm_gain, w_qkv, b_qkv, sink_logits, w_o, b_o):
-        packed, k_out, v_out = local_partials(hidden, seq_lens, rope_cos, rope_sin, k_cache, v_cache, norm_gain, w_qkv, b_qkv, sink_logits)
+        num_seqs, ctx, kv, head_dim = k_cache.shape
+        assert head_dim == LANES and mesh.shape["tp"] == RING and mesh.shape["sp"] == RING * CORES
+        flat = (num_seqs, ctx * kv, head_dim)
+        packed, k_out, v_out = front(
+            hidden, seq_lens, rope_cos.T, rope_sin.T, k_cache.reshape(flat), v_cache.reshape(flat), norm_gain[None, :], w_qkv, b_qkv, sink_logits)
+        packed = packed.reshape((RING, SUBS) + packed.shape[1:])
         sinks = jnp.broadcast_to(sink_logits[:, None], (sink_logits.shape[0], LANES))
         out_hidden = combine(packed, sinks, hidden, b_o[None, :], w_o)
-        return out_hidden, k_out, v_out
+        return out_hidden, k_out.reshape(k_cache.shape), v_out.reshape(v_cache.shape)
 
     return jax.shard_map(block_step, mesh=mesh, in_specs=(P("dp", None), P("dp"), P("dp", None), P("dp", None), cache_spec, cache_spec, P(None), P(None, "tp", None), P("tp", None), P("tp"), P("tp", None), P(None)), out_specs=(P("dp", None), cache_spec, cache_spec), check_vma=False)

time: 93 us -> 97.7 us (1.051)
  Pallas kernels: 41.3 us -> 86.4 us
  matrix products: 23 us -> 0 us
  other arithmetic: 19.3 us -> 0 us
  local copies, waits for them, and re-layouts: 7.98 us -> 10.2 us
    pallas_call x0 -> x1, Pallas kernels: none -> 45.1 us  [front(): pl.pallas_call(functools.partial(front_kernel, LANES ** (-0.5)), out_shap...]
    dot_general x3 -> x0, matrix products: 23 us -> none  [the longest x1 16.9 us: local_partials(): jnp.einsum('bd,dkc->bkc', normed, w_qkv, preferred_element_type=jnp.float32)]
    select_n x1 -> x0, other arithmetic: 14.1 us -> none  [local_partials(): v_out = jnp.where(is_new, v_new[:, None], v_cache)]
    unnamed x14 -> x17, local copies, waits for them, and re-layouts: 4.72 us -> 8.07 us
    reduce_sum x2 -> x0, other arithmetic: 2.41 us -> none  [the longest x1 1.65 us: local_partials(): jnp.mean(x_wide * x_wide, axis=-1, keepdims=True) + NORM_EPS]
    convert_element_type x2 -> x0, other arithmetic: 1.4 us -> none  [the longest x1 0.7 us: local_partials(): norm_gain.astype(jnp.float32)]
where the time goes in v2:
time: 97.7 us; the launch traced here: 97.3 us
  Pallas kernels  86.4 us (88%)
  local copies, waits for them, and re-layouts  10.2 us (10%)
    pallas_call x1, Pallas kernels, front(): pl.pallas_call(functools.partial(front_kernel, LANES ** (-0.5)), out_shap...  45.1 us
    pallas_call x1, Pallas kernels, combine(): pl.pallas_call(functools.partial(combine_kernel, seqs), out_shape=jax.Sha...  41.2 us
    unnamed x17, local copies, waits for them, and re-layouts  8.07 us

profile of v2, /device:TPU:97, one launch (start us, length us, event | category | flops | bytes accessed | tf_op | source)
XLA Modules:
  0.0 97.3 jit_solution(13574364384883834515)
XLA Ops:
  0.6 0.7 broadcast_in_dim.13.sink_ref
  1.4 0.7 broadcast_in_dim.12.gain_hbm
  2.1 0.7 broadcast_in_dim.14.bo_ref
  2.8 0.0 copy-start
  2.8 1.3 %copy-done = bf16[128,5120]{1,0:T(8,128)(2,1)S(1)} copy-done((bf16[128,5120]{1,0:T(8,128)(2,1)S(1)}, bf16[128,5120]{1,0:T(8,128)(2,1)}, u32[]{:S(2)}) %copy-start) | copy-done | bytes 1310744
  4.1 0.0 copy-start.2
  4.1 2.2 %copy-done.2 = bf16[128,64,2,128]{3,2,1,0:T(2,128)(2,1)S(1)} copy-done((bf16[128,64,2,128]{3,2,1,0:T(2,128)(2,1)S(1)}, bf16[128,64,2,128]{3,2,1,0:T(2,128)(2,1)}, u32[]{:S(2)}) %copy-start.2) | copy-done | bytes 4194328
  6.3 0.0 copy-start.3
  6.3 0.8 copy-done.3
  7.1 0.0 copy-start.4
  7.1 0.8 copy-done.4
  7.8 0.0 copy-start.5
  7.8 0.7 copy-done.5
  8.5 0.0 copy-start.6
  8.5 0.7 copy-done.6
  9.2 0.0 copy-start.7
  9.2 0.7 copy-done.7
  9.8 0.0 copy-start.1
  9.8 45.1 %front.1 = (f32[8,2,17,8,128]{4,3,2,1,0:T(8,128)S(1)}, bf16[128,128,128]{2,1,0:T(8,128)(2,1)}, bf16[128,128,128]{2,1,0:T(8,128)(2,1)}) custom-call(bf16[128,5120]{1,0:T(8,128)(2,1)S(1)} %copy-done, s32[128]{0:T(128)S(1)} %copy-done.7, f32[64,128]{1,0:T(8,128)S(1)} %bitcast.9, f32[64,128]{1,0:T(8,128)S(1)} %bitcast.10, bf16[128,128,128]{2,1,0:T(8,128)(2,1)S(1)} %bitcast.7, ...), custom_call_target="tpu_custom_call" | custom-call | flops 6710886400 | bytes 52428800 | tf_op jit(solution)/shard_map/front/pallas_call | solution.py:469
  55.0 0.0 copy-done.1
  55.0 41.2 %combine.1 = bf16[128,5120]{1,0:T(8,128)(2,1)S(1)} custom-call(f32[4,2,2,17,8,128]{5,4,3,2,1,0:T(8,128)S(1)} %bitcast.8, f32[16,128]{1,0:T(8,128)S(1)} %broadcast_in_dim.13.sink_ref, bf16[128,5120]{1,0:T(8,128)(2,1)S(1)} %copy-done.1, bf16[1,5120]{1,0:T(2,128)(2,1)S(1)} %broadcast_in_dim.14.bo_ref, bf16[2048,5120]{1,0:T(8,128)(2,1)} %wo_hbm.1), custom_call_target="tpu_custom_call" | custom-call | flops 335544320 | bytes 31457280 | tf_op jit(solution)/shard_map/combine/pallas_call | solution.py:262
  96.2 1.1 %copy.16 = bf16[128,5120]{1,0:T(8,128)(2,1)} copy(bf16[128,5120]{1,0:T(8,128)(2,1)S(1)} %combine.1) | data formatting | bytes 2621440
Async XLA Ops:
  2.8 1.3 %copy-start = (bf16[128,5120]{1,0:T(8,128)(2,1)S(1)}, bf16[128,5120]{1,0:T(8,128)(2,1)}, u32[]{:S(2)}) copy-start(bf16[128,5120]{1,0:T(8,128)(2,1)} %x_hbm.3) | copy-start | bytes 3932164
  4.1 2.2 %copy-start.2 = (bf16[128,64,2,128]{3,2,1,0:T(2,128)(2,1)S(1)}, bf16[128,64,2,128]{3,2,1,0:T(2,128)(2,1)}, u32[]{:S(2)}) copy-start(bf16[128,64,2,128]{3,2,1,0:T(2,128)(2,1)} %param.16) | copy-start | bytes 12582916
  6.3 0.8 copy-start.3
  7.1 0.8 copy-start.4
  7.8 0.7 copy-start.5
  8.5 0.7 copy-start.6
  9.2 0.7 copy-start.7
  9.8 45.1 %copy-start.1 = (bf16[128,5120]{1,0:T(8,128)(2,1)S(1)}, bf16[128,5120]{1,0:T(8,128)(2,1)}, u32[]{:S(2)}) copy-start(bf16[128,5120]{1,0:T(8,128)(2,1)} %x_hbm.3) | copy-start | bytes 3932164

commit v3 on v2

--- a/solution.py
+++ b/solution.py
@@ -303,21 +303,19 @@
     qkv = w_hbm.shape[2]
     tiles = qkv // LANES
     heads = tiles - 2
-    slots, _, depth2, _ = wbuf.shape
+    slots, depth2, _ = wbuf.shape
     chunks = d_model * kv // depth2
     blocks, _, seqs1 = p_ref.shape[0], p_ref.shape[1], p_ref.shape[2]
     seqs = seqs1 - 1
     ctx2 = k_hbm.shape[1]
     w_rows = w_hbm.reshape(d_model * kv, qkv)
 
-    def w_copy(chunk, slot, t):
+    def w_copy(chunk, slot):
         return pltpu.make_async_copy(
-            w_rows.at[pl.ds(pl.multiple_of(chunk * depth2, depth2), depth2), pl.ds(t * LANES, LANES)],
-            wbuf.at[slot, t], w_sem.at[slot])
+            w_rows.at[pl.ds(pl.multiple_of(chunk * depth2, depth2), depth2), :], wbuf.at[slot], w_sem.at[slot])
 
     def w_start(chunk, slot):
-        for t in range(tiles):
-            w_copy(chunk, slot, t).start()
+        w_copy(chunk, slot).start()
 
     small = [
         pltpu.make_async_copy(src, dst, in_sem.at[i])
@@ -368,13 +366,11 @@
                 cache_copy(k_hbm, kbuf, k_sem, block, False).start()
                 cache_copy(v_hbm, vbuf, v_sem, block, False).start()
 
-        for t in range(tiles):
-            w_copy(chunk, slot, t).wait()
+        w_copy(chunk, slot).wait()
         lhs = hexp.at[chunk]
         for t in range(0, tiles, 2):
-            rhs = jnp.concatenate([wbuf[slot, t], wbuf[slot, t + 1]], axis=1)
             cols = slice(t * LANES, (t + 2) * LANES)
-            acc[:, cols] += jnp.dot(lhs[...], rhs, preferred_element_type=jnp.float32)
+            acc[:, cols] += jnp.dot(lhs[...], wbuf[slot, :, cols], preferred_element_type=jnp.float32)
 
     for copy in small[2:]:
         copy.wait()
@@ -480,7 +476,7 @@
             pltpu.VMEM(b_qkv.shape, bf16),
             pltpu.SMEM(sinks.shape, f32),
             pltpu.VMEM((chunks, kv * num_seqs, depth2), bf16),
-            pltpu.VMEM((slots, tiles, depth2, LANES), bf16),
+            pltpu.VMEM((slots, depth2, qkv), bf16),
             pltpu.VMEM((kv * num_seqs, qkv), f32),
             pltpu.VMEM((num_seqs * kv * heads, LANES), f32),
             pltpu.VMEM((num_seqs * kv, LANES), f32),
@@ -492,7 +488,7 @@
         compiler_params=pltpu.CompilerParams(vmem_limit_bytes=44 * 2**20),
         cost_estimate=pl.CostEstimate(flops=4 * num_seqs * d_model * kv * qkv, bytes_accessed=50 * 2**20, transcendentals=0),
         name="front",
-    )(hidden, seq_lens, cos_t, sin_t, k_cache, v_cache, gain, w_qkv, b_qkv, sinks)
+    )(*(pltpu.with_memory_space_constraint(a, pltpu.HBM) for a in (hidden, seq_lens, cos_t, sin_t, k_cache, v_cache, gain, w_qkv, b_qkv, sinks)))
 
 
 def solution(mesh):

time: 97.7 us -> 92.2 us (0.944)
  local copies, waits for them, and re-layouts: 10.2 us -> 3.83 us
  Pallas kernels: 86.4 us -> 87.5 us
    unnamed x17 -> x3, local copies, waits for them, and re-layouts: 8.07 us -> 1.07 us
    pallas_call x1, Pallas kernels: 45.1 us -> 46.3 us  [front(): pl.pallas_call(functools.partial(front_kernel, LANES ** (-0.5)), out_shap...]
where the time goes in v3:
time: 92.2 us; the launch traced here: 92 us
  Pallas kernels  87.5 us (95%)
  local copies, waits for them, and re-layouts  3.83 us (4%)
    pallas_call x1, Pallas kernels, front(): pl.pallas_call(functools.partial(front_kernel, LANES ** (-0.5)), out_shap...  46.3 us
    pallas_call x1, Pallas kernels, combine(): pl.pallas_call(functools.partial(combine_kernel, seqs), out_shape=jax.Sha...  41.2 us

profile of v3, /device:TPU:97, one launch (start us, length us, event | category | flops | bytes accessed | tf_op | source)
XLA Modules:
  0.0 92.0 jit_solution(6045176891489216880)
XLA Ops:
  0.6 0.7 broadcast_in_dim.13.sink_ref
  1.4 1.3 %broadcast_in_dim.12.gain_hbm = bf16[1,5120]{1,0:T(2,128)(2,1)} reshape(bf16[5120]{0:T(1024)(128)(2,1)} %param.18) | data formatting | bytes 20480 | tf_op jit(solution)/shard_map/broadcast_in_dim | solution.py:502
  2.7 0.7 broadcast_in_dim.14.bo_ref
  3.4 0.0 copy-start
  3.4 46.3 %front.1 = (f32[8,2,17,8,128]{4,3,2,1,0:T(8,128)S(1)}, bf16[128,128,128]{2,1,0:T(8,128)(2,1)}, bf16[128,128,128]{2,1,0:T(8,128)(2,1)}) custom-call(bf16[128,5120]{1,0:T(8,128)(2,1)} %x_hbm.3, s32[128]{0:T(128)} %len_hbm.1, f32[64,128]{1,0:T(8,128)} %bitcast.10, f32[64,128]{1,0:T(8,128)} %bitcast.11, bf16[128,128,128]{2,1,0:T(8,128)(2,1)} %bitcast.8, ...), custom_call_target="tpu_custom_call" | custom-call | flops 6710886400 | bytes 52428800 | tf_op jit(solution)/shard_map/front/pallas_call | solution.py:465
  49.7 0.0 copy-done
  49.7 41.2 %combine.1 = bf16[128,5120]{1,0:T(8,128)(2,1)S(1)} custom-call(f32[4,2,2,17,8,128]{5,4,3,2,1,0:T(8,128)S(1)} %bitcast.7, f32[16,128]{1,0:T(8,128)S(1)} %broadcast_in_dim.13.sink_ref, bf16[128,5120]{1,0:T(8,128)(2,1)S(1)} %copy-done, bf16[1,5120]{1,0:T(2,128)(2,1)S(1)} %broadcast_in_dim.14.bo_ref, bf16[2048,5120]{1,0:T(8,128)(2,1)} %wo_hbm.1), custom_call_target="tpu_custom_call" | custom-call | flops 335544320 | bytes 31457280 | tf_op jit(solution)/shard_map/combine/pallas_call | solution.py:262
  90.9 1.1 %copy.16 = bf16[128,5120]{1,0:T(8,128)(2,1)} copy(bf16[128,5120]{1,0:T(8,128)(2,1)S(1)} %combine.1) | data formatting | bytes 2621440
Async XLA Ops:
  3.4 46.3 %copy-start = (bf16[128,5120]{1,0:T(8,128)(2,1)S(1)}, bf16[128,5120]{1,0:T(8,128)(2,1)}, u32[]{:S(2)}) copy-start(bf16[128,5120]{1,0:T(8,128)(2,1)} %x_hbm.3) | copy-start | bytes 3932164

commit v4 on v3

--- a/solution.py
+++ b/solution.py
@@ -295,27 +295,37 @@
 def front_kernel(
     logit_scale, x_hbm, len_hbm, cos_hbm, sin_hbm, k_hbm, v_hbm, gain_hbm, w_hbm, bias_hbm, sink_hbm,
     p_ref, k_out, v_out,
-    xbuf, lens, cos, sin, gain, bias, sinks, hexp, wbuf, acc, qs, kn, vn, kbuf, vbuf,
-    in_sem, w_sem, k_sem, v_sem, ko_sem, vo_sem,
+    xbuf, lens, cos, sin, gain, bias, sinks, hbuf, wide, narrow, wide_even, narrow_even, wide_odd, narrow_odd,
+    acc, qs, kn, vn, kbuf, vbuf,
+    in_sem, w_sem, n_sem, k_sem, v_sem, ko_sem, vo_sem,
 ):
     num_seqs, d_model = x_hbm.shape
     kv = w_hbm.shape[1]
-    qkv = w_hbm.shape[2]
-    tiles = qkv // LANES
+    tiles = w_hbm.shape[2] // LANES
     heads = tiles - 2
-    slots, depth2, _ = wbuf.shape
-    chunks = d_model * kv // depth2
-    blocks, _, seqs1 = p_ref.shape[0], p_ref.shape[1], p_ref.shape[2]
-    seqs = seqs1 - 1
+    slots, depth = wide.shape[:2]
+    quarter = depth // 4
+    chunks = d_model // depth
+    blocks, seqs = p_ref.shape[0], p_ref.shape[2] - 1
     ctx2 = k_hbm.shape[1]
-    w_rows = w_hbm.reshape(d_model * kv, qkv)
-
-    def w_copy(chunk, slot):
-        return pltpu.make_async_copy(
-            w_rows.at[pl.ds(pl.multiple_of(chunk * depth2, depth2), depth2), :], wbuf.at[slot], w_sem.at[slot])
+    split = heads * LANES
+
+    def w_copies(chunk, slot):
+        first = pl.multiple_of(chunk * depth, depth)
+        copies = [pltpu.make_async_copy(w_hbm.at[pl.ds(first, depth), :, pl.ds(0, split)], wide.at[slot], w_sem.at[slot])]
+        for j in range(4):
+            copies.append(pltpu.make_async_copy(
+                w_hbm.at[pl.ds(first + j * quarter, quarter), :, pl.ds(split, 2 * LANES)],
+                narrow.at[slot, :, :, pl.ds(j * 2 * LANES, 2 * LANES)], n_sem.at[slot]))
+        return copies
 
     def w_start(chunk, slot):
-        w_copy(chunk, slot).start()
+        for copy in w_copies(chunk, slot):
+            copy.start()
+
+    def w_wait(chunk, slot):
+        for copy in w_copies(chunk, slot):
+            copy.wait()
 
     small = [
         pltpu.make_async_copy(src, dst, in_sem.at[i])
@@ -324,7 +334,7 @@
     ]
     for copy in small:
         copy.start()
-    for slot in range(slots - 1):
+    for slot in range(slots):
         w_start(slot, slot)
 
     def cache_copy(hbm, buf, sem, block, out):
@@ -334,43 +344,72 @@
 
     small[0].wait()
     small[1].wait()
-    row = lax.broadcasted_iota(jnp.int32, (LANES, kv * LANES), 0)
-    col = lax.broadcasted_iota(jnp.int32, (LANES, kv * LANES), 1)
-    picks = [(col == row * kv + k).astype(jnp.bfloat16) for k in range(kv)]
     square = jnp.zeros((num_seqs, LANES), jnp.float32)
     for t in range(d_model // LANES):
         xt = xbuf[:, t * LANES : (t + 1) * LANES].astype(jnp.float32)
         square += xt * xt
     inv_rms = lax.rsqrt(jnp.sum(square, axis=-1, keepdims=True) / d_model + NORM_EPS)
-    per_chunk = depth2 // (kv * LANES)
     for t in range(d_model // LANES):
         xt = xbuf[:, t * LANES : (t + 1) * LANES].astype(jnp.float32)
         ht = (xt * inv_rms * gain[:, t * LANES : (t + 1) * LANES].astype(jnp.float32)).astype(jnp.bfloat16)
+        place = t * LANES % depth
+        hbuf[t * LANES // depth, :, place : place + LANES] = ht
+    acc[...] = jnp.zeros_like(acc)
+
+    def relayout(slot, wide_rows, narrow_rows):
+        for ref, rows, count in ((wide, wide_rows, depth), (narrow, narrow_rows, quarter)):
+            for i in range(count):
+                value = ref[slot, i].astype(jnp.float32)
+                for k in range(kv):
+                    rows[k, pl.ds(i, heads, stride=count + 1), :] = value[k : k + 1].reshape(heads, LANES)
+
+    def multiply(chunk, wide_rows, narrow_rows):
+        lhs = hbuf[chunk]
         for k in range(kv):
-            spread = jnp.dot(ht, picks[k], preferred_element_type=jnp.float32).astype(jnp.bfloat16)
-            place = t % per_chunk * kv * LANES
-            hexp[t // per_chunk, k * num_seqs : (k + 1) * num_seqs, place : place + kv * LANES] = spread
-    acc[...] = jnp.zeros_like(acc)
-
-    @pl.loop(0, chunks)
-    def _(chunk):
-        slot = lax.rem(chunk, slots)
-
-        @pl.when(chunk + slots - 1 < chunks)
+            for t in range(0, tiles, 2):
+                if t < heads:
+                    pair = [wide_rows[k, pl.ds((t + j) * (depth + 1), depth), :] for j in range(2)]
+                else:
+                    pair = [jnp.concatenate([
+                        narrow_rows[k, pl.ds((2 * i + j) * (quarter + 1), quarter), :] for i in range(4)], axis=0) for j in range(2)]
+                rhs = jnp.concatenate(pair, axis=1).astype(jnp.bfloat16)
+                cols = slice(t * LANES, (t + 2) * LANES)
+                acc[k, :, cols] += jnp.dot(lhs, rhs, preferred_element_type=jnp.float32)
+
+    w_wait(0, 0)
+    relayout(0, wide_even, narrow_even)
+
+    @pl.loop(0, chunks // 2)
+    def _(i):
+        even = 2 * i
+
+        @pl.when(even + slots < chunks)
         def _():
-            w_start(chunk + slots - 1, lax.rem(chunk + slots - 1, slots))
-
-        @pl.when(chunk == chunks - slots)
+            w_start(even + slots, lax.rem(even, slots))
+
+        odd = even + 1
+        w_wait(odd, lax.rem(odd, slots))
+        relayout(lax.rem(odd, slots), wide_odd, narrow_odd)
+        multiply(even, wide_even, narrow_even)
+
+        @pl.when(odd + slots < chunks)
+        def _():
+            w_start(odd + slots, lax.rem(odd, slots))
+
+        @pl.when(even + 2 + slots == chunks)
         def _():
             for block in range(blocks):
                 cache_copy(k_hbm, kbuf, k_sem, block, False).start()
                 cache_copy(v_hbm, vbuf, v_sem, block, False).start()
 
-        w_copy(chunk, slot).wait()
-        lhs = hexp.at[chunk]
-        for t in range(0, tiles, 2):
-            cols = slice(t * LANES, (t + 2) * LANES)
-            acc[:, cols] += jnp.dot(lhs[...], wbuf[slot, :, cols], preferred_element_type=jnp.float32)
+        later = lax.rem(even + 2, slots)
+
+        @pl.when(even + 2 < chunks)
+        def _():
+            w_wait(even + 2, later)
+
+        relayout(later, wide_even, narrow_even)
+        multiply(odd, wide_odd, narrow_odd)
 
     for copy in small[2:]:
         copy.wait()
@@ -386,9 +425,9 @@
     for k in range(kv):
         for t in range(tiles):
             cols = slice(t * LANES, (t + 1) * LANES)
-            value = acc[k * num_seqs : (k + 1) * num_seqs, cols] + bias[k : k + 1, cols].astype(jnp.float32)
+            value = acc[k, :, cols] + bias[k : k + 1, cols].astype(jnp.float32)
             if t < heads:
-                qs[pl.ds(k * heads + t, num_seqs, stride=kv * heads), :] = rotate(value)
+                qs[pl.ds(k * heads + t, num_seqs, stride=kv * heads + 1), :] = rotate(value)
             elif t == heads:
                 kn[pl.ds(k, num_seqs, stride=kv), :] = rotate(value)
             else:
@@ -428,7 +467,7 @@
                 buf[b, pl.ds(start, group), :] = value.astype(jnp.bfloat16)
         for i in range(seqs):
             b = block * seqs + i
-            q = qs[pl.ds(pl.multiple_of(b * q_rows, q_rows), q_rows), :].astype(jnp.bfloat16)
+            q = qs[pl.ds(b * (q_rows + 1), q_rows), :].astype(jnp.bfloat16)
             logits = lax.dot_general(q, kbuf[b], (((1,), (1,)), ((), ())), preferred_element_type=jnp.float32) * logit_scale
             logits = jnp.where(position <= lens[b], logits, -jnp.inf)
             top = jnp.maximum(jnp.max(logits, axis=-1, keepdims=True), sink_col)
@@ -455,9 +494,8 @@
     heads = tiles - 2
     seqs = num_seqs // (RING * SUBS)
     ctx2 = k_cache.shape[1]
-    depth2 = 1024
-    chunks = d_model * kv // depth2
-    slots = 4
+    depth, slots = 256, 6
+    quarter = depth // 4
     f32, bf16 = jnp.float32, jnp.bfloat16
     dma = pltpu.SemaphoreType.DMA
     hbm = pl.BlockSpec(memory_space=pl.ANY)
@@ -475,15 +513,20 @@
             pltpu.VMEM(gain.shape, bf16),
             pltpu.VMEM(b_qkv.shape, bf16),
             pltpu.SMEM(sinks.shape, f32),
-            pltpu.VMEM((chunks, kv * num_seqs, depth2), bf16),
-            pltpu.VMEM((slots, depth2, qkv), bf16),
-            pltpu.VMEM((kv * num_seqs, qkv), f32),
-            pltpu.VMEM((num_seqs * kv * heads, LANES), f32),
+            pltpu.VMEM((d_model // depth, num_seqs, depth), bf16),
+            pltpu.VMEM((slots, depth, kv, heads * LANES), bf16),
+            pltpu.VMEM((slots, quarter, kv, heads * LANES), bf16),
+            pltpu.VMEM((kv, heads * (depth + 1), LANES), f32),
+            pltpu.VMEM((kv, heads * (quarter + 1), LANES), f32),
+            pltpu.VMEM((kv, heads * (depth + 1), LANES), f32),
+            pltpu.VMEM((kv, heads * (quarter + 1), LANES), f32),
+            pltpu.VMEM((kv, num_seqs, qkv), f32),
+            pltpu.VMEM((num_seqs * (kv * heads + 1), LANES), f32),
             pltpu.VMEM((num_seqs * kv, LANES), f32),
             pltpu.VMEM((num_seqs * kv, LANES), f32),
             pltpu.VMEM(k_cache.shape, bf16),
             pltpu.VMEM(v_cache.shape, bf16),
-            dma((7,)), dma((slots,)), dma((RING * SUBS,)), dma((RING * SUBS,)), dma((RING * SUBS,)), dma((RING * SUBS,)),
+            dma((7,)), dma((slots,)), dma((slots,)), dma((RING * SUBS,)), dma((RING * SUBS,)), dma((RING * SUBS,)), dma((RING * SUBS,)),
         ],
         compiler_params=pltpu.CompilerParams(vmem_limit_bytes=44 * 2**20),
         cost_estimate=pl.CostEstimate(flops=4 * num_seqs * d_model * kv * qkv, bytes_accessed=50 * 2**20, transcendentals=0),

time: 92.2 us -> 94 us (1.020)
  Pallas kernels: 87.5 us -> 89.3 us
    pallas_call x1, Pallas kernels: 46.3 us -> 48.1 us  [front(): pl.pallas_call(functools.partial(front_kernel, LANES ** (-0.5)), out_shap...]
where the time goes in v4:
time: 94 us; the launch traced here: 93.8 us
  Pallas kernels  89.3 us (95%)
  local copies, waits for them, and re-layouts  3.83 us (4%)
    pallas_call x1, Pallas kernels, front(): pl.pallas_call(functools.partial(front_kernel, LANES ** (-0.5)), out_shap...  48.1 us
    pallas_call x1, Pallas kernels, combine(): pl.pallas_call(functools.partial(combine_kernel, seqs), out_shape=jax.Sha...  41.2 us

profile of v4, /device:TPU:97, one launch (start us, length us, event | category | flops | bytes accessed | tf_op | source)
XLA Modules:
  0.0 93.8 jit_solution(609149771317822454)
XLA Ops:
  0.6 0.7 broadcast_in_dim.13.sink_ref
  1.4 1.3 %broadcast_in_dim.12.gain_hbm = bf16[1,5120]{1,0:T(2,128)(2,1)} reshape(bf16[5120]{0:T(1024)(128)(2,1)} %param.18) | data formatting | bytes 20480 | tf_op jit(solution)/shard_map/broadcast_in_dim | solution.py:545
  2.7 0.7 broadcast_in_dim.14.bo_ref
  3.4 0.0 copy-start
  3.4 48.1 %front.1 = (f32[8,2,17,8,128]{4,3,2,1,0:T(8,128)S(1)}, bf16[128,128,128]{2,1,0:T(8,128)(2,1)}, bf16[128,128,128]{2,1,0:T(8,128)(2,1)}) custom-call(bf16[128,5120]{1,0:T(8,128)(2,1)} %x_hbm.3, s32[128]{0:T(128)} %len_hbm.1, f32[64,128]{1,0:T(8,128)} %bitcast.10, f32[64,128]{1,0:T(8,128)} %bitcast.11, bf16[128,128,128]{2,1,0:T(8,128)(2,1)} %bitcast.8, ...), custom_call_target="tpu_custom_call" | custom-call | flops 6710886400 | bytes 52428800 | tf_op jit(solution)/shard_map/front/pallas_call | solution.py:503
  51.5 0.0 copy-done
  51.5 41.2 %combine.1 = bf16[128,5120]{1,0:T(8,128)(2,1)S(1)} custom-call(f32[4,2,2,17,8,128]{5,4,3,2,1,0:T(8,128)S(1)} %bitcast.7, f32[16,128]{1,0:T(8,128)S(1)} %broadcast_in_dim.13.sink_ref, bf16[128,5120]{1,0:T(8,128)(2,1)S(1)} %copy-done, bf16[1,5120]{1,0:T(2,128)(2,1)S(1)} %broadcast_in_dim.14.bo_ref, bf16[2048,5120]{1,0:T(8,128)(2,1)} %wo_hbm.1), custom_call_target="tpu_custom_call" | custom-call | flops 335544320 | bytes 31457280 | tf_op jit(solution)/shard_map/combine/pallas_call | solution.py:262
  92.8 1.1 %copy.16 = bf16[128,5120]{1,0:T(8,128)(2,1)} copy(bf16[128,5120]{1,0:T(8,128)(2,1)S(1)} %combine.1) | data formatting | bytes 2621440
Async XLA Ops:
  3.4 48.1 %copy-start = (bf16[128,5120]{1,0:T(8,128)(2,1)S(1)}, bf16[128,5120]{1,0:T(8,128)(2,1)}, u32[]{:S(2)}) copy-start(bf16[128,5120]{1,0:T(8,128)(2,1)} %x_hbm.3) | copy-start | bytes 3932164

commit v5 on v3

--- a/solution.py
+++ b/solution.py
@@ -28,12 +28,21 @@
     return top, total, scales
 
 
+def weighted_sums(columns, parts, seqs):
+    loaded = [[part[i] for part in parts] for i in range(seqs)]
+    scaled = [[column * value for column, value in zip(cols, values)] for cols, values in zip(columns, loaded)]
+    return [functools.reduce(jnp.add, terms) for terms in scaled]
+
+
 def merge_into(dst, parts, seqs):
     top, total, scales = merge_parts(parts, seqs)
+    columns = [[lane_column(scale, i) for scale in scales] for i in range(seqs)]
+    sums = weighted_sums(columns, parts, seqs)
+    lane = lax.broadcasted_iota(jnp.int32, top.shape, 1)
+    stats = jnp.where(lane < HALF, top, total)
     for i in range(seqs):
-        dst[i] = sum(lane_column(scale, i) * part[i] for scale, part in zip(scales, parts))
-    lane = lax.broadcasted_iota(jnp.int32, top.shape, 1)
-    dst[seqs] = jnp.where(lane < HALF, top, total)
+        dst[i] = sums[i]
+    dst[seqs] = stats
 
 
 def combine_kernel(
@@ -116,10 +125,10 @@
         parts = (cb.at[3, s], rd.at[s], rm.at[s])
         top, total, scales = merge_parts(parts, seqs)
         inverse = 1.0 / (pltpu.roll(total, HALF, 1) + jnp.exp(sink - top))
+        columns = [[lane_column(scale * inverse, i) for scale in scales] for i in range(seqs)]
+        outs = [out.astype(jnp.bfloat16).astype(jnp.float32) for out in weighted_sums(columns, parts, seqs)]
         for i in range(seqs):
-            summed = sum(lane_column(scale, i) * part[i] for scale, part in zip(scales, parts))
-            head_out = summed * lane_column(inverse, i)
-            own_o[s, pl.ds(i * heads, heads), :] = head_out.astype(jnp.bfloat16).astype(jnp.float32)
+            own_o[s, pl.ds(i * heads, heads), :] = outs[i]
         send(own_o.at[s], other_o.at[s], o_send.at[s], o_recv.at[s], partner)
 
     def head_rows(ref):
@@ -388,7 +397,7 @@
             cols = slice(t * LANES, (t + 1) * LANES)
             value = acc[k * num_seqs : (k + 1) * num_seqs, cols] + bias[k : k + 1, cols].astype(jnp.float32)
             if t < heads:
-                qs[pl.ds(k * heads + t, num_seqs, stride=kv * heads), :] = rotate(value)
+                qs[pl.ds(k * heads + t, num_seqs, stride=kv * heads + 1), :] = rotate(value)
             elif t == heads:
                 kn[pl.ds(k, num_seqs, stride=kv), :] = rotate(value)
             else:
@@ -405,6 +414,7 @@
         sink = jnp.where(row == i, sinks[i], sink)
     sink_col = jnp.max(sink, axis=-1, keepdims=True)
     group = 16
+    wave = 16
     group_row = lax.broadcasted_iota(jnp.int32, (group, LANES), 0)
 
     @pl.loop(0, blocks)
@@ -412,32 +422,41 @@
         cache_copy(k_hbm, kbuf, k_sem, block, False).wait()
         cache_copy(v_hbm, vbuf, v_sem, block, False).wait()
         stats = jnp.zeros((q_rows, LANES), jnp.float32)
+        updates = []
         for i in range(seqs):
             b = block * seqs + i
-            n = lens[b]
-            local = n - base
+            local = lens[b] - base
             here = jnp.logical_and(local >= 0, local < ctx2 // kv)
             place = jnp.where(here, local * kv, 0)
             start = pl.multiple_of(place // group * group, group)
             target = jnp.where(here, place - start, group)
             for buf, new in ((kbuf, kn), (vbuf, vn)):
-                fresh = new[pl.ds(b * kv, kv), :]
-                value = buf[b, pl.ds(start, group), :].astype(jnp.float32)
+                updates.append((buf, b, start, target, new[pl.ds(b * kv, kv), :], buf[b, pl.ds(start, group), :]))
+        fresh_groups = []
+        for _, _, _, target, fresh, old in updates:
+            value = old.astype(jnp.float32)
+            for k in range(kv):
+                value = jnp.where(group_row == target + k, fresh[k : k + 1], value)
+            fresh_groups.append(value.astype(jnp.bfloat16))
+        for (buf, b, start, _, _, _), value in zip(updates, fresh_groups):
+            buf[b, pl.ds(start, group), :] = value
+        for first in range(0, seqs, wave):
+            members = range(first, first + wave)
+            queries = [qs[pl.ds((block * seqs + i) * (q_rows + 1), q_rows), :].astype(jnp.bfloat16) for i in members]
+            logits = [
+                lax.dot_general(q, kbuf[block * seqs + i], (((1,), (1,)), ((), ())), preferred_element_type=jnp.float32)
+                for i, q in zip(members, queries)]
+            logits = [jnp.where(position <= lens[block * seqs + i], l * logit_scale, -jnp.inf) for i, l in zip(members, logits)]
+            tops = [jnp.maximum(jnp.max(l, axis=-1, keepdims=True), sink_col) for l in logits]
+            weights = [jnp.exp(l - top) for l, top in zip(logits, tops)]
+            totals = [jnp.sum(w, axis=-1, keepdims=True) for w in weights]
+            numers = [
+                jnp.dot(w.astype(jnp.bfloat16), vbuf[block * seqs + i], preferred_element_type=jnp.float32)
+                for i, w in zip(members, weights)]
+            for i, numer, top, total in zip(members, numers, tops, totals):
                 for k in range(kv):
-                    value = jnp.where(group_row == target + k, fresh[k : k + 1], value)
-                buf[b, pl.ds(start, group), :] = value.astype(jnp.bfloat16)
-        for i in range(seqs):
-            b = block * seqs + i
-            q = qs[pl.ds(pl.multiple_of(b * q_rows, q_rows), q_rows), :].astype(jnp.bfloat16)
-            logits = lax.dot_general(q, kbuf[b], (((1,), (1,)), ((), ())), preferred_element_type=jnp.float32) * logit_scale
-            logits = jnp.where(position <= lens[b], logits, -jnp.inf)
-            top = jnp.maximum(jnp.max(logits, axis=-1, keepdims=True), sink_col)
-            weights = jnp.exp(logits - top)
-            total = jnp.sum(weights, axis=-1, keepdims=True)
-            numer = jnp.dot(weights.astype(jnp.bfloat16), vbuf[b], preferred_element_type=jnp.float32)
-            for k in range(kv):
-                p_ref[block, k, i] = numer[k * heads : (k + 1) * heads]
-            stats = jnp.where(lane == i, top, jnp.where(lane == HALF + i, total, stats))
+                    p_ref[block, k, i] = numer[k * heads : (k + 1) * heads]
+                stats = jnp.where(lane == i, top, jnp.where(lane == HALF + i, total, stats))
         for k in range(kv):
             p_ref[block, k, seqs] = stats[k * heads : (k + 1) * heads]
         cache_copy(k_out, kbuf, ko_sem, block, True).start()
@@ -478,7 +497,7 @@
             pltpu.VMEM((chunks, kv * num_seqs, depth2), bf16),
             pltpu.VMEM((slots, depth2, qkv), bf16),
             pltpu.VMEM((kv * num_seqs, qkv), f32),
-            pltpu.VMEM((num_seqs * kv * heads, LANES), f32),
+            pltpu.VMEM((num_seqs * (kv * heads + 1), LANES), f32),
             pltpu.VMEM((num_seqs * kv, LANES), f32),
             pltpu.VMEM((num_seqs * kv, LANES), f32),
             pltpu.VMEM(k_cache.shape, bf16),

time: 92.2 us -> 65.8 us (0.71)
  Pallas kernels: 87.5 us -> 61.1 us
    pallas_call x1, Pallas kernels: 46.3 us -> 19.8 us  [front(): pl.pallas_call(functools.partial(front_kernel, LANES ** (-0.5)), out_shap...]
where the time goes in v5:
time: 65.8 us; the launch traced here: 65.6 us
  Pallas kernels  61.1 us (93%)
  local copies, waits for them, and re-layouts  3.83 us (6%)
  between operations  0.67 us (1%)
    pallas_call x1, Pallas kernels, combine(): pl.pallas_call(functools.partial(combine_kernel, seqs), out_shape=jax.Sha...  41.3 us
    pallas_call x1, Pallas kernels, front(): pl.pallas_call(functools.partial(front_kernel, LANES ** (-0.5)), out_shap...  19.8 us
    broadcast_in_dim x1, local copies, waits for them, and re-layouts, block_step(): norm_gain[None, :]  1.32 us

profile of v5, /device:TPU:97, one launch (start us, length us, event | category | flops | bytes accessed | tf_op | source)
XLA Modules:
  0.0 65.6 jit_solution(14002170093527099756)
XLA Ops:
  0.6 0.7 %broadcast_in_dim.13.sink_ref = f32[16,128]{1,0:T(8,128)S(1)} broadcast(f32[16]{0:T(128)} %sink_hbm.1), dimensions={0} | broadcast | bytes 8256 | tf_op jit(solution)/shard_map/broadcast_in_dim | solution.py:523
  1.4 1.3 %broadcast_in_dim.12.gain_hbm = bf16[1,5120]{1,0:T(2,128)(2,1)} reshape(bf16[5120]{0:T(1024)(128)(2,1)} %param.18) | data formatting | bytes 20480 | tf_op jit(solution)/shard_map/broadcast_in_dim | solution.py:521
  2.7 0.7 %broadcast_in_dim.14.bo_ref = bf16[1,5120]{1,0:T(2,128)(2,1)S(1)} reshape(bf16[5120]{0:T(1024)(128)(2,1)} %param.23) | data formatting | bytes 20480 | tf_op jit(solution)/shard_map/broadcast_in_dim | solution.py:524
  3.4 0.0 copy-start
  3.4 19.8 %front.1 = (f32[8,2,17,8,128]{4,3,2,1,0:T(8,128)S(1)}, bf16[128,128,128]{2,1,0:T(8,128)(2,1)}, bf16[128,128,128]{2,1,0:T(8,128)(2,1)}) custom-call(bf16[128,5120]{1,0:T(8,128)(2,1)} %x_hbm.3, s32[128]{0:T(128)} %len_hbm.1, f32[64,128]{1,0:T(8,128)} %bitcast.10, f32[64,128]{1,0:T(8,128)} %bitcast.11, bf16[128,128,128]{2,1,0:T(8,128)(2,1)} %bitcast.8, ...), custom_call_target="tpu_custom_call" | custom-call | flops 6710886400 | bytes 52428800 | tf_op jit(solution)/shard_map/front/pallas_call | solution.py:484
  23.2 0.0 copy-done
  23.2 41.3 %combine.1 = bf16[128,5120]{1,0:T(8,128)(2,1)S(1)} custom-call(f32[4,2,2,17,8,128]{5,4,3,2,1,0:T(8,128)S(1)} %bitcast.7, f32[16,128]{1,0:T(8,128)S(1)} %broadcast_in_dim.13.sink_ref, bf16[128,5120]{1,0:T(8,128)(2,1)S(1)} %copy-done, bf16[1,5120]{1,0:T(2,128)(2,1)S(1)} %broadcast_in_dim.14.bo_ref, bf16[2048,5120]{1,0:T(8,128)(2,1)} %wo_hbm.1), custom_call_target="tpu_custom_call" | custom-call | flops 335544320 | bytes 31457280 | tf_op jit(solution)/shard_map/combine/pallas_call | solution.py:271
  64.5 1.1 %copy.16 = bf16[128,5120]{1,0:T(8,128)(2,1)} copy(bf16[128,5120]{1,0:T(8,128)(2,1)S(1)} %combine.1) | data formatting | bytes 2621440
Async XLA Ops:
  3.4 19.8 %copy-start = (bf16[128,5120]{1,0:T(8,128)(2,1)S(1)}, bf16[128,5120]{1,0:T(8,128)(2,1)}, u32[]{:S(2)}) copy-start(bf16[128,5120]{1,0:T(8,128)(2,1)} %x_hbm.3) | copy-start | bytes 3932164

commit v6 on v5

v6 whole, which is shorter than its diff:
```python
import functools

import jax
import jax.numpy as jnp
from jax import lax
from jax.experimental import pallas as pl
from jax.experimental.pallas import tpu as pltpu
from jax.sharding import PartitionSpec as P

NORM_EPS = 1e-5
MESH = pl.DeviceIdType.MESH
LANES = 128
HALF = LANES // 2
SUBS = 2
CORES = 2
FRONT_MIB = 34
COMBINE_MIB = 26
WAVE = 4
RING = 4


def lane_column(tile, index):
    return tile[:, index : index + 1]


def merge_parts(parts, seqs):
    stats = [part[seqs] for part in parts]
    top = functools.reduce(jnp.maximum, stats)
    scales = [jnp.exp(stat - top) for stat in stats]
    total = sum(pltpu.roll(scale, HALF, 1) * stat for scale, stat in zip(scales, stats))
    return top, total, scales


def weighted_sums(columns, parts, seqs):
    loaded = [[part[i] for part in parts] for i in range(seqs)]
    scaled = [[column * value for column, value in zip(cols, values)] for cols, values in zip(columns, loaded)]
    return [functools.reduce(jnp.add, terms) for terms in scaled]


def merge_into(dst, parts, seqs):
    top, total, scales = merge_parts(parts, seqs)
    columns = [[lane_column(scale, i) for scale in scales] for i in range(seqs)]
    sums = weighted_sums(columns, parts, seqs)
    lane = lax.broadcasted_iota(jnp.int32, top.shape, 1)
    stats = jnp.where(lane < HALF, top, total)
    for i in range(seqs):
        dst[i] = sums[i]
    dst[seqs] = stats


def combine_kernel(
    seqs, logit_scale, q_ref, k_ref, v_ref, lens, sink_ref, x_hbm, bo_hbm, wo_hbm, out_ref,
    p_ref, bo_ref, bias_rows, ra, cb, rl, rm, rd, own_o, other_o, wbuf, xbuf, z, yrl, ym, yrm, yrd, g, gp,
    w_sem, x_sem, a_send, a_recv, b_send, rl_recv, rm_recv, rd_recv, o_send, o_recv,
    d_send, yrl_recv, yrm_recv, yrd_recv, g_send, g_recv, gp_send, gp_recv,
):
    y = lax.axis_index("tp")
    sp = lax.axis_index("sp")
    x = sp // CORES
    c = sp % CORES
    step = 1 - 2 * c
    xn, xp, xo = (x + step + RING) % RING, (x - step + RING) % RING, (x + 2) % RING
    yn, yp, yo = (y + step + RING) % RING, (y - step + RING) % RING, (y + 2) % RING
    partner = {"sp": x * CORES + 1 - c}
    to_xn, to_xp = {"sp": xn * CORES + c}, {"sp": xp * CORES + c}
    to_yn, to_yp = {"tp": yn}, {"tp": yp}

    rows_half = wo_hbm.shape[0] // 2
    cols_core = wo_hbm.shape[1] // CORES
    cols_sub = cols_core // SUBS
    heads = p_ref.shape[4]
    block_rows = z.shape[2]

    w_copies = []
    for k in range(2):
        rows = (c if k == 0 else 1 - c) * rows_half
        copy = pltpu.make_async_copy(
            wo_hbm.at[pl.ds(pl.multiple_of(rows, LANES), rows_half), pl.ds(pl.multiple_of(c * cols_core, LANES), cols_core)],
            wbuf.at[k], w_sem.at[k])
        copy.start()
        w_copies.append(copy)
    row0 = pl.multiple_of((x * RING + y) * block_rows, block_rows)
    x_copy = pltpu.make_async_copy(
        x_hbm.at[pl.ds(row0, block_rows), pl.ds(pl.multiple_of(c * cols_core, LANES), cols_core)], xbuf, x_sem.at[0])
    x_copy.start()
    bo_copy = pltpu.make_async_copy(bo_hbm, bo_ref, x_sem.at[1])
    bo_copy.start()

    barrier = pltpu.get_barrier_semaphore()
    for where in (partner, to_xn, to_xp, to_yn, to_yp):
        pl.semaphore_signal(barrier, inc=1, device_id=where, device_id_type=MESH)
    pl.semaphore_wait(barrier, 5)

    def send(src, dst, send_sem, recv_sem, where):
        copy = pltpu.make_async_remote_copy(
            src_ref=src, dst_ref=dst, send_sem=send_sem, recv_sem=recv_sem, device_id=where, device_id_type=MESH)
        copy.start()

    def sent(shape_of, send_sem):
        pltpu.make_async_remote_copy(
            src_ref=shape_of, dst_ref=shape_of, send_sem=send_sem, recv_sem=send_sem, device_id=partner, device_id_type=MESH).wait_send()

    def arrived(dst, recv_sem):
        pltpu.make_async_remote_copy(
            src_ref=dst, dst_ref=dst, send_sem=recv_sem, recv_sem=recv_sem, device_id=partner, device_id_type=MESH).wait_recv()

    kv = p_ref.shape[2]
    q_rows = kv * heads
    ctx2 = k_ref.shape[1]
    row = lax.broadcasted_iota(jnp.int32, (q_rows, ctx2), 0)
    lane = lax.broadcasted_iota(jnp.int32, (q_rows, ctx2), 1)
    position = jnp.where(lane % kv == row // heads, lane // kv + sp * (ctx2 // kv), jnp.iinfo(jnp.int32).max)
    sinks = jnp.zeros((q_rows, LANES), jnp.float32)
    for i in range(q_rows):
        sinks = jnp.where(row == i, sink_ref[i], sinks)
    sink_col = jnp.max(sinks, axis=-1, keepdims=True)

    def attend(b, s):
        first = (b * SUBS + s) * seqs
        waves = [range(j, j + WAVE) for j in range(0, seqs, WAVE)]
        logits, tops, totals, weights, stats = {}, {}, {}, {}, jnp.zeros((q_rows, LANES), jnp.float32)
        for turn in range(len(waves) + 2):
            if turn < len(waves):
                for i in waves[turn]:
                    q = q_ref[pl.ds((first + i) * (q_rows + 1), q_rows), :].astype(jnp.bfloat16)
                    logits[i] = lax.dot_general(q, k_ref[first + i], (((1,), (1,)), ((), ())), preferred_element_type=jnp.float32)
            if 0 <= turn - 1 < len(waves):
                members = waves[turn - 1]
                for i in members:
                    logits[i] = jnp.where(position <= lens[first + i], logits[i] * logit_scale, -jnp.inf)
                for i in members:
                    tops[i] = jnp.maximum(jnp.max(logits[i], axis=-1, keepdims=True), sink_col)
                for i in members:
                    weights[i] = jnp.exp(logits[i] - tops[i])
                for i in members:
                    totals[i] = jnp.sum(weights[i], axis=-1, keepdims=True)
            if 0 <= turn - 2:
                members = waves[turn - 2]
                numers = [
                    jnp.dot(weights[i].astype(jnp.bfloat16), v_ref[first + i], preferred_element_type=jnp.float32) for i in members]
                for i, numer in zip(members, numers):
                    for k in range(kv):
                        p_ref[b, s, k, i] = numer[k * heads : (k + 1) * heads]
                    stats = jnp.where(lane == i, tops[i], jnp.where(lane == HALF + i, totals[i], stats))
        for k in range(kv):
            p_ref[b, s, k, seqs] = stats[k * heads : (k + 1) * heads]
        send(p_ref.at[b, s, 1 - c], ra.at[b, s], a_send.at[0], a_recv.at[b, s], partner)

    def attend_both(b):
        @pl.loop(0, SUBS)
        def _(s):
            attend(b, s)

    def relay(s):
        arrived(ra.at[xo, s], a_recv.at[xo, s])
        merge_into(cb.at[0, s], (p_ref.at[xo, s, c], ra.at[xo, s]), seqs)
        send(cb.at[0, s], rl.at[s], b_send.at[0], rl_recv.at[s], to_xn)

    def pass_on(s):
        arrived(ra.at[xn, s], a_recv.at[xn, s])
        arrived(rl.at[s], rl_recv.at[s])
        merge_into(cb.at[2, s], (p_ref.at[xn, s, c], ra.at[xn, s], rl.at[s]), seqs)
        send(cb.at[2, s], rm.at[s], b_send.at[0], rm_recv.at[s], to_xn)

    attend_both(xo)
    for s in range(SUBS):
        attend(xn, s)
        relay(s)
    attend_both(xp)
    for s in range(SUBS):
        arrived(ra.at[xp, s], a_recv.at[xp, s])
        merge_into(cb.at[1, s], (p_ref.at[xp, s, c], ra.at[xp, s]), seqs)
        send(cb.at[1, s], rd.at[s], b_send.at[0], rd_recv.at[s], to_xp)
    for s in range(SUBS):
        attend(x, s)
        pass_on(s)
    for s in range(SUBS):
        arrived(ra.at[x, s], a_recv.at[x, s])
        merge_into(cb.at[3, s], (p_ref.at[x, s, c], ra.at[x, s]), seqs)
    sink = jnp.zeros((heads, LANES), jnp.float32)
    head_row = lax.broadcasted_iota(jnp.int32, sink.shape, 0)
    for h in range(heads):
        sink = jnp.where(head_row == h, sink_ref[c * heads + h], sink)
    for s in range(SUBS):
        arrived(rd.at[s], rd_recv.at[s])
        arrived(rm.at[s], rm_recv.at[s])
        parts = (cb.at[3, s], rd.at[s], rm.at[s])
        top, total, scales = merge_parts(parts, seqs)
        inverse = 1.0 / (pltpu.roll(total, HALF, 1) + jnp.exp(sink - top))
        columns = [[lane_column(scale * inverse, i) for scale in scales] for i in range(seqs)]
        outs = [out.astype(jnp.bfloat16).astype(jnp.float32) for out in weighted_sums(columns, parts, seqs)]
        for i in range(seqs):
            own_o[s, pl.ds(i * heads, heads), :] = outs[i]
        send(own_o.at[s], other_o.at[s], o_send.at[0], o_recv.at[s], partner)

    def head_rows(ref):
        columns = []
        for h in range(heads):
            columns.append(jnp.concatenate(
                [ref[s, pl.ds(h, seqs, stride=heads), :] for s in range(SUBS)], axis=0).astype(jnp.bfloat16))
        return jnp.concatenate(columns, axis=1)

    own_rows = head_rows(own_o)
    w_copies[0].wait()
    for q in range(SUBS):
        part = jnp.dot(own_rows, wbuf[0, :, pl.ds(q * cols_sub, cols_sub)], preferred_element_type=jnp.float32)
        for r in range(RING):
            z[q, r] = part[r * block_rows : (r + 1) * block_rows]
    for s in range(SUBS):
        arrived(other_o.at[s], o_recv.at[s])
    other_rows = head_rows(other_o)
    w_copies[1].wait()
    for q in range(SUBS):
        part = jnp.dot(other_rows, wbuf[1, :, pl.ds(q * cols_sub, cols_sub)], preferred_element_type=jnp.float32)
        for r in range(RING):
            z[q, r] += part[r * block_rows : (r + 1) * block_rows]
        send(z.at[q, yo], yrl.at[q], d_send.at[0], yrl_recv.at[q], to_yn)
        send(z.at[q, yp], yrd.at[q], d_send.at[0], yrd_recv.at[q], to_yp)
    for q in range(SUBS):
        arrived(yrl.at[q], yrl_recv.at[q])
        ym[q] = z[q, yn] + yrl[q]
        send(ym.at[q], yrm.at[q], d_send.at[0], yrm_recv.at[q], to_yn)
    chunk = g.shape[3:]
    sent(ra, a_send.at[0])
    sent(cb.at[pl.ds(0, 3)], b_send.at[0])
    sent(own_o, o_send.at[0])
    sent(g.reshape((-1,) + chunk).at[pl.ds(0, 3 * SUBS)], d_send.at[0])
    x_copy.wait()
    bo_copy.wait()
    bias_rows[...] = bo_ref[...].astype(jnp.float32)

    def store(q, xx, yy, core, value):
        rows = pl.ds(pl.multiple_of((xx * RING + yy) * block_rows, block_rows), block_rows)
        cols = pl.ds(pl.multiple_of(core * cols_core + q * cols_sub, LANES), cols_sub)
        out_ref[rows, cols] = value.astype(jnp.bfloat16)

    def slot(q, first, second):
        return (first, second) if q == 0 else (second, first)

    ahead = ((to_xn, to_xp), (to_yn, to_yp))
    first_now, first_n, first_p, first_o = (x, y), (xn, yn), (xp, yp), (xo, yo)

    pushes = []

    def push(q, first, second, where):
        xx, yy = slot(q, first, second)
        pushes.append(q)
        send(g.at[q, xx, yy], g.at[q, xx, yy], g_send.at[0], g_recv.at[q, xx, yy], where)

    def share(q, first, second):
        xx, yy = slot(q, first, second)
        send(g.at[q, xx, yy], gp.at[q, xx, yy], gp_send.at[0], gp_recv.at[q, xx, yy], partner)

    def receive(q, first, second):
        xx, yy = slot(q, first, second)
        arrived(g.at[q, xx, yy], g_recv.at[q, xx, yy])

    def keep(q, first, second):
        xx, yy = slot(q, first, second)
        store(q, xx, yy, c, g[q, xx, yy])

    for q in range(SUBS):
        arrived(yrd.at[q], yrd_recv.at[q])
        arrived(yrm.at[q], yrm_recv.at[q])
        first_row = (c * cols_core + q * cols_sub) // LANES
        bias = jnp.concatenate([bias_rows[pl.ds(first_row + t, 1), :] for t in range(cols_sub // LANES)], axis=1)
        summed = z[q, y] + yrd[q] + yrm[q]
        final = xbuf[:, pl.ds(q * cols_sub, cols_sub)].astype(jnp.float32) + summed + bias
        g[q, x, y] = final.astype(jnp.bfloat16).astype(jnp.float32)
        for axis in (q, 1 - q):
            for kind in range(2):
                push(q, first_now[q], first_now[1 - q], ahead[axis][kind])
        share(q, first_now[q], first_now[1 - q])

    def spread(q, first, forward):
        other = 1 - q
        receive(q, first, first_now[other])
        if forward:
            push(q, first, first_now[other], ahead[q][0])
        for kind in range(2):
            push(q, first, first_now[other], ahead[other][kind])
        share(q, first, first_now[other])
        keep(q, first, first_now[other])

    def settle(q, first, second, forward):
        receive(q, first, second)
        if forward:
            push(q, first, second, ahead[1 - q][0])
        share(q, first, second)
        keep(q, first, second)

    both = range(SUBS)
    for q in both:
        spread(q, first_p[q], True)
    for q in both:
        spread(q, first_n[q], False)
    for q in both:
        keep(q, first_now[q], first_now[1 - q])
    for q in both:
        settle(q, first_now[q], first_p[1 - q], True)
    for q in both:
        settle(q, first_now[q], first_n[1 - q], False)
    for q in both:
        spread(q, first_o[q], False)
    for first in (first_p, first_n):
        for q in both:
            settle(q, first[q], first_p[1 - q], True)
        for q in both:
            settle(q, first[q], first_n[1 - q], False)
    for q in both:
        settle(q, first_now[q], first_o[1 - q], False)
    for q in both:
        settle(q, first_o[q], first_p[1 - q], True)
    for q in both:
        settle(q, first_o[q], first_n[1 - q], False)
    for first in (first_p, first_n, first_o):
        for q in both:
            settle(q, first[q], first_o[1 - q], False)
    orders = [first_now, first_p, first_n, first_o]
    for xi in range(RING):
        for yi in range(RING):
            for q in both:
                xx, yy = slot(q, orders[xi][q], orders[yi][1 - q])
                arrived(gp.at[q, xx, yy], gp_recv.at[q, xx, yy])
                store(q, xx, yy, 1 - c, gp[q, xx, yy])
    sent(g.reshape((-1,) + chunk).at[pl.ds(0, len(pushes))], g_send.at[0])
    sent(gp, gp_send.at[0])


def combine(queries, k_out, v_out, seq_lens, sinks, hidden, b_o, w_o):
    num_seqs, d_model = hidden.shape
    seqs = num_seqs // (RING * SUBS)
    kv = CORES
    heads = sinks.shape[0] // kv
    cols_core = d_model // CORES
    cols_sub = cols_core // SUBS
    block_rows = num_seqs // (RING * RING)
    part = (seqs + 1, heads, LANES)
    f32, bf16 = jnp.float32, jnp.bfloat16
    dma = pltpu.SemaphoreType.DMA
    vmem = pl.BlockSpec(memory_space=pltpu.VMEM)
    hbm = pl.BlockSpec(memory_space=pl.ANY)
    smem = pl.BlockSpec(memory_space=pltpu.SMEM)
    chunk = (block_rows, cols_sub)
    return pl.pallas_call(
        functools.partial(combine_kernel, seqs, LANES ** -0.5),
        out_shape=jax.ShapeDtypeStruct((num_seqs, d_model), bf16),
        in_specs=[vmem, vmem, vmem, smem, smem, hbm, hbm, hbm],
        out_specs=vmem,
        scratch_shapes=[
            pltpu.VMEM((RING, SUBS, kv) + part, f32),
            pltpu.VMEM(b_o.shape, bf16),
            pltpu.VMEM(b_o.shape, f32),
            pltpu.VMEM((RING, SUBS) + part, f32),
            pltpu.VMEM((RING, SUBS) + part, f32),
            pltpu.VMEM((SUBS,) + part, f32),
            pltpu.VMEM((SUBS,) + part, f32),
            pltpu.VMEM((SUBS,) + part, f32),
            pltpu.VMEM((SUBS, seqs * heads, LANES), f32),
            pltpu.VMEM((SUBS, seqs * heads, LANES), f32),
            pltpu.VMEM((2, w_o.shape[0] // 2, cols_core), bf16),
            pltpu.VMEM((block_rows, cols_core), bf16),
            pltpu.VMEM((SUBS, RING) + chunk, f32),
            pltpu.VMEM((SUBS,) + chunk, f32),
            pltpu.VMEM((SUBS,) + chunk, f32),
            pltpu.VMEM((SUBS,) + chunk, f32),
            pltpu.VMEM((SUBS,) + chunk, f32),
            pltpu.VMEM((SUBS, RING, RING) + chunk, f32),
            pltpu.VMEM((SUBS, RING, RING) + chunk, f32),
            dma((2,)), dma((2,)), dma((1,)), dma((RING, SUBS)), dma((1,)),
            dma((SUBS,)), dma((SUBS,)), dma((SUBS,)), dma((1,)), dma((SUBS,)),
            dma((1,)), dma((SUBS,)), dma((SUBS,)), dma((SUBS,)),
            dma((1,)), dma((SUBS, RING, RING)), dma((1,)), dma((SUBS, RING, RING)),
        ],
        compiler_params=pltpu.CompilerParams(collective_id=0, has_side_effects=True, vmem_limit_bytes=COMBINE_MIB * 2**20),
        cost_estimate=pl.CostEstimate(flops=2 * num_seqs // RING * w_o.shape[0] * cols_core, bytes_accessed=30 * 2**20, transcendentals=0),
        name="combine",
    )(queries, k_out, v_out, seq_lens, sinks, *(pltpu.with_memory_space_constraint(a, pltpu.HBM) for a in (hidden, b_o, w_o)))


def front_kernel(
    x_hbm, len_hbm, cos_hbm, sin_hbm, k_hbm, v_hbm, gain_hbm, w_hbm, bias_hbm,
    qs, kbuf, vbuf, k_out, v_out,
    xbuf, lens, cos, sin, gain, bias, hexp, wbuf, acc, kn, vn,
    in_sem, w_sem, k_sem, v_sem, ko_sem, vo_sem,
):
    num_seqs, d_model = x_hbm.shape
    kv = w_hbm.shape[1]
    qkv = w_hbm.shape[2]
    tiles = qkv // LANES
    heads = tiles - 2
    slots, depth2, _ = wbuf.shape
    chunks = d_model * kv // depth2
    blocks = k_sem.shape[0]
    seqs = num_seqs // blocks
    ctx2 = k_hbm.shape[1]
    w_rows = w_hbm.reshape(d_model * kv, qkv)

    def w_copy(chunk, slot):
        return pltpu.make_async_copy(
            w_rows.at[pl.ds(pl.multiple_of(chunk * depth2, depth2), depth2), :], wbuf.at[slot], w_sem.at[slot])

    def w_start(chunk, slot):
        w_copy(chunk, slot).start()

    small = [
        pltpu.make_async_copy(src, dst, in_sem.at[i])
        for i, (src, dst) in enumerate((
            (x_hbm, xbuf), (gain_hbm, gain), (len_hbm, lens), (cos_hbm, cos), (sin_hbm, sin), (bias_hbm, bias)))
    ]
    for copy in small:
        copy.start()
    for slot in range(slots - 1):
        w_start(slot, slot)

    def cache_copy(hbm, buf, sem, block):
        rows = pl.ds(block * seqs, seqs)
        return pltpu.make_async_copy(hbm.at[rows], buf.at[rows], sem.at[block])

    def cache_write(hbm, buf, sem, block):
        rows = pl.ds(block * seqs, seqs)
        return pltpu.make_async_copy(buf.at[rows], hbm.at[rows], sem.at[block])

    small[0].wait()
    small[1].wait()
    row = lax.broadcasted_iota(jnp.int32, (LANES, kv * LANES), 0)
    col = lax.broadcasted_iota(jnp.int32, (LANES, kv * LANES), 1)
    pick = (col == row * kv).astype(jnp.bfloat16)
    gains = gain[...].astype(jnp.float32)
    square = jnp.zeros((num_seqs, LANES), jnp.float32)
    for t in range(d_model // LANES):
        xt = xbuf[:, t * LANES : (t + 1) * LANES].astype(jnp.float32)
        square += xt * xt
    inv_rms = lax.rsqrt(jnp.sum(square, axis=-1, keepdims=True) / d_model + NORM_EPS)
    per_chunk = depth2 // (kv * LANES)
    for t in range(d_model // LANES):
        xt = xbuf[:, t * LANES : (t + 1) * LANES].astype(jnp.float32)
        ht = (xt * inv_rms * gains[t : t + 1]).astype(jnp.bfloat16)
        spread = jnp.dot(ht, pick, preferred_element_type=jnp.float32).astype(jnp.bfloat16)
        for k in range(kv):
            for j in range(kv):
                piece = spread[:, j * LANES : (j + 1) * LANES]
                place = t % per_chunk * kv * LANES + j * LANES
                hexp[t // per_chunk, k * num_seqs : (k + 1) * num_seqs, place : place + LANES] = pltpu.roll(piece, k, 1) if k else piece
    acc[...] = jnp.zeros_like(acc)

    @pl.loop(0, chunks)
    def _(chunk):
        slot = lax.rem(chunk, slots)

        @pl.when(chunk + slots - 1 < chunks)
        def _():
            w_start(chunk + slots - 1, lax.rem(chunk + slots - 1, slots))

        @pl.when(chunk == chunks - slots)
        def _():
            for block in range(blocks):
                cache_copy(k_hbm, kbuf, k_sem, block).start()
                cache_copy(v_hbm, vbuf, v_sem, block).start()

        w_copy(chunk, slot).wait()
        lhs = hexp.at[chunk]
        for t in range(0, tiles, 2):
            cols = slice(t * LANES, (t + 2) * LANES)
            acc[:, cols] += jnp.dot(lhs[...], wbuf[slot, :, cols], preferred_element_type=jnp.float32)

    for copy in small[2:]:
        copy.wait()
    cos_t = jnp.transpose(jnp.concatenate([cos[...], cos[...]], axis=0))
    sin_t = jnp.transpose(jnp.concatenate([-sin[...], sin[...]], axis=0))

    def rotate(t):
        return t * cos_t + pltpu.roll(t, HALF, 1) * sin_t

    def rounded(t):
        return t.astype(jnp.bfloat16).astype(jnp.float32)

    for k in range(kv):
        for t in range(tiles):
            cols = slice(t * LANES, (t + 1) * LANES)
            value = acc[k * num_seqs : (k + 1) * num_seqs, cols] + bias[k : k + 1, cols].astype(jnp.float32)
            if t < heads:
                qs[pl.ds(k * heads + t, num_seqs, stride=kv * heads + 1), :] = rotate(value)
            elif t == heads:
                kn[pl.ds(k, num_seqs, stride=kv), :] = rotate(value)
            else:
                vn[pl.ds(k, num_seqs, stride=kv), :] = value

    base = lax.axis_index("sp") * (ctx2 // kv)
    group = 16
    group_row = lax.broadcasted_iota(jnp.int32, (group, LANES), 0)

    @pl.loop(0, blocks)
    def _(block):
        cache_copy(k_hbm, kbuf, k_sem, block).wait()
        cache_copy(v_hbm, vbuf, v_sem, block).wait()
        found = []
        for i in range(seqs):
            b = block * seqs + i
            local = lens[b] - base
            here = jnp.logical_and(local >= 0, local < ctx2 // kv)
            place = jnp.where(here, local * kv, 0)
            start = pl.multiple_of(place // group * group, group)
            target = jnp.where(here, place - start, group)
            for buf, new in ((kbuf, kn), (vbuf, vn)):
                found.append((buf, b, start, target, new[pl.ds(b * kv, kv), :], buf[b, pl.ds(start, group), :]))
        values = []
        for _, _, _, target, fresh, old in found:
            value = old.astype(jnp.float32)
            for k in range(kv):
                value = jnp.where(group_row == target + k, fresh[k : k + 1], value)
            values.append(value.astype(jnp.bfloat16))
        for (buf, b, start, _, _, _), value in zip(found, values):
            buf[b, pl.ds(start, group), :] = value
        cache_write(k_out, kbuf, ko_sem, block).start()
        cache_write(v_out, vbuf, vo_sem, block).start()

    @pl.loop(0, blocks)
    def _(block):
        cache_write(k_out, kbuf, ko_sem, block).wait()
        cache_write(v_out, vbuf, vo_sem, block).wait()


def front(hidden, seq_lens, cos_t, sin_t, k_cache, v_cache, gain, w_qkv, b_qkv):
    num_seqs, d_model = hidden.shape
    kv, qkv = w_qkv.shape[1:]
    heads = qkv // LANES - 2
    depth2, slots = 1024, 4
    chunks = d_model * kv // depth2
    blocks = RING * SUBS
    f32, bf16 = jnp.float32, jnp.bfloat16
    dma = pltpu.SemaphoreType.DMA
    hbm = pl.BlockSpec(memory_space=pl.ANY)
    vmem = pl.BlockSpec(memory_space=pltpu.VMEM)
    operands = (hidden, seq_lens, cos_t, sin_t, k_cache, v_cache, gain, w_qkv, b_qkv)
    return pl.pallas_call(
        front_kernel,
        out_shape=(
            jax.ShapeDtypeStruct((num_seqs * (kv * heads + 1), LANES), f32),
            pltpu.VMEM(k_cache.shape, bf16), pltpu.VMEM(v_cache.shape, bf16),
            jax.ShapeDtypeStruct(k_cache.shape, bf16), jax.ShapeDtypeStruct(v_cache.shape, bf16)),
        in_specs=[hbm] * len(operands),
        out_specs=(vmem, vmem, vmem, hbm, hbm),
        scratch_shapes=[
            pltpu.VMEM(hidden.shape, bf16),
            pltpu.SMEM(seq_lens.shape, jnp.int32),
            pltpu.VMEM(cos_t.shape, f32),
            pltpu.VMEM(sin_t.shape, f32),
            pltpu.VMEM(gain.shape, bf16),
            pltpu.VMEM(b_qkv.shape, bf16),
            pltpu.VMEM((chunks, kv * num_seqs, depth2), bf16),
            pltpu.VMEM((slots, depth2, qkv), bf16),
            pltpu.VMEM((kv * num_seqs, qkv), f32),
            pltpu.VMEM((num_seqs * kv, LANES), f32),
            pltpu.VMEM((num_seqs * kv, LANES), f32),
            dma((6,)), dma((slots,)), dma((blocks,)), dma((blocks,)), dma((blocks,)), dma((blocks,)),
        ],
        compiler_params=pltpu.CompilerParams(vmem_limit_bytes=FRONT_MIB * 2**20),
        cost_estimate=pl.CostEstimate(flops=4 * num_seqs * d_model * kv * qkv, bytes_accessed=40 * 2**20, transcendentals=0),
        name="front",
    )(*(pltpu.with_memory_space_constraint(a, pltpu.HBM) for a in operands))


def solution(mesh):
    cache_spec = P("dp", "sp", "tp", None)

    def block_step(hidden, seq_lens, rope_cos, rope_sin, k_cache, v_cache, norm_gain, w_qkv, b_qkv, sink_logits, w_o, b_o):
        num_seqs, ctx, kv, head_dim = k_cache.shape
        assert head_dim == LANES and mesh.shape["tp"] == RING and mesh.shape["sp"] == RING * CORES
        flat = (num_seqs, ctx * kv, head_dim)
        queries, k_near, v_near, k_out, v_out = front(
            hidden, seq_lens, rope_cos.T, rope_sin.T, k_cache.reshape(flat), v_cache.reshape(flat), norm_gain.reshape(-1, LANES), w_qkv, b_qkv)
        out_hidden = combine(queries, k_near, v_near, seq_lens, sink_logits, hidden, b_o.reshape(-1, LANES), w_o)
        return out_hidden, k_out.reshape(k_cache.shape), v_out.reshape(v_cache.shape)

    return jax.shard_map(block_step, mesh=mesh, in_specs=(P("dp", None), P("dp"), P("dp", None), P("dp", None), cache_spec, cache_spec, P(None), P(None, "tp", None), P("tp", None), P("tp"), P("tp", None), P(None)), out_specs=(P("dp", None), cache_spec, cache_spec), check_vma=False)
```

time: 65.8 us -> 60.2 us (0.915)
  Pallas kernels: 61.1 us -> 58.3 us
  local copies, waits for them, and re-layouts: 3.83 us -> 1.07 us
    pallas_call x2, Pallas kernels: 61.1 us -> 58.3 us  [the longest x1 42.5 us: combine(): pl.pallas_call(functools.partial(combine_kernel, seqs, LANES ** (-0.5)),...]
    broadcast_in_dim x3 -> x0, local copies, waits for them, and re-layouts: 2.76 us -> none  [the longest x1 1.32 us: block_step(): norm_gain[None, :]]
where the time goes in v6:
time: 60.2 us; the launch traced here: 60.1 us
  Pallas kernels  58.3 us (97%)
  local copies, waits for them, and re-layouts  1.07 us (2%)
  between operations  0.68 us (1%)
    pallas_call x1, Pallas kernels, combine(): pl.pallas_call(functools.partial(combine_kernel, seqs, LANES ** (-0.5)),...  42.5 us
    pallas_call x1, Pallas kernels, front(): pl.pallas_call(front_kernel, out_shape=(jax.ShapeDtypeStruct((num_seqs *...  15.8 us

profile of v6, /device:TPU:97, one launch (start us, length us, event | category | flops | bytes accessed | tf_op | source)
XLA Modules:
  0.0 60.1 jit_solution(10432318581355799002)
XLA Ops:
  0.6 0.0 copy-start
  0.6 0.0 copy-start.1
  0.7 15.8 %front.1 = (f32[2176,128]{1,0:T(8,128)S(1)}, bf16[128,128,128]{2,1,0:T(8,128)(2,1)S(1)}, bf16[128,128,128]{2,1,0:T(8,128)(2,1)S(1)}, bf16[128,128,128]{2,1,0:T(8,128)(2,1)}, bf16[128,128,128]{2,1,0:T(8,128)(2,1)}) custom-call(bf16[128,5120]{1,0:T(8,128)(2,1)} %x_hbm.3, s32[128]{0:T(128)} %lens.1, f32[64,128]{1,0:T(8,128)} %bitcast.10, f32[64,128]{1,0:T(8,128)} %bitcast.11, ...), custom_call_target="tpu_custom_call" | custom-call | flops 6710886400 | bytes 41943040 | tf_op jit(solution)/shard_map/front/pallas_call | solution.py:536
  16.5 0.0 copy-done
  16.5 0.0 copy-done.1
  16.5 42.5 %combine.1 = bf16[128,5120]{1,0:T(8,128)(2,1)S(1)} custom-call(f32[2176,128]{1,0:T(8,128)S(1)} %get-tuple-element.8.q_ref, bf16[128,128,128]{2,1,0:T(8,128)(2,1)S(1)} %get-tuple-element.9.k_ref, bf16[128,128,128]{2,1,0:T(8,128)(2,1)S(1)} %get-tuple-element.10.v_ref, s32[128]{0:T(128)S(1)} %copy-done, f32[16]{0:T(128)S(1)} %copy-done.1, ...), custom_call_target="tpu_custom_call" | custom-call | flops 335544320 | bytes 31457280 | tf_op jit(solution)/shard_map/combine/pallas_call | solution.py:345
  59.0 1.1 %copy.16 = bf16[128,5120]{1,0:T(8,128)(2,1)} copy(bf16[128,5120]{1,0:T(8,128)(2,1)S(1)} %combine.1) | data formatting | bytes 2621440
Async XLA Ops:
  0.6 15.8 %copy-start = (s32[128]{0:T(128)S(1)}, s32[128]{0:T(128)}, u32[]{:S(2)}) copy-start(s32[128]{0:T(128)} %lens.1) | copy-start | bytes 1540
  0.6 15.8 %copy-start.1 = (f32[16]{0:T(128)S(1)}, f32[16]{0:T(128)}, u32[]{:S(2)}) copy-start(f32[16]{0:T(128)} %sink_ref.1) | copy-start | bytes 196

commit v7 on v6

--- a/solution.py
+++ b/solution.py
@@ -13,7 +13,8 @@
 HALF = LANES // 2
 SUBS = 2
 CORES = 2
-FRONT_MIB = 34
+PROJECT_MIB = 28
+UPDATE_MIB = 4
 COMBINE_MIB = 26
 WAVE = 4
 RING = 4
@@ -107,6 +108,7 @@
     kv = p_ref.shape[2]
     q_rows = kv * heads
     ctx2 = k_ref.shape[1]
+    q_stride = q_ref.shape[1] // (heads + 2)
     row = lax.broadcasted_iota(jnp.int32, (q_rows, ctx2), 0)
     lane = lax.broadcasted_iota(jnp.int32, (q_rows, ctx2), 1)
     position = jnp.where(lane % kv == row // heads, lane // kv + sp * (ctx2 // kv), jnp.iinfo(jnp.int32).max)
@@ -122,7 +124,7 @@
         for turn in range(len(waves) + 2):
             if turn < len(waves):
                 for i in waves[turn]:
-                    q = q_ref[pl.ds((first + i) * (q_rows + 1), q_rows), :].astype(jnp.bfloat16)
+                    q = jnp.concatenate([q_ref[k, pl.ds(first + i, heads, stride=q_stride), :] for k in range(kv)], axis=0).astype(jnp.bfloat16)
                     logits[i] = lax.dot_general(q, k_ref[first + i], (((1,), (1,)), ((), ())), preferred_element_type=jnp.float32)
             if 0 <= turn - 1 < len(waves):
                 members = waves[turn - 1]
@@ -378,48 +380,39 @@
     )(queries, k_out, v_out, seq_lens, sinks, *(pltpu.with_memory_space_constraint(a, pltpu.HBM) for a in (hidden, b_o, w_o)))
 
 
-def front_kernel(
-    x_hbm, len_hbm, cos_hbm, sin_hbm, k_hbm, v_hbm, gain_hbm, w_hbm, bias_hbm,
-    qs, kbuf, vbuf, k_out, v_out,
-    xbuf, lens, cos, sin, gain, bias, hexp, wbuf, acc, kn, vn,
-    in_sem, w_sem, k_sem, v_sem, ko_sem, vo_sem,
+def project_kernel(
+    x_hbm, cos_hbm, sin_hbm, k_hbm, v_hbm, gain_hbm, w_hbm, bias_hbm,
+    heads_ref, kbuf, vbuf,
+    xbuf, cos, sin, gain, bias, hexp, wbuf, acc,
+    in_sem, w_sem, cache_sem, send_sem, recv_sem,
 ):
     num_seqs, d_model = x_hbm.shape
     kv = w_hbm.shape[1]
     qkv = w_hbm.shape[2]
-    tiles = qkv // LANES
-    heads = tiles - 2
-    slots, depth2, _ = wbuf.shape
+    tiles = qkv // LANES // CORES
+    slots, depth2, cols = wbuf.shape
     chunks = d_model * kv // depth2
-    blocks = k_sem.shape[0]
-    seqs = num_seqs // blocks
-    ctx2 = k_hbm.shape[1]
+    stride = heads_ref.shape[1] // (CORES * tiles)
+    c = lax.axis_index("sp") % CORES
+    partner = {"sp": lax.axis_index("sp") + 1 - 2 * c}
     w_rows = w_hbm.reshape(d_model * kv, qkv)
+    first_col = pl.multiple_of(c * cols, LANES)
 
     def w_copy(chunk, slot):
         return pltpu.make_async_copy(
-            w_rows.at[pl.ds(pl.multiple_of(chunk * depth2, depth2), depth2), :], wbuf.at[slot], w_sem.at[slot])
-
-    def w_start(chunk, slot):
-        w_copy(chunk, slot).start()
+            w_rows.at[pl.ds(pl.multiple_of(chunk * depth2, depth2), depth2), pl.ds(first_col, cols)], wbuf.at[slot], w_sem.at[slot])
 
     small = [
         pltpu.make_async_copy(src, dst, in_sem.at[i])
         for i, (src, dst) in enumerate((
-            (x_hbm, xbuf), (gain_hbm, gain), (len_hbm, lens), (cos_hbm, cos), (sin_hbm, sin), (bias_hbm, bias)))
+            (x_hbm, xbuf), (gain_hbm, gain), (cos_hbm, cos), (sin_hbm, sin), (bias_hbm, bias)))
     ]
     for copy in small:
         copy.start()
-    for slot in range(slots - 1):
-        w_start(slot, slot)
-
-    def cache_copy(hbm, buf, sem, block):
-        rows = pl.ds(block * seqs, seqs)
-        return pltpu.make_async_copy(hbm.at[rows], buf.at[rows], sem.at[block])
-
-    def cache_write(hbm, buf, sem, block):
-        rows = pl.ds(block * seqs, seqs)
-        return pltpu.make_async_copy(buf.at[rows], hbm.at[rows], sem.at[block])
+    for slot in range(slots):
+        w_copy(slot, slot).start()
+    barrier = pltpu.get_barrier_semaphore()
+    pl.semaphore_signal(barrier, inc=1, device_id=partner, device_id_type=MESH)
 
     small[0].wait()
     small[1].wait()
@@ -443,57 +436,107 @@
                 place = t % per_chunk * kv * LANES + j * LANES
                 hexp[t // per_chunk, k * num_seqs : (k + 1) * num_seqs, place : place + LANES] = pltpu.roll(piece, k, 1) if k else piece
     acc[...] = jnp.zeros_like(acc)
+    cache_copies = [pltpu.make_async_copy(src, dst, cache_sem.at[i]) for i, (src, dst) in enumerate(((k_hbm, kbuf), (v_hbm, vbuf)))]
 
     @pl.loop(0, chunks)
     def _(chunk):
         slot = lax.rem(chunk, slots)
-
-        @pl.when(chunk + slots - 1 < chunks)
-        def _():
-            w_start(chunk + slots - 1, lax.rem(chunk + slots - 1, slots))
-
-        @pl.when(chunk == chunks - slots)
-        def _():
-            for block in range(blocks):
-                cache_copy(k_hbm, kbuf, k_sem, block).start()
-                cache_copy(v_hbm, vbuf, v_sem, block).start()
-
         w_copy(chunk, slot).wait()
         lhs = hexp.at[chunk]
         for t in range(0, tiles, 2):
-            cols = slice(t * LANES, (t + 2) * LANES)
-            acc[:, cols] += jnp.dot(lhs[...], wbuf[slot, :, cols], preferred_element_type=jnp.float32)
+            part = slice(t * LANES, min(t + 2, tiles) * LANES)
+            acc[:, part] += jnp.dot(lhs[...], wbuf[slot, :, part], preferred_element_type=jnp.float32)
+
+        @pl.when(chunk + slots < chunks)
+        def _():
+            w_copy(chunk + slots, slot).start()
+
+        @pl.when(chunk + slots == chunks - 1)
+        def _():
+            for copy in cache_copies:
+                copy.start()
 
     for copy in small[2:]:
         copy.wait()
     cos_t = jnp.transpose(jnp.concatenate([cos[...], cos[...]], axis=0))
     sin_t = jnp.transpose(jnp.concatenate([-sin[...], sin[...]], axis=0))
-
-    def rotate(t):
-        return t * cos_t + pltpu.roll(t, HALF, 1) * sin_t
-
-    def rounded(t):
-        return t.astype(jnp.bfloat16).astype(jnp.float32)
+    pl.semaphore_wait(barrier, 1)
+
+    def mine(k):
+        rows = tiles * stride
+        return heads_ref.at[k, pl.ds(pl.multiple_of(c * rows, 8), rows)]
 
     for k in range(kv):
-        for t in range(tiles):
-            cols = slice(t * LANES, (t + 1) * LANES)
-            value = acc[k * num_seqs : (k + 1) * num_seqs, cols] + bias[k : k + 1, cols].astype(jnp.float32)
-            if t < heads:
-                qs[pl.ds(k * heads + t, num_seqs, stride=kv * heads + 1), :] = rotate(value)
-            elif t == heads:
-                kn[pl.ds(k, num_seqs, stride=kv), :] = rotate(value)
-            else:
-                vn[pl.ds(k, num_seqs, stride=kv), :] = value
-
+        for j in range(tiles):
+            tile = c * tiles + j
+            value = acc[k * num_seqs : (k + 1) * num_seqs, j * LANES : (j + 1) * LANES]
+            value += bias[k : k + 1, pl.ds(pl.multiple_of(tile * LANES, LANES), LANES)].astype(jnp.float32)
+            turned = value * cos_t + pltpu.roll(value, HALF, 1) * sin_t
+            value = jnp.where(jnp.full(value.shape, tile, jnp.int32) == CORES * tiles - 1, value, turned)
+            heads_ref[k, pl.ds(pl.multiple_of(tile * stride, 8), num_seqs), :] = value.astype(jnp.bfloat16).astype(jnp.float32)
+        pltpu.make_async_remote_copy(
+            src_ref=mine(k), dst_ref=mine(k), send_sem=send_sem.at[k], recv_sem=recv_sem.at[k],
+            device_id=partner, device_id_type=MESH).start()
+    for copy in cache_copies:
+        copy.wait()
+    for k in range(kv):
+        copy = pltpu.make_async_remote_copy(
+            src_ref=mine(k), dst_ref=mine(k), send_sem=send_sem.at[k], recv_sem=recv_sem.at[k],
+            device_id=partner, device_id_type=MESH)
+        copy.wait_send()
+        copy.wait_recv()
+
+
+def project(hidden, cos_t, sin_t, k_cache, v_cache, gain, w_qkv, b_qkv):
+    num_seqs, d_model = hidden.shape
+    kv, qkv = w_qkv.shape[1:]
+    tiles = qkv // LANES
+    depth2, slots = 1024, 6
+    chunks = d_model * kv // depth2
+    f32, bf16 = jnp.float32, jnp.bfloat16
+    dma = pltpu.SemaphoreType.DMA
+    hbm = pl.BlockSpec(memory_space=pl.ANY)
+    vmem = pl.BlockSpec(memory_space=pltpu.VMEM)
+    operands = (hidden, cos_t, sin_t, k_cache, v_cache, gain, w_qkv, b_qkv)
+    return pl.pallas_call(
+        project_kernel,
+        out_shape=(pltpu.VMEM((kv, tiles * (num_seqs + 8), LANES), f32), pltpu.VMEM(k_cache.shape, bf16), pltpu.VMEM(v_cache.shape, bf16)),
+        in_specs=[hbm] * len(operands),
+        out_specs=(vmem, vmem, vmem),
+        scratch_shapes=[
+            pltpu.VMEM(hidden.shape, bf16),
+            pltpu.VMEM(cos_t.shape, f32),
+            pltpu.VMEM(sin_t.shape, f32),
+            pltpu.VMEM(gain.shape, bf16),
+            pltpu.VMEM(b_qkv.shape, bf16),
+            pltpu.VMEM((chunks, kv * num_seqs, depth2), bf16),
+            pltpu.VMEM((slots, depth2, qkv // CORES), bf16),
+            pltpu.VMEM((kv * num_seqs, qkv // CORES), f32),
+            dma((5,)), dma((slots,)), dma((2,)), dma((kv,)), dma((kv,)),
+        ],
+        compiler_params=pltpu.CompilerParams(collective_id=1, has_side_effects=True, vmem_limit_bytes=PROJECT_MIB * 2**20),
+        cost_estimate=pl.CostEstimate(flops=2 * num_seqs * d_model * kv * qkv, bytes_accessed=24 * 2**20, transcendentals=0),
+        name="project",
+    )(*(pltpu.with_memory_space_constraint(a, pltpu.HBM) for a in operands))
+
+
+def update_kernel(lens, heads_ref, k_in, v_in, kbuf, vbuf, k_out, v_out, ko_sem, vo_sem):
+    kv = heads_ref.shape[0]
+    num_seqs, ctx2 = kbuf.shape[:2]
+    blocks = ko_sem.shape[0]
+    seqs = num_seqs // blocks
+    stride = num_seqs + 8
+    tiles = heads_ref.shape[1] // stride
     base = lax.axis_index("sp") * (ctx2 // kv)
     group = 16
     group_row = lax.broadcasted_iota(jnp.int32, (group, LANES), 0)
 
+    def cache_write(hbm, buf, sem, block):
+        rows = pl.ds(block * seqs, seqs)
+        return pltpu.make_async_copy(buf.at[rows], hbm.at[rows], sem.at[block])
+
     @pl.loop(0, blocks)
     def _(block):
-        cache_copy(k_hbm, kbuf, k_sem, block).wait()
-        cache_copy(v_hbm, vbuf, v_sem, block).wait()
         found = []
         for i in range(seqs):
             b = block * seqs + i
@@ -502,13 +545,14 @@
             place = jnp.where(here, local * kv, 0)
             start = pl.multiple_of(place // group * group, group)
             target = jnp.where(here, place - start, group)
-            for buf, new in ((kbuf, kn), (vbuf, vn)):
-                found.append((buf, b, start, target, new[pl.ds(b * kv, kv), :], buf[b, pl.ds(start, group), :]))
+            for n, buf in enumerate((kbuf, vbuf)):
+                fresh = [heads_ref[k, pl.ds((tiles - 2 + n) * stride + b, 1), :] for k in range(kv)]
+                found.append((buf, b, start, target, fresh, buf[b, pl.ds(start, group), :]))
         values = []
         for _, _, _, target, fresh, old in found:
             value = old.astype(jnp.float32)
             for k in range(kv):
-                value = jnp.where(group_row == target + k, fresh[k : k + 1], value)
+                value = jnp.where(group_row == target + k, fresh[k], value)
             values.append(value.astype(jnp.bfloat16))
         for (buf, b, start, _, _, _), value in zip(found, values):
             buf[b, pl.ds(start, group), :] = value
@@ -521,44 +565,24 @@
         cache_write(v_out, vbuf, vo_sem, block).wait()
 
 
-def front(hidden, seq_lens, cos_t, sin_t, k_cache, v_cache, gain, w_qkv, b_qkv):
-    num_seqs, d_model = hidden.shape
-    kv, qkv = w_qkv.shape[1:]
-    heads = qkv // LANES - 2
-    depth2, slots = 1024, 4
-    chunks = d_model * kv // depth2
+def update(seq_lens, heads_out, k_near, v_near):
     blocks = RING * SUBS
-    f32, bf16 = jnp.float32, jnp.bfloat16
-    dma = pltpu.SemaphoreType.DMA
     hbm = pl.BlockSpec(memory_space=pl.ANY)
     vmem = pl.BlockSpec(memory_space=pltpu.VMEM)
-    operands = (hidden, seq_lens, cos_t, sin_t, k_cache, v_cache, gain, w_qkv, b_qkv)
+    near = pltpu.VMEM(k_near.shape, k_near.dtype)
+    far = jax.ShapeDtypeStruct(k_near.shape, k_near.dtype)
+    dma = pltpu.SemaphoreType.DMA
     return pl.pallas_call(
-        front_kernel,
-        out_shape=(
-            jax.ShapeDtypeStruct((num_seqs * (kv * heads + 1), LANES), f32),
-            pltpu.VMEM(k_cache.shape, bf16), pltpu.VMEM(v_cache.shape, bf16),
-            jax.ShapeDtypeStruct(k_cache.shape, bf16), jax.ShapeDtypeStruct(v_cache.shape, bf16)),
-        in_specs=[hbm] * len(operands),
-        out_specs=(vmem, vmem, vmem, hbm, hbm),
-        scratch_shapes=[
-            pltpu.VMEM(hidden.shape, bf16),
-            pltpu.SMEM(seq_lens.shape, jnp.int32),
-            pltpu.VMEM(cos_t.shape, f32),
-            pltpu.VMEM(sin_t.shape, f32),
-            pltpu.VMEM(gain.shape, bf16),
-            pltpu.VMEM(b_qkv.shape, bf16),
-            pltpu.VMEM((chunks, kv * num_seqs, depth2), bf16),
-            pltpu.VMEM((slots, depth2, qkv), bf16),
-            pltpu.VMEM((kv * num_seqs, qkv), f32),
-            pltpu.VMEM((num_seqs * kv, LANES), f32),
-            pltpu.VMEM((num_seqs * kv, LANES), f32),
-            dma((6,)), dma((slots,)), dma((blocks,)), dma((blocks,)), dma((blocks,)), dma((blocks,)),
-        ],
-        compiler_params=pltpu.CompilerParams(vmem_limit_bytes=FRONT_MIB * 2**20),
-        cost_estimate=pl.CostEstimate(flops=4 * num_seqs * d_model * kv * qkv, bytes_accessed=40 * 2**20, transcendentals=0),
-        name="front",
-    )(*(pltpu.with_memory_space_constraint(a, pltpu.HBM) for a in operands))
+        update_kernel,
+        out_shape=(near, near, far, far),
+        in_specs=[pl.BlockSpec(memory_space=pltpu.SMEM), vmem, vmem, vmem],
+        out_specs=(vmem, vmem, hbm, hbm),
+        scratch_shapes=[dma((blocks,)), dma((blocks,))],
+        input_output_aliases={2: 0, 3: 1},
+        compiler_params=pltpu.CompilerParams(vmem_limit_bytes=UPDATE_MIB * 2**20),
+        cost_estimate=pl.CostEstimate(flops=10**6, bytes_accessed=10 * 2**20, transcendentals=0),
+        name="update",
+    )(seq_lens, heads_out, k_near, v_near)
 
 
 def solution(mesh):
@@ -568,9 +592,10 @@
         num_seqs, ctx, kv, head_dim = k_cache.shape
         assert head_dim == LANES and mesh.shape["tp"] == RING and mesh.shape["sp"] == RING * CORES
         flat = (num_seqs, ctx * kv, head_dim)
-        queries, k_near, v_near, k_out, v_out = front(
-            hidden, seq_lens, rope_cos.T, rope_sin.T, k_cache.reshape(flat), v_cache.reshape(flat), norm_gain.reshape(-1, LANES), w_qkv, b_qkv)
-        out_hidden = combine(queries, k_near, v_near, seq_lens, sink_logits, hidden, b_o.reshape(-1, LANES), w_o)
+        heads_out, k_near, v_near = project(
+            hidden, rope_cos.T, rope_sin.T, k_cache.reshape(flat), v_cache.reshape(flat), norm_gain.reshape(-1, LANES), w_qkv, b_qkv)
+        k_near, v_near, k_out, v_out = update(seq_lens, heads_out, k_near, v_near)
+        out_hidden = combine(heads_out, k_near, v_near, seq_lens, sink_logits, hidden, b_o.reshape(-1, LANES), w_o)
         return out_hidden, k_out.reshape(k_cache.shape), v_out.reshape(v_cache.shape)
 
     return jax.shard_map(block_step, mesh=mesh, in_specs=(P("dp", None), P("dp"), P("dp", None), P("dp", None), cache_spec, cache_spec, P(None), P(None, "tp", None), P("tp", None), P("tp"), P("tp", None), P(None)), out_specs=(P("dp", None), cache_spec, cache_spec), check_vma=False)

time: 60.2 us -> 59 us (0.980)
  Pallas kernels: 58.3 us -> 57.2 us
    pallas_call x1, Pallas kernels: 42.5 us -> 40.3 us  [combine(): pl.pallas_call(functools.partial(combine_kernel, seqs, LANES ** (-0.5)),...]
    pallas_call x1 -> x2, Pallas kernels: 15.8 us -> 16.9 us  [the longest x1 12.7 us: project(): pl.pallas_call(project_kernel, out_shape=(pltpu.VMEM((kv, tiles * (num_se...]
where the time goes in v7:
time: 59 us; the launch traced here: 58.9 us
  Pallas kernels  57.2 us (97%)
  local copies, waits for them, and re-layouts  1.07 us (2%)
  between operations  0.69 us (1%)
    pallas_call x1, Pallas kernels, combine(): pl.pallas_call(functools.partial(combine_kernel, seqs, LANES ** (-0.5)),...  40.3 us
    pallas_call x1, Pallas kernels, project(): pl.pallas_call(project_kernel, out_shape=(pltpu.VMEM((kv, tiles * (num_se...  12.7 us
    pallas_call x1, Pallas kernels, update(): pl.pallas_call(update_kernel, out_shape=(near, near, far, far), in_specs=...  4.14 us

profile of v7, /device:TPU:97, one launch (start us, length us, event | category | flops | bytes accessed | tf_op | source)
XLA Modules:
  0.0 58.9 jit_solution(17328239940415366226)
XLA Ops:
  0.6 0.0 copy-start
  0.6 12.7 %project.1 = (f32[2,1360,128]{2,1,0:T(8,128)S(1)}, bf16[128,128,128]{2,1,0:T(8,128)(2,1)S(1)}, bf16[128,128,128]{2,1,0:T(8,128)(2,1)S(1)}) custom-call(bf16[128,5120]{1,0:T(8,128)(2,1)} %x_hbm.3, f32[64,128]{1,0:T(8,128)} %bitcast.10, f32[64,128]{1,0:T(8,128)} %bitcast.11, bf16[128,128,128]{2,1,0:T(8,128)(2,1)} %bitcast.8, bf16[128,128,128]{2,1,0:T(8,128)(2,1)} %bitcast.9, ...), custom_call_target="tpu_custom_call" | custom-call | flops 3355443200 | bytes 25165824 | tf_op jit(solution)/shard_map/project/pallas_call | solution.py:501
  13.4 0.0 copy-done
  13.4 0.0 copy-start.1
  13.4 4.1 %update.1 = (bf16[128,128,128]{2,1,0:T(8,128)(2,1)S(1)}, bf16[128,128,128]{2,1,0:T(8,128)(2,1)S(1)}, bf16[128,128,128]{2,1,0:T(8,128)(2,1)}, bf16[128,128,128]{2,1,0:T(8,128)(2,1)}) custom-call(s32[128]{0:T(128)S(1)} %copy-done, f32[2,1360,128]{2,1,0:T(8,128)S(1)} %get-tuple-element.10.heads_ref.q_ref, ...), custom_call_target="tpu_custom_call", output_to_operand_aliasing={{0}: (2, {}), {1}: (3, {})} | custom-call | flops 1000000 | bytes 10485760 | tf_op jit(solution)/shard_map/update/pallas_call | solution.py:575
  17.6 0.0 copy-done.1
  17.6 40.3 %combine.1 = bf16[128,5120]{1,0:T(8,128)(2,1)S(1)} custom-call(f32[2,1360,128]{2,1,0:T(8,128)S(1)} %get-tuple-element.10.heads_ref.q_ref, bf16[128,128,128]{2,1,0:T(8,128)(2,1)S(1)} %get-tuple-element.13.k_ref, bf16[128,128,128]{2,1,0:T(8,128)(2,1)S(1)} %get-tuple-element.14.v_ref, s32[128]{0:T(128)S(1)} %copy-done, f32[16]{0:T(128)S(1)} %copy-done.1, ...), custom_call_target="tpu_custom_call" | custom-call | flops 335544320 | bytes 31457280 | tf_op jit(solution)/shard_map/combine/pallas_call | solution.py:347
  57.9 1.1 %copy.20 = bf16[128,5120]{1,0:T(8,128)(2,1)} copy(bf16[128,5120]{1,0:T(8,128)(2,1)S(1)} %combine.1) | data formatting | bytes 2621440
Async XLA Ops:
  0.6 12.8 %copy-start = (s32[128]{0:T(128)S(1)}, s32[128]{0:T(128)}, u32[]{:S(2)}) copy-start(s32[128]{0:T(128)} %lens.3) | copy-start | bytes 1540
  13.4 4.2 %copy-start.1 = (f32[16]{0:T(128)S(1)}, f32[16]{0:T(128)}, u32[]{:S(2)}) copy-start(f32[16]{0:T(128)} %sink_ref.1) | copy-start | bytes 196

commit v8 on v7

--- a/solution.py
+++ b/solution.py
@@ -13,7 +13,7 @@
 HALF = LANES // 2
 SUBS = 2
 CORES = 2
-PROJECT_MIB = 28
+PROJECT_MIB = 30
 UPDATE_MIB = 4
 COMBINE_MIB = 26
 WAVE = 4
@@ -165,17 +165,19 @@
         send(cb.at[2, s], rm.at[s], b_send.at[0], rm_recv.at[s], to_xn)
 
     attend_both(xo)
+    attend(xn, 0)
     for s in range(SUBS):
+        relay(s)
+    for s in range(1, SUBS):
         attend(xn, s)
-        relay(s)
     attend_both(xp)
     for s in range(SUBS):
         arrived(ra.at[xp, s], a_recv.at[xp, s])
         merge_into(cb.at[1, s], (p_ref.at[xp, s, c], ra.at[xp, s]), seqs)
         send(cb.at[1, s], rd.at[s], b_send.at[0], rd_recv.at[s], to_xp)
     for s in range(SUBS):
-        attend(x, s)
         pass_on(s)
+    attend_both(x)
     for s in range(SUBS):
         arrived(ra.at[x, s], a_recv.at[x, s])
         merge_into(cb.at[3, s], (p_ref.at[x, s, c], ra.at[x, s]), seqs)
@@ -390,17 +392,16 @@
     kv = w_hbm.shape[1]
     qkv = w_hbm.shape[2]
     tiles = qkv // LANES // CORES
-    slots, depth2, cols = wbuf.shape
-    chunks = d_model * kv // depth2
+    chunks, depth2, cols = wbuf.shape
     stride = heads_ref.shape[1] // (CORES * tiles)
     c = lax.axis_index("sp") % CORES
     partner = {"sp": lax.axis_index("sp") + 1 - 2 * c}
     w_rows = w_hbm.reshape(d_model * kv, qkv)
     first_col = pl.multiple_of(c * cols, LANES)
 
-    def w_copy(chunk, slot):
+    def w_copy(chunk):
         return pltpu.make_async_copy(
-            w_rows.at[pl.ds(pl.multiple_of(chunk * depth2, depth2), depth2), pl.ds(first_col, cols)], wbuf.at[slot], w_sem.at[slot])
+            w_rows.at[pl.ds(chunk * depth2, depth2), pl.ds(first_col, cols)], wbuf.at[chunk], w_sem.at[chunk])
 
     small = [
         pltpu.make_async_copy(src, dst, in_sem.at[i])
@@ -409,8 +410,8 @@
     ]
     for copy in small:
         copy.start()
-    for slot in range(slots):
-        w_copy(slot, slot).start()
+    for chunk in range(chunks):
+        w_copy(chunk).start()
     barrier = pltpu.get_barrier_semaphore()
     pl.semaphore_signal(barrier, inc=1, device_id=partner, device_id_type=MESH)
 
@@ -425,7 +426,6 @@
         xt = xbuf[:, t * LANES : (t + 1) * LANES].astype(jnp.float32)
         square += xt * xt
     inv_rms = lax.rsqrt(jnp.sum(square, axis=-1, keepdims=True) / d_model + NORM_EPS)
-    per_chunk = depth2 // (kv * LANES)
     for t in range(d_model // LANES):
         xt = xbuf[:, t * LANES : (t + 1) * LANES].astype(jnp.float32)
         ht = (xt * inv_rms * gains[t : t + 1]).astype(jnp.bfloat16)
@@ -433,28 +433,19 @@
         for k in range(kv):
             for j in range(kv):
                 piece = spread[:, j * LANES : (j + 1) * LANES]
-                place = t % per_chunk * kv * LANES + j * LANES
-                hexp[t // per_chunk, k * num_seqs : (k + 1) * num_seqs, place : place + LANES] = pltpu.roll(piece, k, 1) if k else piece
-    acc[...] = jnp.zeros_like(acc)
+                hexp[t * kv + j, k * num_seqs : (k + 1) * num_seqs] = pltpu.roll(piece, k, 1) if k else piece
     cache_copies = [pltpu.make_async_copy(src, dst, cache_sem.at[i]) for i, (src, dst) in enumerate(((k_hbm, kbuf), (v_hbm, vbuf)))]
 
-    @pl.loop(0, chunks)
-    def _(chunk):
-        slot = lax.rem(chunk, slots)
-        w_copy(chunk, slot).wait()
-        lhs = hexp.at[chunk]
+    for copy in cache_copies:
+        copy.start()
+    pieces = depth2 // LANES
+    for chunk in range(chunks):
+        w_copy(chunk).wait()
+        lhs = jnp.concatenate([hexp[chunk * pieces + i] for i in range(pieces)], axis=1)
         for t in range(0, tiles, 2):
             part = slice(t * LANES, min(t + 2, tiles) * LANES)
-            acc[:, part] += jnp.dot(lhs[...], wbuf[slot, :, part], preferred_element_type=jnp.float32)
-
-        @pl.when(chunk + slots < chunks)
-        def _():
-            w_copy(chunk + slots, slot).start()
-
-        @pl.when(chunk + slots == chunks - 1)
-        def _():
-            for copy in cache_copies:
-                copy.start()
+            product = jnp.dot(lhs, wbuf[chunk, :, part], preferred_element_type=jnp.float32)
+            acc[:, part] = acc[:, part] + product if chunk else product
 
     for copy in small[2:]:
         copy.wait()
@@ -491,8 +482,8 @@
     num_seqs, d_model = hidden.shape
     kv, qkv = w_qkv.shape[1:]
     tiles = qkv // LANES
-    depth2, slots = 1024, 6
-    chunks = d_model * kv // depth2
+    chunks = 4
+    depth2 = d_model * kv // chunks
     f32, bf16 = jnp.float32, jnp.bfloat16
     dma = pltpu.SemaphoreType.DMA
     hbm = pl.BlockSpec(memory_space=pl.ANY)
@@ -509,10 +500,10 @@
             pltpu.VMEM(sin_t.shape, f32),
             pltpu.VMEM(gain.shape, bf16),
             pltpu.VMEM(b_qkv.shape, bf16),
-            pltpu.VMEM((chunks, kv * num_seqs, depth2), bf16),
-            pltpu.VMEM((slots, depth2, qkv // CORES), bf16),
+            pltpu.VMEM((d_model * kv // LANES, kv * num_seqs, LANES), bf16),
+            pltpu.VMEM((chunks, depth2, qkv // CORES), bf16),
             pltpu.VMEM((kv * num_seqs, qkv // CORES), f32),
-            dma((5,)), dma((slots,)), dma((2,)), dma((kv,)), dma((kv,)),
+            dma((5,)), dma((chunks,)), dma((2,)), dma((kv,)), dma((kv,)),
         ],
         compiler_params=pltpu.CompilerParams(collective_id=1, has_side_effects=True, vmem_limit_bytes=PROJECT_MIB * 2**20),
         cost_estimate=pl.CostEstimate(flops=2 * num_seqs * d_model * kv * qkv, bytes_accessed=24 * 2**20, transcendentals=0),

time: 59 us -> 58.4 us (0.990)
  Pallas kernels: 57.2 us -> 56.6 us
    pallas_call x1, Pallas kernels: 12.7 us -> 11.4 us  [project(): pl.pallas_call(project_kernel, out_shape=(pltpu.VMEM((kv, tiles * (num_se...]
    pallas_call x1, Pallas kernels: 40.3 us -> 41 us  [combine(): pl.pallas_call(functools.partial(combine_kernel, seqs, LANES ** (-0.5)),...]
where the time goes in v8:
time: 58.4 us; the launch traced here: 58.3 us
  Pallas kernels  56.6 us (97%)
  local copies, waits for them, and re-layouts  1.07 us (2%)
  between operations  0.69 us (1%)
    pallas_call x1, Pallas kernels, combine(): pl.pallas_call(functools.partial(combine_kernel, seqs, LANES ** (-0.5)),...  41 us
    pallas_call x1, Pallas kernels, project(): pl.pallas_call(project_kernel, out_shape=(pltpu.VMEM((kv, tiles * (num_se...  11.4 us
    pallas_call x1, Pallas kernels, update(): pl.pallas_call(update_kernel, out_shape=(near, near, far, far), in_specs=...  4.14 us

profile of v8, /device:TPU:97, one launch (start us, length us, event | category | flops | bytes accessed | tf_op | source)
XLA Modules:
  0.0 58.3 jit_solution(4582328876545034677)
XLA Ops:
  0.6 0.0 copy-start
  0.6 11.4 %project.1 = (f32[2,1360,128]{2,1,0:T(8,128)S(1)}, bf16[128,128,128]{2,1,0:T(8,128)(2,1)S(1)}, bf16[128,128,128]{2,1,0:T(8,128)(2,1)S(1)}) custom-call(bf16[128,5120]{1,0:T(8,128)(2,1)} %x_hbm.3, f32[64,128]{1,0:T(8,128)} %bitcast.10, f32[64,128]{1,0:T(8,128)} %bitcast.11, bf16[128,128,128]{2,1,0:T(8,128)(2,1)} %bitcast.8, bf16[128,128,128]{2,1,0:T(8,128)(2,1)} %bitcast.9, ...), custom_call_target="tpu_custom_call" | custom-call | flops 3355443200 | bytes 25165824 | tf_op jit(solution)/shard_map/project/pallas_call | solution.py:492
  12.0 0.0 copy-done
  12.1 0.0 copy-start.1
  12.1 4.1 %update.1 = (bf16[128,128,128]{2,1,0:T(8,128)(2,1)S(1)}, bf16[128,128,128]{2,1,0:T(8,128)(2,1)S(1)}, bf16[128,128,128]{2,1,0:T(8,128)(2,1)}, bf16[128,128,128]{2,1,0:T(8,128)(2,1)}) custom-call(s32[128]{0:T(128)S(1)} %copy-done, f32[2,1360,128]{2,1,0:T(8,128)S(1)} %get-tuple-element.10.heads_ref.q_ref, ...), custom_call_target="tpu_custom_call", output_to_operand_aliasing={{0}: (2, {}), {1}: (3, {})} | custom-call | flops 1000000 | bytes 10485760 | tf_op jit(solution)/shard_map/update/pallas_call | solution.py:566
  16.2 0.0 copy-done.1
  16.2 41.0 %combine.1 = bf16[128,5120]{1,0:T(8,128)(2,1)S(1)} custom-call(f32[2,1360,128]{2,1,0:T(8,128)S(1)} %get-tuple-element.10.heads_ref.q_ref, bf16[128,128,128]{2,1,0:T(8,128)(2,1)S(1)} %get-tuple-element.13.k_ref, bf16[128,128,128]{2,1,0:T(8,128)(2,1)S(1)} %get-tuple-element.14.v_ref, s32[128]{0:T(128)S(1)} %copy-done, f32[16]{0:T(128)S(1)} %copy-done.1, ...), custom_call_target="tpu_custom_call" | custom-call | flops 335544320 | bytes 31457280 | tf_op jit(solution)/shard_map/combine/pallas_call | solution.py:349
  57.3 1.1 %copy.20 = bf16[128,5120]{1,0:T(8,128)(2,1)} copy(bf16[128,5120]{1,0:T(8,128)(2,1)S(1)} %combine.1) | data formatting | bytes 2621440
Async XLA Ops:
  0.6 11.4 %copy-start = (s32[128]{0:T(128)S(1)}, s32[128]{0:T(128)}, u32[]{:S(2)}) copy-start(s32[128]{0:T(128)} %lens.3) | copy-start | bytes 1540
  12.1 4.2 %copy-start.1 = (f32[16]{0:T(128)S(1)}, f32[16]{0:T(128)}, u32[]{:S(2)}) copy-start(f32[16]{0:T(128)} %sink_ref.1) | copy-start | bytes 196

commit v9 on v8

--- a/solution.py
+++ b/solution.py
@@ -251,9 +251,9 @@
         pushes.append(q)
         send(g.at[q, xx, yy], g.at[q, xx, yy], g_send.at[0], g_recv.at[q, xx, yy], where)
 
-    def share(q, first, second):
+    def share(q, first, second, group):
         xx, yy = slot(q, first, second)
-        send(g.at[q, xx, yy], gp.at[q, xx, yy], gp_send.at[0], gp_recv.at[q, xx, yy], partner)
+        send(g.at[q, xx, yy], gp.at[q, xx, yy], gp_send.at[0], gp_recv.at[group], partner)
 
     def receive(q, first, second):
         xx, yy = slot(q, first, second)
@@ -274,7 +274,7 @@
         for axis in (q, 1 - q):
             for kind in range(2):
                 push(q, first_now[q], first_now[1 - q], ahead[axis][kind])
-        share(q, first_now[q], first_now[1 - q])
+        share(q, first_now[q], first_now[1 - q], 0)
 
     def spread(q, first, forward):
         other = 1 - q
@@ -283,49 +283,49 @@
             push(q, first, first_now[other], ahead[q][0])
         for kind in range(2):
             push(q, first, first_now[other], ahead[other][kind])
-        share(q, first, first_now[other])
-        keep(q, first, first_now[other])
-
-    def settle(q, first, second, forward):
+        share(q, first, first_now[other], 0)
+
+    def settle(q, first, second, where, group):
         receive(q, first, second)
-        if forward:
-            push(q, first, second, ahead[1 - q][0])
-        share(q, first, second)
-        keep(q, first, second)
+        for target in where:
+            push(q, first, second, target)
+        share(q, first, second, group)
 
     both = range(SUBS)
-    for q in both:
-        spread(q, first_p[q], True)
-    for q in both:
-        spread(q, first_n[q], False)
+    along = [ahead[1 - q][0] for q in both]
+    diagonal = dict(to_xn, **to_yn)
+    steps = [
+        (lambda q: spread(q, first_p[q], True), first_p, first_now),
+        (lambda q: spread(q, first_n[q], False), first_n, first_now),
+        (lambda q: settle(q, first_now[q], first_p[1 - q], (along[q],), 0), first_now, first_p),
+        (lambda q: settle(q, first_now[q], first_n[1 - q], (), 0), first_now, first_n),
+        (lambda q: settle(q, first_p[q], first_p[1 - q], (diagonal, along[q]), 0), first_p, first_p),
+        (lambda q: spread(q, first_o[q], False), first_o, first_now),
+        (lambda q: settle(q, first_n[q], first_p[1 - q], (along[q],), 0), first_n, first_p),
+        (lambda q: settle(q, first_p[q], first_n[1 - q], (), 0), first_p, first_n),
+        (lambda q: settle(q, first_n[q], first_n[1 - q], (), 0), first_n, first_n),
+        (lambda q: settle(q, first_now[q], first_o[1 - q], (), 0), first_now, first_o),
+        (lambda q: settle(q, first_o[q], first_p[1 - q], (), 1), first_o, first_p),
+        (lambda q: settle(q, first_o[q], first_n[1 - q], (), 1), first_o, first_n),
+        (lambda q: settle(q, first_p[q], first_o[1 - q], (), 1), first_p, first_o),
+        (lambda q: settle(q, first_n[q], first_o[1 - q], (), 1), first_n, first_o),
+        (lambda q: settle(q, first_o[q], first_o[1 - q], (), 2), first_o, first_o),
+    ]
     for q in both:
         keep(q, first_now[q], first_now[1 - q])
-    for q in both:
-        settle(q, first_now[q], first_p[1 - q], True)
-    for q in both:
-        settle(q, first_now[q], first_n[1 - q], False)
-    for q in both:
-        spread(q, first_o[q], False)
-    for first in (first_p, first_n):
+    for step_fn, first, second in steps:
         for q in both:
-            settle(q, first[q], first_p[1 - q], True)
+            step_fn(q)
         for q in both:
-            settle(q, first[q], first_n[1 - q], False)
-    for q in both:
-        settle(q, first_now[q], first_o[1 - q], False)
-    for q in both:
-        settle(q, first_o[q], first_p[1 - q], True)
-    for q in both:
-        settle(q, first_o[q], first_n[1 - q], False)
-    for first in (first_p, first_n, first_o):
-        for q in both:
-            settle(q, first[q], first_o[1 - q], False)
-    orders = [first_now, first_p, first_n, first_o]
-    for xi in range(RING):
-        for yi in range(RING):
+            keep(q, first[q], second[1 - q])
+    blocks = [(first_now, first_now, 0)] + [(first, second, 0) for _, first, second in steps[:10]]
+    blocks += [(first, second, 1) for _, first, second in steps[10:14]] + [(first_o, first_o, 2)]
+    for group in range(3):
+        members = [(first, second) for first, second, which in blocks if which == group]
+        arrived(gp.reshape((-1,) + chunk).at[pl.ds(0, SUBS * len(members))], gp_recv.at[group])
+        for first, second in members:
             for q in both:
-                xx, yy = slot(q, orders[xi][q], orders[yi][1 - q])
-                arrived(gp.at[q, xx, yy], gp_recv.at[q, xx, yy])
+                xx, yy = slot(q, first[q], second[1 - q])
                 store(q, xx, yy, 1 - c, gp[q, xx, yy])
     sent(g.reshape((-1,) + chunk).at[pl.ds(0, len(pushes))], g_send.at[0])
     sent(gp, gp_send.at[0])
@@ -374,7 +374,7 @@
             dma((2,)), dma((2,)), dma((1,)), dma((RING, SUBS)), dma((1,)),
             dma((SUBS,)), dma((SUBS,)), dma((SUBS,)), dma((1,)), dma((SUBS,)),
             dma((1,)), dma((SUBS,)), dma((SUBS,)), dma((SUBS,)),
-            dma((1,)), dma((SUBS, RING, RING)), dma((1,)), dma((SUBS, RING, RING)),
+            dma((1,)), dma((SUBS, RING, RING)), dma((1,)), dma((3,)),
         ],
         compiler_params=pltpu.CompilerParams(collective_id=0, has_side_effects=True, vmem_limit_bytes=COMBINE_MIB * 2**20),
         cost_estimate=pl.CostEstimate(flops=2 * num_seqs // RING * w_o.shape[0] * cols_core, bytes_accessed=30 * 2**20, transcendentals=0),

time: 58.4 us -> 55.5 us (0.950)
  Pallas kernels: 56.6 us -> 53.6 us
    pallas_call x1, Pallas kernels: 41 us -> 38.1 us  [combine(): pl.pallas_call(functools.partial(combine_kernel, seqs, LANES ** (-0.5)),...]
where the time goes in v9:
time: 55.5 us; the launch traced here: 55.4 us
  Pallas kernels  53.6 us (97%)
  local copies, waits for them, and re-layouts  1.07 us (2%)
  between operations  0.69 us (1%)
    pallas_call x1, Pallas kernels, combine(): pl.pallas_call(functools.partial(combine_kernel, seqs, LANES ** (-0.5)),...  38.1 us
    pallas_call x1, Pallas kernels, project(): pl.pallas_call(project_kernel, out_shape=(pltpu.VMEM((kv, tiles * (num_se...  11.4 us
    pallas_call x1, Pallas kernels, update(): pl.pallas_call(update_kernel, out_shape=(near, near, far, far), in_specs=...  4.14 us

profile of v9, /device:TPU:97, one launch (start us, length us, event | category | flops | bytes accessed | tf_op | source)
XLA Modules:
  0.0 55.4 jit_solution(3776004319702563515)
XLA Ops:
  0.6 0.0 copy-start
  0.6 11.4 %project.1 = (f32[2,1360,128]{2,1,0:T(8,128)S(1)}, bf16[128,128,128]{2,1,0:T(8,128)(2,1)S(1)}, bf16[128,128,128]{2,1,0:T(8,128)(2,1)S(1)}) custom-call(bf16[128,5120]{1,0:T(8,128)(2,1)} %x_hbm.3, f32[64,128]{1,0:T(8,128)} %bitcast.10, f32[64,128]{1,0:T(8,128)} %bitcast.11, bf16[128,128,128]{2,1,0:T(8,128)(2,1)} %bitcast.8, bf16[128,128,128]{2,1,0:T(8,128)(2,1)} %bitcast.9, ...), custom_call_target="tpu_custom_call" | custom-call | flops 3355443200 | bytes 25165824 | tf_op jit(solution)/shard_map/project/pallas_call | solution.py:492
  12.0 0.0 copy-done
  12.1 0.0 copy-start.1
  12.1 4.1 %update.1 = (bf16[128,128,128]{2,1,0:T(8,128)(2,1)S(1)}, bf16[128,128,128]{2,1,0:T(8,128)(2,1)S(1)}, bf16[128,128,128]{2,1,0:T(8,128)(2,1)}, bf16[128,128,128]{2,1,0:T(8,128)(2,1)}) custom-call(s32[128]{0:T(128)S(1)} %copy-done, f32[2,1360,128]{2,1,0:T(8,128)S(1)} %get-tuple-element.10.heads_ref.q_ref, ...), custom_call_target="tpu_custom_call", output_to_operand_aliasing={{0}: (2, {}), {1}: (3, {})} | custom-call | flops 1000000 | bytes 10485760 | tf_op jit(solution)/shard_map/update/pallas_call | solution.py:566
  16.2 0.0 copy-done.1
  16.2 38.1 %combine.1 = bf16[128,5120]{1,0:T(8,128)(2,1)S(1)} custom-call(f32[2,1360,128]{2,1,0:T(8,128)S(1)} %get-tuple-element.10.heads_ref.q_ref, bf16[128,128,128]{2,1,0:T(8,128)(2,1)S(1)} %get-tuple-element.13.k_ref, bf16[128,128,128]{2,1,0:T(8,128)(2,1)S(1)} %get-tuple-element.14.v_ref, s32[128]{0:T(128)S(1)} %copy-done, f32[16]{0:T(128)S(1)} %copy-done.1, ...), custom_call_target="tpu_custom_call" | custom-call | flops 335544320 | bytes 31457280 | tf_op jit(solution)/shard_map/combine/pallas_call | solution.py:349
  54.3 1.1 %copy.20 = bf16[128,5120]{1,0:T(8,128)(2,1)} copy(bf16[128,5120]{1,0:T(8,128)(2,1)S(1)} %combine.1) | data formatting | bytes 2621440
Async XLA Ops:
  0.6 11.4 %copy-start = (s32[128]{0:T(128)S(1)}, s32[128]{0:T(128)}, u32[]{:S(2)}) copy-start(s32[128]{0:T(128)} %lens.3) | copy-start | bytes 1540
  12.1 4.2 %copy-start.1 = (f32[16]{0:T(128)S(1)}, f32[16]{0:T(128)}, u32[]{:S(2)}) copy-start(f32[16]{0:T(128)} %sink_ref.1) | copy-start | bytes 196

commit v10 on v9

--- a/solution.py
+++ b/solution.py
@@ -49,8 +49,53 @@
     dst[seqs] = stats
 
 
+def attention_setup(kv, heads, ctx2, sink_ref):
+    row = lax.broadcasted_iota(jnp.int32, (kv * heads, ctx2), 0)
+    lane = lax.broadcasted_iota(jnp.int32, (kv * heads, ctx2), 1)
+    base = lax.axis_index("sp") * (ctx2 // kv)
+    position = jnp.where(lane % kv == row // heads, lane // kv + base, jnp.iinfo(jnp.int32).max)
+    sinks = jnp.zeros((kv * heads, ctx2), jnp.float32)
+    for i in range(kv * heads):
+        sinks = jnp.where(row == i, sink_ref[i], sinks)
+    return position, jnp.max(sinks, axis=-1, keepdims=True)
+
+
+def attend_block(first, seqs, logit_scale, q_ref, k_ref, v_ref, lens, position, sink_col, dst):
+    kv, _, heads, _ = dst.shape
+    q_rows = kv * heads
+    q_stride = q_ref.shape[1] // (heads + 2)
+    lane = lax.broadcasted_iota(jnp.int32, (q_rows, LANES), 1)
+    waves = [range(j, j + WAVE) for j in range(0, seqs, WAVE)]
+    logits, tops, totals, weights, stats = {}, {}, {}, {}, jnp.zeros((q_rows, LANES), jnp.float32)
+    for turn in range(len(waves) + 2):
+        if turn < len(waves):
+            for i in waves[turn]:
+                q = jnp.concatenate([q_ref[k, pl.ds(first + i, heads, stride=q_stride), :] for k in range(kv)], axis=0).astype(jnp.bfloat16)
+                logits[i] = lax.dot_general(q, k_ref[first + i], (((1,), (1,)), ((), ())), preferred_element_type=jnp.float32)
+        if 0 <= turn - 1 < len(waves):
+            members = waves[turn - 1]
+            for i in members:
+                logits[i] = jnp.where(position <= lens[first + i], logits[i] * logit_scale, -jnp.inf)
+            for i in members:
+                tops[i] = jnp.maximum(jnp.max(logits[i], axis=-1, keepdims=True), sink_col)
+            for i in members:
+                weights[i] = jnp.exp(logits[i] - tops[i])
+            for i in members:
+                totals[i] = jnp.sum(weights[i], axis=-1, keepdims=True)
+        if 0 <= turn - 2:
+            members = waves[turn - 2]
+            numers = [
+                jnp.dot(weights[i].astype(jnp.bfloat16), v_ref[first + i], preferred_element_type=jnp.float32) for i in members]
+            for i, numer in zip(members, numers):
+                for k in range(kv):
+                    dst[k, i] = numer[k * heads : (k + 1) * heads]
+                stats = jnp.where(lane == i, tops[i], jnp.where(lane == HALF + i, totals[i], stats))
+    for k in range(kv):
+        dst[k, seqs] = stats[k * heads : (k + 1) * heads]
+
+
 def combine_kernel(
-    seqs, logit_scale, q_ref, k_ref, v_ref, lens, sink_ref, x_hbm, bo_hbm, wo_hbm, out_ref,
+    seqs, logit_scale, early_ref, q_ref, k_ref, v_ref, lens, sink_ref, x_hbm, bo_hbm, wo_hbm, out_ref,
     p_ref, bo_ref, bias_rows, ra, cb, rl, rm, rd, own_o, other_o, wbuf, xbuf, z, yrl, ym, yrm, yrd, g, gp,
     w_sem, x_sem, a_send, a_recv, b_send, rl_recv, rm_recv, rd_recv, o_send, o_recv,
     d_send, yrl_recv, yrm_recv, yrd_recv, g_send, g_recv, gp_send, gp_recv,
@@ -106,46 +151,14 @@
             src_ref=dst, dst_ref=dst, send_sem=recv_sem, recv_sem=recv_sem, device_id=partner, device_id_type=MESH).wait_recv()
 
     kv = p_ref.shape[2]
-    q_rows = kv * heads
     ctx2 = k_ref.shape[1]
-    q_stride = q_ref.shape[1] // (heads + 2)
-    row = lax.broadcasted_iota(jnp.int32, (q_rows, ctx2), 0)
-    lane = lax.broadcasted_iota(jnp.int32, (q_rows, ctx2), 1)
-    position = jnp.where(lane % kv == row // heads, lane // kv + sp * (ctx2 // kv), jnp.iinfo(jnp.int32).max)
-    sinks = jnp.zeros((q_rows, LANES), jnp.float32)
-    for i in range(q_rows):
-        sinks = jnp.where(row == i, sink_ref[i], sinks)
-    sink_col = jnp.max(sinks, axis=-1, keepdims=True)
+    position, sink_col = attention_setup(kv, heads, ctx2, sink_ref)
 
     def attend(b, s):
-        first = (b * SUBS + s) * seqs
-        waves = [range(j, j + WAVE) for j in range(0, seqs, WAVE)]
-        logits, tops, totals, weights, stats = {}, {}, {}, {}, jnp.zeros((q_rows, LANES), jnp.float32)
-        for turn in range(len(waves) + 2):
-            if turn < len(waves):
-                for i in waves[turn]:
-                    q = jnp.concatenate([q_ref[k, pl.ds(first + i, heads, stride=q_stride), :] for k in range(kv)], axis=0).astype(jnp.bfloat16)
-                    logits[i] = lax.dot_general(q, k_ref[first + i], (((1,), (1,)), ((), ())), preferred_element_type=jnp.float32)
-            if 0 <= turn - 1 < len(waves):
-                members = waves[turn - 1]
-                for i in members:
-                    logits[i] = jnp.where(position <= lens[first + i], logits[i] * logit_scale, -jnp.inf)
-                for i in members:
-                    tops[i] = jnp.maximum(jnp.max(logits[i], axis=-1, keepdims=True), sink_col)
-                for i in members:
-                    weights[i] = jnp.exp(logits[i] - tops[i])
-                for i in members:
-                    totals[i] = jnp.sum(weights[i], axis=-1, keepdims=True)
-            if 0 <= turn - 2:
-                members = waves[turn - 2]
-                numers = [
-                    jnp.dot(weights[i].astype(jnp.bfloat16), v_ref[first + i], preferred_element_type=jnp.float32) for i in members]
-                for i, numer in zip(members, numers):
-                    for k in range(kv):
-                        p_ref[b, s, k, i] = numer[k * heads : (k + 1) * heads]
-                    stats = jnp.where(lane == i, tops[i], jnp.where(lane == HALF + i, totals[i], stats))
-        for k in range(kv):
-            p_ref[b, s, k, seqs] = stats[k * heads : (k + 1) * heads]
+        attend_block((b * SUBS + s) * seqs, seqs, logit_scale, q_ref, k_ref, v_ref, lens, position, sink_col, p_ref.at[b, s])
+        join(b, s)
+
+    def join(b, s):
         send(p_ref.at[b, s, 1 - c], ra.at[b, s], a_send.at[0], a_recv.at[b, s], partner)
 
     def attend_both(b):
@@ -155,7 +168,7 @@
 
     def relay(s):
         arrived(ra.at[xo, s], a_recv.at[xo, s])
-        merge_into(cb.at[0, s], (p_ref.at[xo, s, c], ra.at[xo, s]), seqs)
+        merge_into(cb.at[0, s], (early_ref.at[s, c], ra.at[xo, s]), seqs)
         send(cb.at[0, s], rl.at[s], b_send.at[0], rl_recv.at[s], to_xn)
 
     def pass_on(s):
@@ -164,7 +177,8 @@
         merge_into(cb.at[2, s], (p_ref.at[xn, s, c], ra.at[xn, s], rl.at[s]), seqs)
         send(cb.at[2, s], rm.at[s], b_send.at[0], rm_recv.at[s], to_xn)
 
-    attend_both(xo)
+    for s in range(SUBS):
+        send(early_ref.at[s, 1 - c], ra.at[xo, s], a_send.at[0], a_recv.at[xo, s], partner)
     attend(xn, 0)
     for s in range(SUBS):
         relay(s)
@@ -331,7 +345,7 @@
     sent(gp, gp_send.at[0])
 
 
-def combine(queries, k_out, v_out, seq_lens, sinks, hidden, b_o, w_o):
+def combine(early, queries, k_out, v_out, seq_lens, sinks, hidden, b_o, w_o):
     num_seqs, d_model = hidden.shape
     seqs = num_seqs // (RING * SUBS)
     kv = CORES
@@ -349,7 +363,7 @@
     return pl.pallas_call(
         functools.partial(combine_kernel, seqs, LANES ** -0.5),
         out_shape=jax.ShapeDtypeStruct((num_seqs, d_model), bf16),
-        in_specs=[vmem, vmem, vmem, smem, smem, hbm, hbm, hbm],
+        in_specs=[vmem, vmem, vmem, vmem, smem, smem, hbm, hbm, hbm],
         out_specs=vmem,
         scratch_shapes=[
             pltpu.VMEM((RING, SUBS, kv) + part, f32),
@@ -379,7 +393,7 @@
         compiler_params=pltpu.CompilerParams(collective_id=0, has_side_effects=True, vmem_limit_bytes=COMBINE_MIB * 2**20),
         cost_estimate=pl.CostEstimate(flops=2 * num_seqs // RING * w_o.shape[0] * cols_core, bytes_accessed=30 * 2**20, transcendentals=0),
         name="combine",
-    )(queries, k_out, v_out, seq_lens, sinks, *(pltpu.with_memory_space_constraint(a, pltpu.HBM) for a in (hidden, b_o, w_o)))
+    )(early, queries, k_out, v_out, seq_lens, sinks, *(pltpu.with_memory_space_constraint(a, pltpu.HBM) for a in (hidden, b_o, w_o)))
 
 
 def project_kernel(
@@ -426,19 +440,23 @@
         xt = xbuf[:, t * LANES : (t + 1) * LANES].astype(jnp.float32)
         square += xt * xt
     inv_rms = lax.rsqrt(jnp.sum(square, axis=-1, keepdims=True) / d_model + NORM_EPS)
-    for t in range(d_model // LANES):
-        xt = xbuf[:, t * LANES : (t + 1) * LANES].astype(jnp.float32)
-        ht = (xt * inv_rms * gains[t : t + 1]).astype(jnp.bfloat16)
-        spread = jnp.dot(ht, pick, preferred_element_type=jnp.float32).astype(jnp.bfloat16)
-        for k in range(kv):
-            for j in range(kv):
-                piece = spread[:, j * LANES : (j + 1) * LANES]
-                hexp[t * kv + j, k * num_seqs : (k + 1) * num_seqs] = pltpu.roll(piece, k, 1) if k else piece
+    def spread_chunk(chunk):
+        for t in range(chunk * pieces // kv, (chunk + 1) * pieces // kv):
+            xt = xbuf[:, t * LANES : (t + 1) * LANES].astype(jnp.float32)
+            ht = (xt * inv_rms * gains[t : t + 1]).astype(jnp.bfloat16)
+            spread = jnp.dot(ht, pick, preferred_element_type=jnp.float32).astype(jnp.bfloat16)
+            for k in range(kv):
+                for j in range(kv):
+                    piece = spread[:, j * LANES : (j + 1) * LANES]
+                    hexp[t * kv + j, k * num_seqs : (k + 1) * num_seqs] = pltpu.roll(piece, k, 1) if k else piece
+
+    pieces = depth2 // LANES
+    for chunk in range(chunks):
+        spread_chunk(chunk)
     cache_copies = [pltpu.make_async_copy(src, dst, cache_sem.at[i]) for i, (src, dst) in enumerate(((k_hbm, kbuf), (v_hbm, vbuf)))]
 
     for copy in cache_copies:
         copy.start()
-    pieces = depth2 // LANES
     for chunk in range(chunks):
         w_copy(chunk).wait()
         lhs = jnp.concatenate([hexp[chunk * pieces + i] for i in range(pieces)], axis=1)
@@ -511,7 +529,7 @@
     )(*(pltpu.with_memory_space_constraint(a, pltpu.HBM) for a in operands))
 
 
-def update_kernel(lens, heads_ref, k_in, v_in, kbuf, vbuf, k_out, v_out, ko_sem, vo_sem):
+def update_kernel(logit_scale, lens, sink_ref, heads_ref, k_in, v_in, kbuf, vbuf, k_out, v_out, early_ref, ko_sem, vo_sem):
     kv = heads_ref.shape[0]
     num_seqs, ctx2 = kbuf.shape[:2]
     blocks = ko_sem.shape[0]
@@ -550,30 +568,41 @@
         cache_write(k_out, kbuf, ko_sem, block).start()
         cache_write(v_out, vbuf, vo_sem, block).start()
 
+    position, sink_col = attention_setup(kv, tiles - 2, ctx2, sink_ref)
+    opposite = (lax.axis_index("sp") // CORES + RING // 2) % RING
+
+    @pl.loop(0, SUBS)
+    def _(s):
+        attend_block((opposite * SUBS + s) * seqs, seqs, logit_scale, heads_ref, kbuf, vbuf, lens, position, sink_col, early_ref.at[s])
+
     @pl.loop(0, blocks)
     def _(block):
         cache_write(k_out, kbuf, ko_sem, block).wait()
         cache_write(v_out, vbuf, vo_sem, block).wait()
 
 
-def update(seq_lens, heads_out, k_near, v_near):
+def update(seq_lens, sinks, heads_out, k_near, v_near):
     blocks = RING * SUBS
     hbm = pl.BlockSpec(memory_space=pl.ANY)
     vmem = pl.BlockSpec(memory_space=pltpu.VMEM)
+    smem = pl.BlockSpec(memory_space=pltpu.SMEM)
+    kv = heads_out.shape[0]
+    heads = sinks.shape[0] // kv
+    seqs = k_near.shape[0] // blocks
     near = pltpu.VMEM(k_near.shape, k_near.dtype)
     far = jax.ShapeDtypeStruct(k_near.shape, k_near.dtype)
     dma = pltpu.SemaphoreType.DMA
     return pl.pallas_call(
-        update_kernel,
-        out_shape=(near, near, far, far),
-        in_specs=[pl.BlockSpec(memory_space=pltpu.SMEM), vmem, vmem, vmem],
-        out_specs=(vmem, vmem, hbm, hbm),
+        functools.partial(update_kernel, LANES ** -0.5),
+        out_shape=(near, near, far, far, pltpu.VMEM((SUBS, kv, seqs + 1, heads, LANES), jnp.float32)),
+        in_specs=[smem, smem, vmem, vmem, vmem],
+        out_specs=(vmem, vmem, hbm, hbm, vmem),
         scratch_shapes=[dma((blocks,)), dma((blocks,))],
-        input_output_aliases={2: 0, 3: 1},
+        input_output_aliases={3: 0, 4: 1},
         compiler_params=pltpu.CompilerParams(vmem_limit_bytes=UPDATE_MIB * 2**20),
         cost_estimate=pl.CostEstimate(flops=10**6, bytes_accessed=10 * 2**20, transcendentals=0),
         name="update",
-    )(seq_lens, heads_out, k_near, v_near)
+    )(seq_lens, sinks, heads_out, k_near, v_near)
 
 
 def solution(mesh):
@@ -585,8 +614,8 @@
         flat = (num_seqs, ctx * kv, head_dim)
         heads_out, k_near, v_near = project(
             hidden, rope_cos.T, rope_sin.T, k_cache.reshape(flat), v_cache.reshape(flat), norm_gain.reshape(-1, LANES), w_qkv, b_qkv)
-        k_near, v_near, k_out, v_out = update(seq_lens, heads_out, k_near, v_near)
-        out_hidden = combine(heads_out, k_near, v_near, seq_lens, sink_logits, hidden, b_o.reshape(-1, LANES), w_o)
+        k_near, v_near, k_out, v_out, early = update(seq_lens, sink_logits, heads_out, k_near, v_near)
+        out_hidden = combine(early, heads_out, k_near, v_near, seq_lens, sink_logits, hidden, b_o.reshape(-1, LANES), w_o)
         return out_hidden, k_out.reshape(k_cache.shape), v_out.reshape(v_cache.shape)
 
     return jax.shard_map(block_step, mesh=mesh, in_specs=(P("dp", None), P("dp"), P("dp", None), P("dp", None), cache_spec, cache_spec, P(None), P(None, "tp", None), P("tp", None), P("tp"), P("tp", None), P(None)), out_specs=(P("dp", None), cache_spec, cache_spec), check_vma=False)

time: 55.5 us -> 54.3 us (0.978)
  Pallas kernels: 53.6 us -> 52.5 us
    pallas_call x1, Pallas kernels: 38.1 us -> 36.9 us  [combine(): pl.pallas_call(functools.partial(combine_kernel, seqs, LANES ** (-0.5)),...]
where the time goes in v10:
time: 54.3 us; the launch traced here: 54.2 us
  Pallas kernels  52.5 us (97%)
  local copies, waits for them, and re-layouts  1.07 us (2%)
  between operations  0.69 us (1%)
    pallas_call x1, Pallas kernels, combine(): pl.pallas_call(functools.partial(combine_kernel, seqs, LANES ** (-0.5)),...  36.9 us
    pallas_call x1, Pallas kernels, project(): pl.pallas_call(project_kernel, out_shape=(pltpu.VMEM((kv, tiles * (num_se...  11.4 us
    pallas_call x1, Pallas kernels, update(): pl.pallas_call(functools.partial(update_kernel, LANES ** (-0.5)), out_sha...  4.15 us

profile of v10, /device:TPU:97, one launch (start us, length us, event | category | flops | bytes accessed | tf_op | source)
XLA Modules:
  0.0 54.2 jit_solution(12389775443530559271)
XLA Ops:
  0.6 0.0 copy-start
  0.6 0.0 copy-start.1
  0.7 11.4 %project.1 = (f32[2,1360,128]{2,1,0:T(8,128)S(1)}, bf16[128,128,128]{2,1,0:T(8,128)(2,1)S(1)}, bf16[128,128,128]{2,1,0:T(8,128)(2,1)S(1)}) custom-call(bf16[128,5120]{1,0:T(8,128)(2,1)} %x_hbm.3, f32[64,128]{1,0:T(8,128)} %bitcast.10, f32[64,128]{1,0:T(8,128)} %bitcast.11, bf16[128,128,128]{2,1,0:T(8,128)(2,1)} %bitcast.8, bf16[128,128,128]{2,1,0:T(8,128)(2,1)} %bitcast.9, ...), custom_call_target="tpu_custom_call" | custom-call | flops 3355443200 | bytes 25165824 | tf_op jit(solution)/shard_map/project/pallas_call | solution.py:510
  12.1 0.0 copy-done
  12.1 0.0 copy-done.1
  12.1 4.1 %update.1 = (bf16[128,128,128]{2,1,0:T(8,128)(2,1)S(1)}, bf16[128,128,128]{2,1,0:T(8,128)(2,1)S(1)}, bf16[128,128,128]{2,1,0:T(8,128)(2,1)}, bf16[128,128,128]{2,1,0:T(8,128)(2,1)}, f32[2,2,17,8,128]{4,3,2,1,0:T(8,128)S(1)}) custom-call(s32[128]{0:T(128)S(1)} %copy-done, f32[16]{0:T(128)S(1)} %copy-done.1, ...), custom_call_target="tpu_custom_call", output_to_operand_aliasing={{0}: (3, {}), {1}: (4, {})} | custom-call | flops 1000000 | bytes 10485760 | tf_op jit(solution)/shard_map/update/pallas_call | solution.py:595
  16.2 36.9 %combine.1 = bf16[128,5120]{1,0:T(8,128)(2,1)S(1)} custom-call(f32[2,2,17,8,128]{4,3,2,1,0:T(8,128)S(1)} %get-tuple-element.14.early_ref, f32[2,1360,128]{2,1,0:T(8,128)S(1)} %get-tuple-element.11.heads_ref.q_ref, bf16[128,128,128]{2,1,0:T(8,128)(2,1)S(1)} %get-tuple-element.15.k_ref, bf16[128,128,128]{2,1,0:T(8,128)(2,1)S(1)} %get-tuple-element.16.v_ref, ...), custom_call_target="tpu_custom_call" | custom-call | flops 335544320 | bytes 31457280 | tf_op jit(solution)/shard_map/combine/pallas_call | solution.py:363
  53.1 1.1 %copy.20 = bf16[128,5120]{1,0:T(8,128)(2,1)} copy(bf16[128,5120]{1,0:T(8,128)(2,1)S(1)} %combine.1) | data formatting | bytes 2621440
Async XLA Ops:
  0.6 11.4 %copy-start = (s32[128]{0:T(128)S(1)}, s32[128]{0:T(128)}, u32[]{:S(2)}) copy-start(s32[128]{0:T(128)} %lens.3) | copy-start | bytes 1540
  0.6 11.4 %copy-start.1 = (f32[16]{0:T(128)S(1)}, f32[16]{0:T(128)}, u32[]{:S(2)}) copy-start(f32[16]{0:T(128)} %sink_ref.3) | copy-start | bytes 196

commit v11 on v10

--- a/solution.py
+++ b/solution.py
@@ -288,14 +288,15 @@
         for axis in (q, 1 - q):
             for kind in range(2):
                 push(q, first_now[q], first_now[1 - q], ahead[axis][kind])
+        push(q, first_now[q], first_now[1 - q], dict(to_xn, **to_yn))
         share(q, first_now[q], first_now[1 - q], 0)
 
-    def spread(q, first, forward):
+    def spread(q, first, forward, kinds):
         other = 1 - q
         receive(q, first, first_now[other])
         if forward:
             push(q, first, first_now[other], ahead[q][0])
-        for kind in range(2):
+        for kind in kinds:
             push(q, first, first_now[other], ahead[other][kind])
         share(q, first, first_now[other], 0)
 
@@ -306,24 +307,24 @@
         share(q, first, second, group)
 
     both = range(SUBS)
-    along = [ahead[1 - q][0] for q in both]
+    along, onward = [ahead[1 - q][0] for q in both], [ahead[q][0] for q in both]
     diagonal = dict(to_xn, **to_yn)
     steps = [
-        (lambda q: spread(q, first_p[q], True), first_p, first_now),
-        (lambda q: spread(q, first_n[q], False), first_n, first_now),
+        (lambda q: spread(q, first_p[q], True, (1,)), first_p, first_now),
         (lambda q: settle(q, first_now[q], first_p[1 - q], (along[q],), 0), first_now, first_p),
+        (lambda q: spread(q, first_n[q], False, (0, 1)), first_n, first_now),
+        (lambda q: settle(q, first_p[q], first_p[1 - q], (diagonal, along[q], onward[q]), 0), first_p, first_p),
         (lambda q: settle(q, first_now[q], first_n[1 - q], (), 0), first_now, first_n),
-        (lambda q: settle(q, first_p[q], first_p[1 - q], (diagonal, along[q]), 0), first_p, first_p),
-        (lambda q: spread(q, first_o[q], False), first_o, first_now),
+        (lambda q: spread(q, first_o[q], False, (1,)), first_o, first_now),
         (lambda q: settle(q, first_n[q], first_p[1 - q], (along[q],), 0), first_n, first_p),
         (lambda q: settle(q, first_p[q], first_n[1 - q], (), 0), first_p, first_n),
         (lambda q: settle(q, first_n[q], first_n[1 - q], (), 0), first_n, first_n),
         (lambda q: settle(q, first_now[q], first_o[1 - q], (), 0), first_now, first_o),
         (lambda q: settle(q, first_o[q], first_p[1 - q], (), 1), first_o, first_p),
+        (lambda q: settle(q, first_p[q], first_o[1 - q], (), 1), first_p, first_o),
+        (lambda q: settle(q, first_o[q], first_o[1 - q], (), 2), first_o, first_o),
         (lambda q: settle(q, first_o[q], first_n[1 - q], (), 1), first_o, first_n),
-        (lambda q: settle(q, first_p[q], first_o[1 - q], (), 1), first_p, first_o),
         (lambda q: settle(q, first_n[q], first_o[1 - q], (), 1), first_n, first_o),
-        (lambda q: settle(q, first_o[q], first_o[1 - q], (), 2), first_o, first_o),
     ]
     for q in both:
         keep(q, first_now[q], first_now[1 - q])
@@ -333,7 +334,7 @@
         for q in both:
             keep(q, first[q], second[1 - q])
     blocks = [(first_now, first_now, 0)] + [(first, second, 0) for _, first, second in steps[:10]]
-    blocks += [(first, second, 1) for _, first, second in steps[10:14]] + [(first_o, first_o, 2)]
+    blocks += [(first, second, 1 if first is not second else 2) for _, first, second in steps[10:]]
     for group in range(3):
         members = [(first, second) for first, second, which in blocks if which == group]
         arrived(gp.reshape((-1,) + chunk).at[pl.ds(0, SUBS * len(members))], gp_recv.at[group])

time: 54.3 us -> 54.3 us (level)
  no operation moved by 1% of the time
where the time goes in v11:
time: 54.3 us; the launch traced here: 54.2 us
  Pallas kernels  52.4 us (97%)
  local copies, waits for them, and re-layouts  1.07 us (2%)
  between operations  0.69 us (1%)
    pallas_call x1, Pallas kernels, combine(): pl.pallas_call(functools.partial(combine_kernel, seqs, LANES ** (-0.5)),...  36.9 us
    pallas_call x1, Pallas kernels, project(): pl.pallas_call(project_kernel, out_shape=(pltpu.VMEM((kv, tiles * (num_se...  11.4 us
    pallas_call x1, Pallas kernels, update(): pl.pallas_call(functools.partial(update_kernel, LANES ** (-0.5)), out_sha...  4.15 us

profile of v11, /device:TPU:97, one launch (start us, length us, event | category | flops | bytes accessed | tf_op | source)
XLA Modules:
  0.0 54.2 jit_solution(1581409401239301156)
XLA Ops:
  0.6 0.0 copy-start
  0.6 0.0 copy-start.1
  0.7 11.4 %project.1 = (f32[2,1360,128]{2,1,0:T(8,128)S(1)}, bf16[128,128,128]{2,1,0:T(8,128)(2,1)S(1)}, bf16[128,128,128]{2,1,0:T(8,128)(2,1)S(1)}) custom-call(bf16[128,5120]{1,0:T(8,128)(2,1)} %x_hbm.3, f32[64,128]{1,0:T(8,128)} %bitcast.10, f32[64,128]{1,0:T(8,128)} %bitcast.11, bf16[128,128,128]{2,1,0:T(8,128)(2,1)} %bitcast.8, bf16[128,128,128]{2,1,0:T(8,128)(2,1)} %bitcast.9, ...), custom_call_target="tpu_custom_call" | custom-call | flops 3355443200 | bytes 25165824 | tf_op jit(solution)/shard_map/project/pallas_call | solution.py:511
  12.1 0.0 copy-done
  12.1 0.0 copy-done.1
  12.1 4.1 %update.1 = (bf16[128,128,128]{2,1,0:T(8,128)(2,1)S(1)}, bf16[128,128,128]{2,1,0:T(8,128)(2,1)S(1)}, bf16[128,128,128]{2,1,0:T(8,128)(2,1)}, bf16[128,128,128]{2,1,0:T(8,128)(2,1)}, f32[2,2,17,8,128]{4,3,2,1,0:T(8,128)S(1)}) custom-call(s32[128]{0:T(128)S(1)} %copy-done, f32[16]{0:T(128)S(1)} %copy-done.1, ...), custom_call_target="tpu_custom_call", output_to_operand_aliasing={{0}: (3, {}), {1}: (4, {})} | custom-call | flops 1000000 | bytes 10485760 | tf_op jit(solution)/shard_map/update/pallas_call | solution.py:596
  16.2 36.9 %combine.1 = bf16[128,5120]{1,0:T(8,128)(2,1)S(1)} custom-call(f32[2,2,17,8,128]{4,3,2,1,0:T(8,128)S(1)} %get-tuple-element.14.early_ref, f32[2,1360,128]{2,1,0:T(8,128)S(1)} %get-tuple-element.11.heads_ref.q_ref, bf16[128,128,128]{2,1,0:T(8,128)(2,1)S(1)} %get-tuple-element.15.k_ref, bf16[128,128,128]{2,1,0:T(8,128)(2,1)S(1)} %get-tuple-element.16.v_ref, ...), custom_call_target="tpu_custom_call" | custom-call | flops 335544320 | bytes 31457280 | tf_op jit(solution)/shard_map/combine/pallas_call | solution.py:364
  53.1 1.1 %copy.20 = bf16[128,5120]{1,0:T(8,128)(2,1)} copy(bf16[128,5120]{1,0:T(8,128)(2,1)S(1)} %combine.1) | data formatting | bytes 2621440
Async XLA Ops:
  0.6 11.4 %copy-start = (s32[128]{0:T(128)S(1)}, s32[128]{0:T(128)}, u32[]{:S(2)}) copy-start(s32[128]{0:T(128)} %lens.3) | copy-start | bytes 1540
  0.6 11.4 %copy-start.1 = (f32[16]{0:T(128)S(1)}, f32[16]{0:T(128)}, u32[]{:S(2)}) copy-start(f32[16]{0:T(128)} %sink_ref.3) | copy-start | bytes 196

commit v12 on v10

--- a/solution.py
+++ b/solution.py
@@ -16,7 +16,7 @@
 PROJECT_MIB = 30
 UPDATE_MIB = 4
 COMBINE_MIB = 26
-WAVE = 4
+WAVE = 8
 RING = 4
 
 

time: 54.3 us -> 54.5 us (level)
  no operation moved by 1% of the time
where the time goes in v12:
time: 54.5 us; the launch traced here: 54.4 us
  Pallas kernels  52.6 us (97%)
  local copies, waits for them, and re-layouts  1.07 us (2%)
  between operations  0.69 us (1%)
    pallas_call x1, Pallas kernels, combine(): pl.pallas_call(functools.partial(combine_kernel, seqs, LANES ** (-0.5)),...  37.1 us
    pallas_call x1, Pallas kernels, project(): pl.pallas_call(project_kernel, out_shape=(pltpu.VMEM((kv, tiles * (num_se...  11.4 us
    pallas_call x1, Pallas kernels, update(): pl.pallas_call(functools.partial(update_kernel, LANES ** (-0.5)), out_sha...  4.15 us

profile of v12, /device:TPU:97, one launch (start us, length us, event | category | flops | bytes accessed | tf_op | source)
XLA Modules:
  0.0 54.4 jit_solution(1744261900047119107)
XLA Ops:
  0.6 0.0 copy-start
  0.6 0.0 copy-start.1
  0.7 11.4 %project.1 = (f32[2,1360,128]{2,1,0:T(8,128)S(1)}, bf16[128,128,128]{2,1,0:T(8,128)(2,1)S(1)}, bf16[128,128,128]{2,1,0:T(8,128)(2,1)S(1)}) custom-call(bf16[128,5120]{1,0:T(8,128)(2,1)} %x_hbm.3, f32[64,128]{1,0:T(8,128)} %bitcast.10, f32[64,128]{1,0:T(8,128)} %bitcast.11, bf16[128,128,128]{2,1,0:T(8,128)(2,1)} %bitcast.8, bf16[128,128,128]{2,1,0:T(8,128)(2,1)} %bitcast.9, ...), custom_call_target="tpu_custom_call" | custom-call | flops 3355443200 | bytes 25165824 | tf_op jit(solution)/shard_map/project/pallas_call | solution.py:510
  12.1 0.0 copy-done
  12.1 0.0 copy-done.1
  12.1 4.1 %update.1 = (bf16[128,128,128]{2,1,0:T(8,128)(2,1)S(1)}, bf16[128,128,128]{2,1,0:T(8,128)(2,1)S(1)}, bf16[128,128,128]{2,1,0:T(8,128)(2,1)}, bf16[128,128,128]{2,1,0:T(8,128)(2,1)}, f32[2,2,17,8,128]{4,3,2,1,0:T(8,128)S(1)}) custom-call(s32[128]{0:T(128)S(1)} %copy-done, f32[16]{0:T(128)S(1)} %copy-done.1, ...), custom_call_target="tpu_custom_call", output_to_operand_aliasing={{0}: (3, {}), {1}: (4, {})} | custom-call | flops 1000000 | bytes 10485760 | tf_op jit(solution)/shard_map/update/pallas_call | solution.py:595
  16.2 37.1 %combine.1 = bf16[128,5120]{1,0:T(8,128)(2,1)S(1)} custom-call(f32[2,2,17,8,128]{4,3,2,1,0:T(8,128)S(1)} %get-tuple-element.14.early_ref, f32[2,1360,128]{2,1,0:T(8,128)S(1)} %get-tuple-element.11.heads_ref.q_ref, bf16[128,128,128]{2,1,0:T(8,128)(2,1)S(1)} %get-tuple-element.15.k_ref, bf16[128,128,128]{2,1,0:T(8,128)(2,1)S(1)} %get-tuple-element.16.v_ref, ...), custom_call_target="tpu_custom_call" | custom-call | flops 335544320 | bytes 31457280 | tf_op jit(solution)/shard_map/combine/pallas_call | solution.py:363
  53.3 1.1 %copy.20 = bf16[128,5120]{1,0:T(8,128)(2,1)} copy(bf16[128,5120]{1,0:T(8,128)(2,1)S(1)} %combine.1) | data formatting | bytes 2621440
Async XLA Ops:
  0.6 11.4 %copy-start = (s32[128]{0:T(128)S(1)}, s32[128]{0:T(128)}, u32[]{:S(2)}) copy-start(s32[128]{0:T(128)} %lens.3) | copy-start | bytes 1540
  0.6 11.4 %copy-start.1 = (f32[16]{0:T(128)S(1)}, f32[16]{0:T(128)}, u32[]{:S(2)}) copy-start(f32[16]{0:T(128)} %sink_ref.3) | copy-start | bytes 196
